TPU v7x, 512 devices: a 4x2x32 block of a 4x8x32 slice. The times are simulated.
512 devices in a mesh: real: 2 (over y), env: 32 (over z), mpo: 4 (over x), col: 2 (over core).
Axes of the slice: x: 4, y: 2, z: 32, core: 2. Of those that a mesh axis runs over, the one named last changes fastest.
The devices are a block of a 4x8x32 slice.
Arguments:
- held: bfloat16 [24576, 8, 384], P(('real', 'env', 'col')), parts along dimension 0, may hold values from -0.15625 to 0.15625
- owner_map: int32 [64, 192], P('real'), parts along dimension 0, may hold values from 0 to 12287, as said below
- kept: int32 [64], P(('real', 'env')), parts along dimension 0, may hold values from 96 to 384
- left_env: bfloat16 [16, 64, 384, 384], P('mpo', ('real', 'env')), parts along dimension 1, may hold values from -6 to 6
- mpo_tensor: float32 [14, 14, 4, 4], replicated, may hold values from -1 to 1
- mpo_mask: int32 [14, 14], replicated, may hold values 0 or 1
- fields: float32 [4], P('real'), parts along dimension 0, may hold values from -2 to 2
Outputs:
- new_env: float32 [16, 64, 384, 384], P('mpo', ('real', 'env'), None, 'col'), parts along dimension 1
There are 2 independent parts, one for each index of `real`. A program takes and returns all parts, laid end to end along the dimension named above; an argument that names none is the same for every part. Nothing has to cross between parts.
Inputs may be any that keep to these rules, and one draw needn't show every extreme that they name: owner_map[t, j] is the slot of held that holds tile j of sector t; all entries differ. The owner of index o along env+col holds the slots o * 192 to (o + 1) * 192 - 1. Among the tiles of one sector (the sector of one env index), one owner holds at most 6, and for every sector some owner holds exactly 6.
All inputs are finite; a program needn't handle non-finite values.
Results may differ from a plain program's by a relative error of at most 0.0042.
Values may be sent and summed in bfloat16 or wider, within the bound.
No kernel may reach another device: no remote copies, remote signals or barrier semaphores. Data moves between devices by JAX's collectives and lax.ppermute only.
A program may use at most 64 MiB of HBM per device.

v0:
```python
import jax
import jax.numpy as jnp
from jax import lax
from jax.sharding import PartitionSpec as P


def in_order(tiles, dim):
    tiles = jnp.moveaxis(tiles, 0, dim)
    lengths = tiles.shape
    return tiles.reshape(*lengths[:dim], lengths[dim] * lengths[dim + 1], *lengths[dim + 2 :])


def sent_to_all(shard, axis):
    copies = jnp.broadcast_to(shard, (lax.axis_size(axis), *shard.shape))
    return lax.all_to_all(copies, axis, split_axis=0, concat_axis=0, tiled=True)


def collect(shard, axis, dim):
    return in_order(sent_to_all(shard, axis), dim)


def split_up(shard, dim, count):
    before, after = (shard.shape[:dim], shard.shape[dim + 1 :])
    return jnp.moveaxis(shard.reshape(*before, count, -1, *after), dim, 0)


def summed_on_arrival(shard, axis, dim):
    count = lax.axis_size(axis)
    tiles = lax.all_to_all(split_up(shard, dim, count), axis, 0, 0, tiled=True)
    return jnp.sum(tiles.astype(jnp.float32), axis=0)


def build_couplings(mpo_tensor, mpo_mask, fields, padded):
    bond = mpo_tensor.shape[0]
    states = mpo_tensor.shape[2]
    base = mpo_tensor * mpo_mask.astype(jnp.float32)[:, :, None, None]
    level = jnp.arange(states, dtype=jnp.int32)
    spin_first = 0.5 - (level // 2).astype(jnp.float32)
    spin_second = 0.5 - (level % 2).astype(jnp.float32)
    onsite = jnp.diag(fields[0] * spin_first + fields[1] * spin_second)
    bond_index = jnp.arange(bond, dtype=jnp.int32)
    corner = (bond_index[:, None] == bond - 1) & (bond_index[None, :] == 0)
    base = base + jnp.where(corner[:, :, None, None], onsite[None, None, :, :], jnp.float32(0.0))
    return jnp.pad(base, ((0, padded - bond), (0, padded - bond), (0, 0), (0, 0)))


def on_device(held, owner_map, kept, left_env, mpo_tensor, mpo_mask, fields):
    env_count = lax.axis_size("env")
    core_count = lax.axis_size("col")
    plane_count = lax.axis_size("mpo")
    env_row = lax.axis_index("env")
    core = lax.axis_index("col")
    plane = lax.axis_index("mpo")
    pool, tile, width = held.shape
    sectors_here = kept.shape[0]
    tiles_sector = owner_map.shape[1]
    states = tiles_sector * tile // width
    per_row = sectors_here * tiles_sector
    capacity = 2 * per_row // (env_count * core_count)
    owner_self = env_row * core_count + core
    leading_sector = lax.Precision.HIGHEST
    holder = owner_map // pool
    local_slot = owner_map % pool
    mine = (holder == owner_self).astype(jnp.int32)
    rank = jnp.cumsum(mine, axis=1) - 1
    slot_ids = jnp.arange(capacity, dtype=jnp.int32)
    picked = (mine[:, None, :] == 1) & (rank[:, None, :] == slot_ids[None, :, None])
    source_slot = jnp.sum(jnp.where(picked, local_slot[:, None, :], 0), axis=2)
    part_width = width // plane_count
    source = lax.dynamic_slice_in_dim(held, plane * part_width, part_width, 2)
    outgoing = jnp.take(source, source_slot.reshape(-1), axis=0).reshape(
        env_count, capacity, tile, part_width
    )
    arrived = lax.all_to_all(outgoing, "env", split_axis=0, concat_axis=0, tiled=True)
    arrived = collect(arrived, "col", 1)
    arrived = collect(arrived, "mpo", 3)
    mine_rows = lax.dynamic_slice_in_dim(
        owner_map, env_row * sectors_here, sectors_here, 0
    ).reshape(per_row)
    sender = mine_rows // pool
    position = jnp.arange(per_row, dtype=jnp.int32)
    earlier = (sender[:, None] == sender[None, :]) & (position[None, :] < position[:, None])
    order_within = jnp.sum(earlier.astype(jnp.int32), axis=1)
    index = (
        sender // core_count * (core_count * capacity)
        + sender % core_count * capacity
        + order_within
    )
    flat = arrived.reshape(env_count * core_count * capacity, tile * width)
    sector_matrices = jnp.take(flat, index, axis=0).reshape(sectors_here, states, width, width)
    columns = jnp.arange(width, dtype=jnp.int32)
    keep = columns[None, :] < kept[:, None]
    sector_matrices = jnp.where(
        keep[:, None, None, :], sector_matrices, jnp.zeros((), jnp.bfloat16)
    )
    slab = left_env.shape[0]
    couplings = build_couplings(mpo_tensor, mpo_mask, fields, slab * plane_count)
    share = width // core_count
    own_columns = lax.dynamic_slice_in_dim(sector_matrices, core * share, share, 3)
    mine_coupling = lax.dynamic_slice_in_dim(couplings, plane * slab, slab, 0)
    firsts = jnp.einsum(
        "wij,sja->wsia", left_env[:, 0], own_columns[0], preferred_element_type=jnp.float32
    )
    next_spin = jnp.einsum(
        "wvts,wsia->vtia", mine_coupling, firsts, precision=leading_sector
    ).astype(jnp.bfloat16)
    operator_pieces = [
        jnp.einsum(
            "hze,shzo->seo", sector_matrices[0], next_spin, preferred_element_type=jnp.float32
        )
    ]
    return summed_on_arrival(jnp.stack(operator_pieces, axis=1).astype(jnp.bfloat16), "mpo", 0)


def solution(mesh):
    return jax.shard_map(
        on_device,
        mesh=mesh,
        in_specs=(
            P(("real", "env", "col"), None, None),
            P("real", None),
            P(("real", "env")),
            P("mpo", ("real", "env"), None, None),
            P(),
            P(),
            P("real"),
        ),
        out_specs=P("mpo", ("real", "env"), None, "col"),
        check_vma=False,
    )
```

profile of v0, /device:TPU:40, one launch (start us, length us, event | category | flops | bytes accessed | tf_op | source)
XLA Modules:
  0.0 237.1 jit_solution(11464659930123475766)
XLA Ops:
  0.0 0.9 add_select_fusion
  0.9 0.8 broadcast_compare_fusion
  1.7 0.6 reduce-window.6
  2.9 0.7 fusion.53
  4.2 1.4 fusion.52
  6.0 1.3 constant_dynamic-slice_fusion.1
  7.3 0.7 gather_fusion
  8.3 98.7 %all_to_all.20 = bf16[32,6,8,96]{3,2,1,0:T(8,128)(2,1)S(1)} all-to-all(bf16[32,6,8,96]{3,2,1,0:T(8,128)(2,1)S(1)} %broadcast_select_fusion), channel_id=1, replica_groups=mesh['real'=2,'env'=32,'mpo'=4,'col'=2] {'env'}, dimensions={0} | all-to-all | bytes 589824 | tf_op jit(solution)/shard_map/all_to_all | solution.py:74
  107.2 4.4 %all_to_all.21 = bf16[2,32,6,8,96]{4,3,2,1,0:T(8,128)(2,1)S(1)} all-to-all(bf16[2,32,6,8,96]{4,3,2,1,0:T(8,128)(2,1)S(1)} %broadcast_in_dim.129), channel_id=1, replica_groups=mesh['real'=2,'env'=32,'mpo'=4,'col'=2] {'col'}, dimensions={0} | all-to-all | bytes 1179648 | tf_op jit(solution)/shard_map/all_to_all | solution.py:15
  111.6 2.2 broadcast_in_dim.130
  113.8 5.0 %all-to-all-start.2 = ((bf16[4,32,12,8,96]{4,3,2,1,0:T(8,128)(2,1)}), bf16[4,32,12,8,96]{4,3,2,1,0:T(8,128)(2,1)}, u32[]{:S(2)}, u32[]{:S(2)}) async-start(bf16[4,32,12,8,96]{4,3,2,1,0:T(8,128)(2,1)} %broadcast_in_dim.130), calls=%async_computation.2 | async-start | bytes 6291456 | tf_op jit(solution)/shard_map/all_to_all | solution.py:15
  120.7 1.2 fusion.43
  122.2 0.6 fusion.59
  122.8 34.3 %all-to-all-done.2 = bf16[4,32,12,8,96]{4,3,2,1,0:T(8,128)(2,1)} async-done(((bf16[4,32,12,8,96]{4,3,2,1,0:T(8,128)(2,1)}), bf16[4,32,12,8,96]{4,3,2,1,0:T(8,128)(2,1)}, u32[]{:S(2)}, u32[]{:S(2)}) %all-to-all-start.2) | async-done | bytes 2359328 | tf_op jit(solution)/shard_map/all_to_all | solution.py:15
  157.0 7.6 %copy.34 = bf16[32,12,8,4,96]{4,3,2,1,0:T(4,128)(2,1)} copy(bf16[32,12,8,4,96]{4,2,1,0,3:T(8,128)(2,1)} %bitcast.11) | data formatting | bytes 4718592 | tf_op jit(solution)/shard_map/transpose | solution.py:8
  164.7 7.0 %reshape_reshape.3 = bf16[384,3072]{1,0:T(8,128)(2,1)S(1)} reshape(bf16[32,12,8,4,96]{4,3,2,1,0:T(4,128)(2,1)} %copy.34) | data formatting | bytes 4718592 | tf_op jit(solution)/shard_map/reshape;reshape | solution.py:89
  171.7 2.3 gather_fusion.1
  174.0 2.4 gather.17
  176.4 1.4 gather.18
  178.5 1.4 convolution_bitcast_fusion
  179.9 18.9 %bitcast_convert_fusion = bf16[16,4,384,192]{2,0,3,1:T(8,128)(2,1)S(1)} fusion(f32[4,4,384,192]{2,3,0,1:T(8,128)S(1)} %convolution_bitcast_fusion, f32[4,16,4,4,1]{1,3,0,4,2:T(4,128)S(1)} %copy-done.4), kind=kOutput, calls=%fused_computation.2 | convolution fusion | flops 910688256 | bytes 14159872 | tf_op jit(solution)/shard_map/wvts,wsia->vtia/dot_general | solution.py:104
  198.8 5.3 %bitcast_convert_fusion.1 = bf16[16,192,384]{2,1,0:T(8,128)(2,1)S(1)} fusion(bf16[16,4,384,192]{2,0,3,1:T(8,128)(2,1)S(1)} %bitcast_convert_fusion, bf16[4,384,384]{2,1,0:T(8,128)(2,1)S(1)} %copy-done.2, pred[4,384]{1,0:T(4,128)(4,1)S(1)} %broadcast_in_dim.123, pred[384]{0:T(512)(128)(4,1)S(1)} %iota_compare_fusion.2), kind=kOutput, calls=%fused_computation.5 | convolution fusion | flops 3626237952 | bytes 12978048 | tf_op jit(solution)/shard_map/hze,shzo->seo/dot_general | solution.py:108
  204.1 31.6 %all_to_all.22 = bf16[4,4,1,384,192]{3,4,1,2,0:T(8,128)(2,1)S(1)} all-to-all(bf16[4,4,1,384,192]{3,4,1,2,0:T(8,128)(2,1)S(1)} %bitcast.78), channel_id=1, replica_groups=mesh['real'=2,'env'=32,'mpo'=4,'col'=2] {'mpo'}, dimensions={0} | all-to-all | bytes 4718592 | tf_op jit(solution)/shard_map/all_to_all | solution.py:29
  235.7 1.4 convert_reduce_fusion
  (51 shorter events, 4.1 us)
Async XLA Ops:
  0.0 178.5 %copy-start = (bf16[4,1,384,384]{3,2,1,0:T(8,128)(2,1)S(1)}, bf16[4,1,384,384]{3,2,1,0:T(8,128)(2,1)}, u32[]{:S(2)}) copy-start(bf16[4,1,384,384]{3,2,1,0:T(8,128)(2,1)} %param.10) | copy-start | bytes 3538948
  113.8 6.0 %copy-start.5 = (s32[14,14]{1,0:T(8,128)S(1)}, s32[14,14]{1,0:T(8,128)}, u32[]{:S(2)}) copy-start(s32[14,14]{1,0:T(8,128)} %param.12) | copy-start | bytes 2356
  113.8 6.3 %copy-start.6 = (f32[2]{0:T(128)S(1)}, f32[2]{0:T(128)}, u32[]{:S(2)}) copy-start(f32[2]{0:T(128)} %param.13) | copy-start | bytes 28
  113.8 8.3 %copy-start.3 = (f32[14,14,4,4]{1,3,2,0:T(4,128)S(1)}, f32[14,14,4,4]{1,3,2,0:T(4,128)}, u32[]{:S(2)}) copy-start(f32[14,14,4,4]{1,3,2,0:T(4,128)} %param.11) | copy-start | bytes 37636
  113.8 43.3 %all-to-all-start.2 = ((bf16[4,32,12,8,96]{4,3,2,1,0:T(8,128)(2,1)}), bf16[4,32,12,8,96]{4,3,2,1,0:T(8,128)(2,1)}, u32[]{:S(2)}, u32[]{:S(2)}) async-start(bf16[4,32,12,8,96]{4,3,2,1,0:T(8,128)(2,1)} %broadcast_in_dim.130), calls=%async_computation.2 | async-start | bytes 6291456 | tf_op jit(solution)/shard_map/all_to_all | solution.py:15
  174.0 2.4 %copy-start.1 = (bf16[192,3072]{1,0:T(8,128)(2,1)S(1)}, bf16[192,3072]{1,0:T(8,128)(2,1)}, u32[]{:S(2)}) copy-start(bf16[192,3072]{1,0:T(8,128)(2,1)} %gather_fusion.1) | copy-start | bytes 3538948
  178.5 1.4 copy-start.4
  179.9 18.9 %copy-start.2 = (bf16[4,384,384]{2,1,0:T(8,128)(2,1)S(1)}, bf16[4,384,384]{2,1,0:T(8,128)(2,1)}, u32[]{:S(2)}) copy-start(bf16[4,384,384]{2,1,0:T(8,128)(2,1)} %gather.18) | copy-start | bytes 3538948
where the time goes:
time: 238 us; the launch traced here: 237 us
  blocking collectives  135 us (57%)
  waiting for transfers between devices  34.3 us (14%)
  local copies, waits for them, and re-layouts  28.6 us (12%)
  matrix products  25.6 us (11%)
  other arithmetic  8.04 us (3%)
  starting transfers between devices  5.03 us (2%)
    all_to_all x1, blocking collectives, on_device(): lax.all_to_all(outgoing, 'env', split_axis=0, concat_axis=0, tiled=True)  98.7 us
    all_to_all x1, waiting for transfers between devices, sent_to_all(): return lax.all_to_all(copies, axis, split_axis=0, concat_axis=0, tiled=True)  34.3 us
    all_to_all x1, blocking collectives, summed_on_arrival(): tiles = lax.all_to_all(split_up(shard, dim, count), axis, 0, 0, tiled=True)  31.6 us
    dot_general x1, matrix products, on_device(): jnp.einsum('wvts,wsia->vtia', mine_coupling, firsts, precision=leading_se...  18.9 us
    transpose x1, local copies, waits for them, and re-layouts, in_order(): tiles = jnp.moveaxis(tiles, 0, dim)  7.64 us
    another operation x1, local copies, waits for them, and re-layouts, on_device(): flat = arrived.reshape(env_count * core_count * capacity, tile * width)  7.01 us
    gather x3, local copies, waits for them, and re-layouts, on_device(): jnp.take(flat, index, axis=0).reshape(sectors_here, states, width, width)  6.07 us
    dot_general x1, matrix products, on_device(): jnp.einsum('hze,shzo->seo', sector_matrices[0], next_spin, preferred_elem...  5.29 us
  transfers between devices with their start and end apart: 1, of which 1 were waited for; matrix products, arithmetic and copies ran while one was open for 1% of the time, Pallas kernels for 0%

commit v1 on v0

v1 whole, which is shorter than its diff:
```python
import functools

import jax
import jax.numpy as jnp
from jax import lax
from jax.experimental import pallas as pl
from jax.experimental.pallas import tpu as pltpu
from jax.sharding import PartitionSpec as P


F32 = jnp.float32
BF16 = jnp.bfloat16
CHUNKS = 2
PLANES = 4


def iota(shape, dim):
    return lax.broadcasted_iota(jnp.int32, shape, dim)


def onehot(condition):
    return jnp.where(condition, F32(1.0), F32(0.0)).astype(BF16)


def dot(a, b):
    return lax.dot_general(a, b, (((1,), (0,)), ((), ())), preferred_element_type=F32)


def dot_t(a, b):
    return lax.dot_general(a, b, (((1,), (1,)), ((), ())), preferred_element_type=F32)


def vmem(n):
    return [pl.BlockSpec(memory_space=pltpu.VMEM)] * n


SMEM = pl.BlockSpec(memory_space=pltpu.SMEM)


def pack_kernel(capacity, tile, rows, ids_ref, map_ref, held_ref, out_ref, spread_ref):
    me, plane = ids_ref[0], ids_ref[1]
    sectors, tiles = map_ref.shape
    count, width = held_ref.shape
    pool = count // tile
    blocks = width // 128
    local = map_ref[...] - me * pool
    mine = (local >= 0) & (local < pool)
    upto = onehot(iota((tiles, tiles), 0) <= iota((tiles, tiles), 1))
    rank = dot(onehot(mine), upto)
    slots = jnp.zeros((sectors, 128), F32)
    lane = iota((sectors, 128), 1)
    for s in range(capacity):
        hit = mine & (rank == F32(s + 1))
        value = jnp.sum(jnp.where(hit, local, 0).astype(F32), axis=1, keepdims=True)
        slots = slots + jnp.where(lane == s, value, F32(0.0))
    group = capacity * rows
    message = blocks * group
    total = sectors * group
    inner = iota((total, 1), 0) % group
    sector = iota((total, sectors), 0) // group
    spread = dot(onehot(sector == iota((total, sectors), 1)), slots.astype(BF16))
    slot = jnp.sum(jnp.where(iota((total, 128), 1) == inner // rows, spread, F32(0.0)), axis=1, keepdims=True)
    source = slot.astype(jnp.int32) * tile + plane * rows + inner % rows
    result = dot(onehot(source == iota((total, count), 1)), held_ref[...])
    for t in range(sectors):
        for b in range(blocks):
            at = t * message + b * group
            spread_ref[at : at + group, :] = result[t * group : (t + 1) * group, b * 128 : (b + 1) * 128]
    out_ref[...] = spread_ref[...].astype(BF16)


def unpack_kernel(capacity, pool, cores, rows, ids_ref, map_ref, own_ref, peer_ref, out_ref):
    core = ids_ref[2]
    tiles = map_ref.shape[1]
    width = out_ref.shape[1]
    blocks = width // 128
    group = capacity * rows
    message = blocks * group
    owner_row = jnp.broadcast_to(map_ref[...], (tiles, tiles)) // pool
    eye = iota((tiles, tiles), 0) == iota((tiles, tiles), 1)
    owner = jnp.sum(jnp.where(eye, owner_row, 0).astype(F32), axis=1, keepdims=True).astype(jnp.int32)
    before = (owner == owner_row) & (iota((tiles, tiles), 1) < iota((tiles, tiles), 0))
    rank = jnp.sum(jnp.where(before, F32(1.0), F32(0.0)), axis=1, keepdims=True).astype(jnp.int32)
    place = (owner // cores) * message + rank * rows + core
    own = jnp.where(owner % cores == core, place, -2 * message)
    peer = jnp.where(owner % cores == core, -2 * message, place)
    column = iota((tiles, own_ref.shape[0]), 1)
    for b in range(blocks):
        value = dot(onehot(column == own + b * group), own_ref[...])
        value = value + dot(onehot(column == peer + b * group), peer_ref[...])
        out_ref[:, b * 128 : (b + 1) * 128] = value.astype(BF16)


def fold_kernel(ids_ref, fields_ref, tensor_ref, mask_ref, own_ref, *rest):
    out_ref, weight_ref = rest[-2:]
    got = rest[: PLANES - 1]
    planes = PLANES
    plane = ids_ref[1]
    slab, step_rows, width = own_ref.shape
    slots = planes * slab
    states = out_ref.shape[2] // width
    pairs = out_ref.shape[0]
    cols = slots * states * states
    half = step_rows // 2
    rows = pairs * half
    total = states * rows
    deep = slots * half

    @pl.when(pl.program_id(0) == 0)
    def _():
        mask = mask_ref[...].astype(BF16)
        lanes_v = onehot(iota((slots, cols), 1) // (states * states) == iota((slots, cols), 0))
        base = tensor_ref[...] * dot(mask, lanes_v)
        w = iota((slots, cols), 0)
        lane = iota((slots, cols), 1)
        q, s = lane // states, lane % states
        first = F32(0.5) - (s // 2).astype(F32)
        second = F32(0.5) - (s % 2).astype(F32)
        onsite = fields_ref[0] * first + fields_ref[1] * second
        bond = ids_ref[3]
        base = base + jnp.where((w == bond - 1) & (q == s) & (lane < states * states), onsite, F32(0.0))
        high = base.astype(BF16)
        low = (base - high.astype(F32)).astype(BF16)
        row = iota((total, cols), 0)
        pair = (row // half) % pairs
        state = row // rows
        wanted = (plane * (pairs // states) + pair // states) * (states * states) + (pair % states) * states + state
        choose = onehot(wanted == iota((total, cols), 1))
        rel = iota((slots, deep), 1) // half
        absolute = ((plane - rel // slab + planes) % planes) * slab + rel % slab
        widen = onehot(absolute == iota((slots, deep), 0))
        diagonal = iota((total, deep), 0) % half == iota((total, deep), 1) % half
        for part, value in ((0, high), (1, low)):
            tall = dot_t(choose, value).astype(BF16)
            weight_ref[:, part * deep : (part + 1) * deep] = jnp.where(diagonal, dot(tall, widen), F32(0.0)).astype(BF16)

    env = jnp.concatenate([r[...] for r in (own_ref, *got)], axis=0).astype(F32)
    parts = []
    for h in range(2):
        part = env[:, h * half : (h + 1) * half, :].reshape(deep, width).astype(BF16)
        parts.append(jnp.concatenate([part, part], axis=0))
    for s in range(states):
        weight = weight_ref[s * rows : (s + 1) * rows, :]
        value = [dot(weight, part).reshape(pairs, half, width) for part in parts]
        out_ref[:, :, s * width : (s + 1) * width] = jnp.concatenate(value, axis=1).astype(BF16)


def apply_kernel(tile, ids_ref, kept_ref, *refs):
    pieces = refs[: 2 * PLANES]
    fold_ref, out_ref, ordered, natural, own, turned = refs[2 * PLANES :]
    plane, core = ids_ref[1], ids_ref[2]
    tiles, width = pieces[0].shape
    states = tiles * tile // width
    planes = len(pieces) // 2
    per_state = tiles // states
    share = own.shape[1]
    q = pl.program_id(1)

    @pl.when((pl.program_id(0) == 0) & (q == 0))
    def _():
        keep = iota((tiles, width), 1) < kept_ref[0]
        for d in range(planes):
            for other in range(2):
                r = ((plane - d + planes) % planes) * 2 + (core + other) % 2
                ordered[r] = jnp.where(keep, pieces[d * 2 + other][...], jnp.zeros((), BF16))
        n, k = iota((width, width), 0), iota((width, width), 1)
        turn = onehot((n % tile) * per_state + n // tile == k)
        for s in range(states):
            mixed = ordered[:, s * per_state : (s + 1) * per_state, :].reshape(width, width)
            value = dot(turn, mixed)
            rows = slice(s * width, (s + 1) * width)
            natural[rows, :] = value.astype(BF16)
            own[rows, :] = jnp.where(core == 0, value[:, :share], value[:, share:]).astype(BF16)

    mid = dot(fold_ref[0], own[...])
    turned[q] = jnp.swapaxes(mid, 0, 1).astype(BF16)

    @pl.when(q == states - 1)
    def _():
        total = dot(turned[0], natural[0:width, :])
        for s in range(1, states):
            total = total + dot(turned[s], natural[s * width : (s + 1) * width, :])
        out_ref[0, 0] = total


def fold(ids, fields, tensor, mask, own, got, half, chunk, previous, states):
    slab, width, _ = own.shape
    planes = len(got) + 1
    pairs = slab * states
    step = 16
    steps = got[0].shape[1] // step
    half_steps = width // 2 // step
    fixed = lambda shape: pl.BlockSpec(shape, lambda i, ids: (0,) * len(shape))
    at = lambda i, ids: ((ids[2] + half) % 2) * half_steps + chunk * steps + i
    in_specs = [
        SMEM,
        fixed(tensor.shape),
        fixed(mask.shape),
        pl.BlockSpec((slab, step, width), lambda i, ids: (0, at(i, ids), 0)),
    ] + [pl.BlockSpec((slab, step, width), lambda i, ids: (0, i, 0))] * len(got)
    args = [ids, fields, tensor, mask, own, *got]
    alias = {}
    if previous is not None:
        in_specs.append(pl.BlockSpec(memory_space=pl.ANY))
        alias = {len(args): 0}
        args.append(previous)
    slots = planes * slab
    return pl.pallas_call(
        fold_kernel,
        grid_spec=pltpu.PrefetchScalarGridSpec(
            num_scalar_prefetch=1,
            grid=(steps,),
            in_specs=in_specs,
            out_specs=pl.BlockSpec((pairs, step, states * width), lambda i, ids: (0, at(i, ids), 0)),
            scratch_shapes=[pltpu.VMEM((states * pairs * step // 2, slots * step), BF16)],
        ),
        out_shape=jax.ShapeDtypeStruct((pairs, width, states * width), BF16),
        input_output_aliases=alias,
        cost_estimate=pl.CostEstimate(flops=2 * steps * 1024 * 256 * width, bytes_accessed=6 << 20, transcendentals=0),
    )(*args)


def on_device(held, owner_map, kept, left_env, mpo_tensor, mpo_mask, fields):
    env_count = lax.axis_size("env")
    cores = lax.axis_size("col")
    planes = lax.axis_size("mpo")
    env_row = lax.axis_index("env")
    core = lax.axis_index("col")
    plane = lax.axis_index("mpo")
    pool, tile, width = held.shape
    tiles = owner_map.shape[1]
    states = tiles * tile // width
    capacity = 2 * tiles // (env_count * cores)
    rows = tile // planes
    slab = left_env.shape[0]
    slots = slab * planes
    bond = mpo_tensor.shape[0]
    ids = jnp.stack([env_row * cores + core, plane, core, jnp.int32(bond)]).astype(jnp.int32)

    def shift(x, axis, d):
        n = lax.axis_size(axis)
        return lax.ppermute(x, axis, [(i, (i + d) % n) for i in range(n)])

    env_own = left_env[:, 0]
    share_rows = width // cores
    piece_rows = share_rows // CHUNKS
    env_got, env_other = [], []
    for chunk in range(CHUNKS):
        part = lax.dynamic_slice_in_dim(env_own, core * share_rows + chunk * piece_rows, piece_rows, 1)
        env_got.append([shift(part, "mpo", d) for d in (1, 3, 2)])
        env_got[-1] = [env_got[-1][0], env_got[-1][2], env_got[-1][1]]
        env_other.append([shift(x, "col", 1) for x in env_got[-1]])

    message = rows * capacity * width // 128
    packed = pl.pallas_call(
        functools.partial(pack_kernel, capacity, tile, rows),
        in_specs=[SMEM] + vmem(2),
        out_specs=pl.BlockSpec(memory_space=pltpu.VMEM),
        out_shape=jax.ShapeDtypeStruct((env_count * message, 128), BF16),
        scratch_shapes=[pltpu.VMEM((env_count * message, 128), F32)],
        cost_estimate=pl.CostEstimate(flops=2 * 1536 * 1152 * 384, bytes_accessed=2 << 20, transcendentals=0),
        name="pack",
    )(ids, owner_map, held.reshape(pool * tile, width))
    arrived = lax.all_to_all(packed.reshape(env_count, message // 4, 4, 128), "env", 0, 0, tiled=True)

    tensor = jnp.pad(mpo_tensor.reshape(bond, bond * states * states), ((0, slots - bond), (0, (slots - bond) * states * states)))
    mask = jnp.pad(mpo_mask.astype(F32), ((0, slots - bond), (0, slots - bond)))
    folded = None
    for chunk in range(CHUNKS):
        for half, got in ((0, env_got[chunk]), (1, env_other[chunk])):
            folded = fold(ids, fields, tensor, mask, env_own, got, half, chunk, folded, states)

    map_here = lax.dynamic_slice_in_dim(owner_map, env_row, 1, 0)
    arrived = arrived.reshape(env_count * message, 128)
    swapped = shift(arrived, "col", 1)
    mine = pl.pallas_call(
        functools.partial(unpack_kernel, capacity, pool, cores, rows),
        in_specs=[SMEM] + vmem(3),
        out_specs=pl.BlockSpec(memory_space=pltpu.VMEM),
        out_shape=jax.ShapeDtypeStruct((tiles, width), BF16),
        cost_estimate=pl.CostEstimate(flops=2 * 384 * 1152 * 384, bytes_accessed=1 << 20, transcendentals=0),
        name="unpack",
    )(ids, map_here, arrived, swapped)
    by_plane = [mine]
    for d in range(1, planes):
        by_plane.append(shift(mine, "mpo", d))
    pieces = []
    for piece in by_plane:
        pieces += [piece, shift(piece, "col", 1)]

    share = width // cores
    result = pl.pallas_call(
        functools.partial(apply_kernel, tile),
        grid_spec=pltpu.PrefetchScalarGridSpec(
            num_scalar_prefetch=2,
            grid=(slab, states),
            in_specs=[pl.BlockSpec((tiles, width), lambda v, q, *_: (0, 0))] * (2 * planes)
            + [pl.BlockSpec((1, width, states * width), lambda v, q, *_: (v * states + q, 0, 0))],
            out_specs=pl.BlockSpec((1, 1, share, width), lambda v, q, *_: (v, 0, 0, 0)),
            scratch_shapes=[
                pltpu.VMEM((tile, tiles, width), BF16),
                pltpu.VMEM((states * width, width), BF16),
                pltpu.VMEM((states * width, share), BF16),
                pltpu.VMEM((states, share, width), BF16),
            ],
        ),
        out_shape=jax.ShapeDtypeStruct((slab, 1, share, width), F32),
        cost_estimate=pl.CostEstimate(flops=9 << 29, bytes_accessed=22 << 20, transcendentals=0),
        name="apply",
    )(ids, kept, *pieces, folded)
    return jnp.swapaxes(result, 2, 3)


def solution(mesh):
    return jax.shard_map(
        on_device,
        mesh=mesh,
        in_specs=(
            P(("real", "env", "col"), None, None),
            P("real", None),
            P(("real", "env")),
            P("mpo", ("real", "env"), None, None),
            P(),
            P(),
            P("real"),
        ),
        out_specs=P("mpo", ("real", "env"), None, "col"),
        check_vma=False,
    )
```

time: 238 us -> 195 us (0.82); the launches traced: 237 us -> 192 us
  blocking collectives: 135 us -> 0 us
  starting transfers between devices: 5.03 us -> 102 us
  Pallas kernels: 0 us -> 57.2 us
  matrix products: 25.6 us -> 0 us
  local copies, waits for them, and re-layouts: 28.6 us -> 6.95 us
  waiting for transfers between devices: 34.3 us -> 22.7 us
  other arithmetic: 8.04 us -> 1.3 us
    all_to_all x3 -> x0, blocking collectives: 135 us -> none  [the longest x1 98.7 us: on_device(): lax.all_to_all(outgoing, 'env', split_axis=0, concat_axis=0, tiled=True)]
    pallas_call x0 -> x7, Pallas kernels: none -> 57.2 us  [the longest x4 30.5 us: fold(): pl.pallas_call(fold_kernel, grid_spec=pltpu.PrefetchScalarGridSpec(num_sc...]
    ppermute x0 -> x20, starting transfers between devices: none -> 56.6 us  [shift(): return lax.ppermute(x, axis, [(i, (i + d) % n) for i in range(n)])]
    all_to_all x1, starting transfers between devices: 5.03 us -> 45.8 us  [on_device(): lax.all_to_all(packed.reshape(env_count, message // 4, 4, 128), 'env', 0,...]
    dot_general x3 -> x0, matrix products: 25.6 us -> none  [the longest x1 18.9 us: on_device(): jnp.einsum('wvts,wsia->vtia', mine_coupling, firsts, precision=leading_se...]
    all_to_all x1, waiting for transfers between devices: 34.3 us -> 22.6 us  [on_device(): lax.all_to_all(packed.reshape(env_count, message // 4, 4, 128), 'env', 0,...]
    transpose x1 -> x0, local copies, waits for them, and re-layouts: 7.64 us -> none  [in_order(): tiles = jnp.moveaxis(tiles, 0, dim)]
    another operation x2 -> x0, local copies, waits for them, and re-layouts: 7.02 us -> none  [the longest x1 7.01 us: on_device(): flat = arrived.reshape(env_count * core_count * capacity, tile * width)]
  transfers between devices with their start and end apart: 1 -> 21, of which waited for: 1 -> 1; matrix products, arithmetic and copies ran while one was open for 1% -> 3% of each run, Pallas kernels for 0% -> 17%
where the time goes in v1:
time: 195 us; the launch traced here: 192 us
  starting transfers between devices  102 us (52%)
  Pallas kernels  57.2 us (29%)
  waiting for transfers between devices  22.7 us (12%)
  local copies, waits for them, and re-layouts  6.95 us (4%)
    ppermute x20, starting transfers between devices, shift(): return lax.ppermute(x, axis, [(i, (i + d) % n) for i in range(n)])  56.6 us
    all_to_all x1, starting transfers between devices, on_device(): lax.all_to_all(packed.reshape(env_count, message // 4, 4, 128), 'env', 0,...  45.8 us
    pallas_call x4, Pallas kernels, fold(): pl.pallas_call(fold_kernel, grid_spec=pltpu.PrefetchScalarGridSpec(num_sc...  30.5 us
    all_to_all x1, waiting for transfers between devices, on_device(): lax.all_to_all(packed.reshape(env_count, message // 4, 4, 128), 'env', 0,...  22.6 us
    pallas_call x1, Pallas kernels, on_device(): pl.pallas_call(functools.partial(apply_kernel, tile), grid_spec=pltpu.Pre...  20.7 us
  transfers between devices with their start and end apart: 21, of which 1 were waited for; matrix products, arithmetic and copies ran while one was open for 3% of the time, Pallas kernels for 17%

profile of v1, /device:TPU:40, one launch (start us, length us, event | category | flops | bytes accessed | tf_op | source)
XLA Modules:
  0.0 191.6 jit_solution(16345083839345716496)
XLA Ops:
  0.6 3.3 %pack.1 = bf16[1152,128]{1,0:T(8,128)(2,1)} custom-call(s32[4]{0:T(128)} %pad_add_fusion.ids_ref, s32[32,192]{1,0:T(8,128)} %map_ref.1, bf16[1536,384]{1,0:T(8,128)(2,1)} %bitcast.21), custom_call_target="tpu_custom_call" | custom-call | flops 1358954496 | bytes 2097152 | tf_op jit(solution)/shard_map/pack/pallas_call | solution.py:255
  3.9 45.8 %all-to-all-start = ((bf16[32,9,4,128]{3,2,1,0:T(4,128)(2,1)}), bf16[32,9,4,128]{3,2,1,0:T(4,128)(2,1)S(1)}, u32[]{:S(2)}, u32[]{:S(2)}) async-start(bf16[32,9,4,128]{3,2,1,0:T(4,128)(2,1)} %bitcast.20), calls=%async_computation | async-start | bytes 589824 | tf_op jit(solution)/shard_map/all_to_all | solution.py:264
  50.8 3.6 %collective-permute-start.14 = (bf16[4,96,384]{2,1,0:T(8,128)(2,1)S(1)}, bf16[4,96,384]{2,1,0:T(8,128)(2,1)S(1)}, u32[]{:S(2)}, u32[]{:S(2)}) collective-permute-start(bf16[4,96,384]{2,1,0:T(8,128)(2,1)S(1)} %get-tuple-element.5), channel_id=1, source_target_pairs={{0,2},{2,4},{4,6},{6,0},{1,3},{3,5},{5,7},{7,1},{8,10},{10,12},{12... | collective-permute-start | bytes 884744 | tf_op jit(solution)/shard_map/ppermute | solution.py:242
  54.4 4.9 %collective-permute-start.16 = (bf16[4,96,384]{2,1,0:T(8,128)(2,1)S(1)}, bf16[4,96,384]{2,1,0:T(8,128)(2,1)S(1)}, u32[]{:S(2)}, u32[]{:S(2)}) collective-permute-start(bf16[4,96,384]{2,1,0:T(8,128)(2,1)S(1)} %get-tuple-element.5), channel_id=1, source_target_pairs={{0,4},{2,6},{4,0},{6,2},{1,5},{3,7},{5,1},{7,3},{8,12},{10,14},{12... | collective-permute-start | bytes 884744 | tf_op jit(solution)/shard_map/ppermute | solution.py:242
  59.3 3.2 %collective-permute-start.18 = (bf16[4,96,384]{2,1,0:T(8,128)(2,1)S(1)}, bf16[4,96,384]{2,1,0:T(8,128)(2,1)}, u32[]{:S(2)}, u32[]{:S(2)}) collective-permute-start(bf16[4,96,384]{2,1,0:T(8,128)(2,1)S(1)} %get-tuple-element.5), channel_id=1, source_target_pairs={{0,6},{2,0},{4,2},{6,4},{1,7},{3,1},{5,3},{7,5},{8,14},{10,8},{12,... | collective-permute-start | bytes 884744 | tf_op jit(solution)/shard_map/ppermute | solution.py:242
  62.5 2.2 %collective-permute-start.10 = (bf16[4,96,384]{2,1,0:T(8,128)(2,1)S(1)}, bf16[4,96,384]{2,1,0:T(8,128)(2,1)S(1)}, u32[]{:S(2)}, u32[]{:S(2)}) collective-permute-start(bf16[4,96,384]{2,1,0:T(8,128)(2,1)S(1)} %get-tuple-element.6), channel_id=1, source_target_pairs={{0,4},{2,6},{4,0},{6,2},{1,5},{3,7},{5,1},{7,3},{8,12},{10,14},{12... | collective-permute-start | bytes 884744 | tf_op jit(solution)/shard_map/ppermute | solution.py:242
  64.7 5.1 %collective-permute-start.12 = (bf16[4,96,384]{2,1,0:T(8,128)(2,1)S(1)}, bf16[4,96,384]{2,1,0:T(8,128)(2,1)S(1)}, u32[]{:S(2)}, u32[]{:S(2)}) collective-permute-start(bf16[4,96,384]{2,1,0:T(8,128)(2,1)S(1)} %get-tuple-element.6), channel_id=1, source_target_pairs={{0,6},{2,0},{4,2},{6,4},{1,7},{3,1},{5,3},{7,5},{8,14},{10,8},{12,... | collective-permute-start | bytes 884744 | tf_op jit(solution)/shard_map/ppermute | solution.py:242
  69.9 2.0 %collective-permute-start.8 = (bf16[4,96,384]{2,1,0:T(8,128)(2,1)S(1)}, bf16[4,96,384]{2,1,0:T(8,128)(2,1)S(1)}, u32[]{:S(2)}, u32[]{:S(2)}) collective-permute-start(bf16[4,96,384]{2,1,0:T(8,128)(2,1)S(1)} %get-tuple-element.6), channel_id=1, source_target_pairs={{0,2},{2,4},{4,6},{6,0},{1,3},{3,5},{5,7},{7,1},{8,10},{10,12},{12... | collective-permute-start | bytes 884744 | tf_op jit(solution)/shard_map/ppermute | solution.py:242
  71.8 22.6 %all-to-all-done = bf16[32,9,4,128]{3,2,1,0:T(4,128)(2,1)S(1)} async-done(((bf16[32,9,4,128]{3,2,1,0:T(4,128)(2,1)}), bf16[32,9,4,128]{3,2,1,0:T(4,128)(2,1)S(1)}, u32[]{:S(2)}, u32[]{:S(2)}) %all-to-all-start) | async-done | bytes 294944 | tf_op jit(solution)/shard_map/all_to_all | solution.py:264
  96.4 2.4 %collective-permute-start.15 = (bf16[4,96,384]{2,1,0:T(8,128)(2,1)S(1)}, bf16[4,96,384]{2,1,0:T(8,128)(2,1)S(1)}, u32[]{:S(2)}, u32[]{:S(2)}) collective-permute-start(bf16[4,96,384]{2,1,0:T(8,128)(2,1)S(1)} %collective-permute-done.14.rest_0_), channel_id=1, source_target_pairs={{0,1},{1,0},{2,3},{3,2},{4,5},{5,4},{6,7},{7,6},{8,9},{9,8},{10,11... | collective-permute-start | bytes 884744 | tf_op jit(solution)/shard_map/ppermute | solution.py:242
  100.9 2.4 %collective-permute-start.19 = (bf16[4,96,384]{2,1,0:T(8,128)(2,1)}, bf16[4,96,384]{2,1,0:T(8,128)(2,1)S(1)}, u32[]{:S(2)}, u32[]{:S(2)}) collective-permute-start(bf16[4,96,384]{2,1,0:T(8,128)(2,1)} %collective-permute-done.18.rest_2_), channel_id=1, source_target_pairs={{0,1},{1,0},{2,3},{3,2},{4,5},{5,4},{6,7},{7,6},{8,9},{9,8},{10,11... | collective-permute-start | bytes 884744 | tf_op jit(solution)/shard_map/ppermute | solution.py:242
  103.3 2.0 %collective-permute-start.11 = (bf16[4,96,384]{2,1,0:T(8,128)(2,1)S(1)}, bf16[4,96,384]{2,1,0:T(8,128)(2,1)S(1)}, u32[]{:S(2)}, u32[]{:S(2)}) collective-permute-start(bf16[4,96,384]{2,1,0:T(8,128)(2,1)S(1)} %collective-permute-done.10.rest_1_), channel_id=1, source_target_pairs={{0,1},{1,0},{2,3},{3,2},{4,5},{5,4},{6,7},{7,6},{8,9},{9,8},{10,11... | collective-permute-start | bytes 884744 | tf_op jit(solution)/shard_map/ppermute | solution.py:242
  105.3 2.4 %collective-permute-start.13 = (bf16[4,96,384]{2,1,0:T(8,128)(2,1)S(1)}, bf16[4,96,384]{2,1,0:T(8,128)(2,1)S(1)}, u32[]{:S(2)}, u32[]{:S(2)}) collective-permute-start(bf16[4,96,384]{2,1,0:T(8,128)(2,1)S(1)} %collective-permute-done.12.rest_2_), channel_id=1, source_target_pairs={{0,1},{1,0},{2,3},{3,2},{4,5},{5,4},{6,7},{7,6},{8,9},{9,8},{10,11... | collective-permute-start | bytes 884744 | tf_op jit(solution)/shard_map/ppermute | solution.py:242
  112.8 2.8 %unpack.1.refs_0_ = bf16[192,384]{1,0:T(8,128)(2,1)} custom-call(s32[4]{0:T(128)} %pad_add_fusion.ids_ref, s32[1,192]{1,0:T(1,128)} %constant_dynamic-slice_fusion.map_ref, bf16[1152,128]{1,0:T(8,128)(2,1)} %bitcast.19, bf16[1152,128]{1,0:T(8,128)(2,1)} %collective-permute-done.peer_ref), custom_call_target="tpu_custom_call" | custom-call | flops 339738624 | bytes 1048576 | tf_op jit(solution)/shard_map/unpack/pallas_call | solution.py:276
  117.5 3.6 %collective-permute-start.2 = (bf16[192,384]{1,0:T(8,128)(2,1)}, bf16[192,384]{1,0:T(8,128)(2,1)S(1)}, u32[]{:S(2)}, u32[]{:S(2)}) collective-permute-start(bf16[192,384]{1,0:T(8,128)(2,1)} %unpack.1.refs_0_), channel_id=1, source_target_pairs={{0,2},{2,4},{4,6},{6,0},{1,3},{3,5},{5,7},{7,1},{8,10},{10,12},{12... | collective-permute-start | bytes 442376 | tf_op jit(solution)/shard_map/ppermute | solution.py:242
  121.1 4.9 %collective-permute-start.4 = (bf16[192,384]{1,0:T(8,128)(2,1)}, bf16[192,384]{1,0:T(8,128)(2,1)}, u32[]{:S(2)}, u32[]{:S(2)}) collective-permute-start(bf16[192,384]{1,0:T(8,128)(2,1)} %unpack.1.refs_0_), channel_id=1, source_target_pairs={{0,4},{2,6},{4,0},{6,2},{1,5},{3,7},{5,1},{7,3},{8,12},{10,14},{12... | collective-permute-start | bytes 442376 | tf_op jit(solution)/shard_map/ppermute | solution.py:242
  126.1 3.2 %collective-permute-start.6 = (bf16[192,384]{1,0:T(8,128)(2,1)}, bf16[192,384]{1,0:T(8,128)(2,1)}, u32[]{:S(2)}, u32[]{:S(2)}) collective-permute-start(bf16[192,384]{1,0:T(8,128)(2,1)} %unpack.1.refs_0_), channel_id=1, source_target_pairs={{0,6},{2,0},{4,2},{6,4},{1,7},{3,1},{5,3},{7,5},{8,14},{10,8},{12,... | collective-permute-start | bytes 442376 | tf_op jit(solution)/shard_map/ppermute | solution.py:242
  129.4 7.6 %shard_map.73.rest_3_ = bf16[16,384,1536]{2,1,0:T(8,128)(2,1)} custom-call(s32[4]{0:T(128)} %pad_add_fusion.ids_ref, f32[2]{0:T(128)} %fields_ref.7, f32[16,256]{1,0:T(8,128)} %pad.8.tensor_ref, f32[16,16]{1,0:T(8,128)} %pad.9.mask_ref, bf16[4,384,384]{2,1,0:T(8,128)(2,1)} %bitcast.13, bf16[4,96,384]{2,1,0:T(8,128)(2,1)} %copy-done.10, ...), custom_call_target="tpu_custom_call" | custom-call | flops 1207959552 | bytes 6291456 | tf_op jit(solution)/shard_map/pallas_call | solution.py:208
  137.0 7.7 %shard_map.74.rest_3_ = bf16[16,384,1536]{2,1,0:T(8,128)(2,1)} custom-call(s32[4]{0:T(128)} %pad_add_fusion.ids_ref, f32[2]{0:T(128)} %fields_ref.7, f32[16,256]{1,0:T(8,128)} %pad.8.tensor_ref, f32[16,16]{1,0:T(8,128)} %pad.9.mask_ref, bf16[4,384,384]{2,1,0:T(8,128)(2,1)} %bitcast.14, ...), custom_call_target="tpu_custom_call", output_to_operand_aliasing={{}: (8, {})} | custom-call | flops 1207959552 | bytes 6291456 | tf_op jit(solution)/shard_map/pallas_call | solution.py:208
  146.8 2.4 %collective-permute-start.3 = (bf16[192,384]{1,0:T(8,128)(2,1)S(1)}, bf16[192,384]{1,0:T(8,128)(2,1)S(1)}, u32[]{:S(2)}, u32[]{:S(2)}) collective-permute-start(bf16[192,384]{1,0:T(8,128)(2,1)S(1)} %collective-permute-done.2.refs_2_), channel_id=1, source_target_pairs={{0,1},{1,0},{2,3},{3,2},{4,5},{5,4},{6,7},{7,6},{8,9},{9,8},{10,11... | collective-permute-start | bytes 442376 | tf_op jit(solution)/shard_map/ppermute | solution.py:242
  151.2 2.4 %collective-permute-start.7 = (bf16[192,384]{1,0:T(8,128)(2,1)}, bf16[192,384]{1,0:T(8,128)(2,1)S(1)}, u32[]{:S(2)}, u32[]{:S(2)}) collective-permute-start(bf16[192,384]{1,0:T(8,128)(2,1)} %collective-permute-done.6.refs_6_), channel_id=1, source_target_pairs={{0,1},{1,0},{2,3},{3,2},{4,5},{5,4},{6,7},{7,6},{8,9},{9,8},{10,11... | collective-permute-start | bytes 442376 | tf_op jit(solution)/shard_map/ppermute | solution.py:242
  153.6 7.6 %shard_map.75.rest_3_ = bf16[16,384,1536]{2,1,0:T(8,128)(2,1)} custom-call(s32[4]{0:T(128)} %pad_add_fusion.ids_ref, f32[2]{0:T(128)} %fields_ref.7, f32[16,256]{1,0:T(8,128)} %pad.8.tensor_ref, f32[16,16]{1,0:T(8,128)} %pad.9.mask_ref, bf16[4,384,384]{2,1,0:T(8,128)(2,1)} %bitcast.15, ...), custom_call_target="tpu_custom_call", output_to_operand_aliasing={{}: (8, {})} | custom-call | flops 1207959552 | bytes 6291456 | tf_op jit(solution)/shard_map/pallas_call | solution.py:208
  161.9 7.6 %shard_map.76.refs_8_ = bf16[16,384,1536]{2,1,0:T(8,128)(2,1)} custom-call(s32[4]{0:T(128)} %pad_add_fusion.ids_ref, f32[2]{0:T(128)} %fields_ref.7, f32[16,256]{1,0:T(8,128)} %pad.8.tensor_ref, f32[16,16]{1,0:T(8,128)} %pad.9.mask_ref, bf16[4,384,384]{2,1,0:T(8,128)(2,1)} %bitcast.16, ...), custom_call_target="tpu_custom_call", output_to_operand_aliasing={{}: (8, {})} | custom-call | flops 1207959552 | bytes 6291456 | tf_op jit(solution)/shard_map/pallas_call | solution.py:208
  170.9 20.7 %apply.1 = f32[4,1,192,384]{3,2,1,0:T(8,128)} custom-call(s32[4]{0:T(128)} %pad_add_fusion.ids_ref, s32[1]{0:T(128)S(6)} %copy.17.kept_ref, bf16[192,384]{1,0:T(8,128)(2,1)} %unpack.1.refs_0_, bf16[192,384]{1,0:T(8,128)(2,1)} %copy-done.14, bf16[192,384]{1,0:T(8,128)(2,1)} %copy-done.13, bf16[192,384]{1,0:T(8,128)(2,1)} %copy-done.15, ...), custom_call_target="tpu_custom_call" | custom-call | flops 4831838208 | bytes 23068672 | tf_op jit(solution)/shard_map/apply/pallas_call | solution.py:292
  (69 shorter events, 18.0 us)
Async XLA Ops:
  3.9 90.6 %all-to-all-start = ((bf16[32,9,4,128]{3,2,1,0:T(4,128)(2,1)}), bf16[32,9,4,128]{3,2,1,0:T(4,128)(2,1)S(1)}, u32[]{:S(2)}, u32[]{:S(2)}) async-start(bf16[32,9,4,128]{3,2,1,0:T(4,128)(2,1)} %bitcast.20), calls=%async_computation | async-start | bytes 589824 | tf_op jit(solution)/shard_map/all_to_all | solution.py:264
  50.8 19.1 %collective-permute-start.14 = (bf16[4,96,384]{2,1,0:T(8,128)(2,1)S(1)}, bf16[4,96,384]{2,1,0:T(8,128)(2,1)S(1)}, u32[]{:S(2)}, u32[]{:S(2)}) collective-permute-start(bf16[4,96,384]{2,1,0:T(8,128)(2,1)S(1)} %get-tuple-element.5), channel_id=1, source_target_pairs={{0,2},{2,4},{4,6},{6,0},{1,3},{3,5},{5,7},{7,1},{8,10},{10,12},{12... | collective-permute-start | bytes 884744 | tf_op jit(solution)/shard_map/ppermute | solution.py:242
  54.4 17.5 %collective-permute-start.16 = (bf16[4,96,384]{2,1,0:T(8,128)(2,1)S(1)}, bf16[4,96,384]{2,1,0:T(8,128)(2,1)S(1)}, u32[]{:S(2)}, u32[]{:S(2)}) collective-permute-start(bf16[4,96,384]{2,1,0:T(8,128)(2,1)S(1)} %get-tuple-element.5), channel_id=1, source_target_pairs={{0,4},{2,6},{4,0},{6,2},{1,5},{3,7},{5,1},{7,3},{8,12},{10,14},{12... | collective-permute-start | bytes 884744 | tf_op jit(solution)/shard_map/ppermute | solution.py:242
  59.3 37.1 %collective-permute-start.18 = (bf16[4,96,384]{2,1,0:T(8,128)(2,1)S(1)}, bf16[4,96,384]{2,1,0:T(8,128)(2,1)}, u32[]{:S(2)}, u32[]{:S(2)}) collective-permute-start(bf16[4,96,384]{2,1,0:T(8,128)(2,1)S(1)} %get-tuple-element.5), channel_id=1, source_target_pairs={{0,6},{2,0},{4,2},{6,4},{1,7},{3,1},{5,3},{7,5},{8,14},{10,8},{12,... | collective-permute-start | bytes 884744 | tf_op jit(solution)/shard_map/ppermute | solution.py:242
  62.5 36.3 %collective-permute-start.10 = (bf16[4,96,384]{2,1,0:T(8,128)(2,1)S(1)}, bf16[4,96,384]{2,1,0:T(8,128)(2,1)S(1)}, u32[]{:S(2)}, u32[]{:S(2)}) collective-permute-start(bf16[4,96,384]{2,1,0:T(8,128)(2,1)S(1)} %get-tuple-element.6), channel_id=1, source_target_pairs={{0,4},{2,6},{4,0},{6,2},{1,5},{3,7},{5,1},{7,3},{8,12},{10,14},{12... | collective-permute-start | bytes 884744 | tf_op jit(solution)/shard_map/ppermute | solution.py:242
  64.7 36.1 %collective-permute-start.12 = (bf16[4,96,384]{2,1,0:T(8,128)(2,1)S(1)}, bf16[4,96,384]{2,1,0:T(8,128)(2,1)S(1)}, u32[]{:S(2)}, u32[]{:S(2)}) collective-permute-start(bf16[4,96,384]{2,1,0:T(8,128)(2,1)S(1)} %get-tuple-element.6), channel_id=1, source_target_pairs={{0,6},{2,0},{4,2},{6,4},{1,7},{3,1},{5,3},{7,5},{8,14},{10,8},{12,... | collective-permute-start | bytes 884744 | tf_op jit(solution)/shard_map/ppermute | solution.py:242
  69.8 59.5 %copy-start.10 = (bf16[4,96,384]{2,1,0:T(8,128)(2,1)}, bf16[4,96,384]{2,1,0:T(8,128)(2,1)S(1)}, u32[]{:S(2)}) copy-start(bf16[4,96,384]{2,1,0:T(8,128)(2,1)S(1)} %collective-permute-done.14.rest_0_) | copy-start | bytes 884740
  69.9 33.4 %collective-permute-start.8 = (bf16[4,96,384]{2,1,0:T(8,128)(2,1)S(1)}, bf16[4,96,384]{2,1,0:T(8,128)(2,1)S(1)}, u32[]{:S(2)}, u32[]{:S(2)}) collective-permute-start(bf16[4,96,384]{2,1,0:T(8,128)(2,1)S(1)} %get-tuple-element.6), channel_id=1, source_target_pairs={{0,2},{2,4},{4,6},{6,0},{1,3},{3,5},{5,7},{7,1},{8,10},{10,12},{12... | collective-permute-start | bytes 884744 | tf_op jit(solution)/shard_map/ppermute | solution.py:242
  71.8 57.5 %copy-start.11 = (bf16[4,96,384]{2,1,0:T(8,128)(2,1)}, bf16[4,96,384]{2,1,0:T(8,128)(2,1)S(1)}, u32[]{:S(2)}) copy-start(bf16[4,96,384]{2,1,0:T(8,128)(2,1)S(1)} %collective-permute-done.16.rest_1_) | copy-start | bytes 884740
  94.4 10.8 %collective-permute-start = (bf16[1152,128]{1,0:T(8,128)(2,1)S(1)}, bf16[1152,128]{1,0:T(8,128)(2,1)}, u32[]{:S(2)}, u32[]{:S(2)}) collective-permute-start(bf16[1152,128]{1,0:T(8,128)(2,1)S(1)} %bitcast.18), channel_id=1, source_target_pairs={{0,1},{1,0},{2,3},{3,2},{4,5},{5,4},{6,7},{7,6},{8,9},{9,8},{10,11... | collective-permute-start | bytes 884744 | tf_op jit(solution)/shard_map/ppermute | solution.py:242
  96.4 19.2 %collective-permute-start.15 = (bf16[4,96,384]{2,1,0:T(8,128)(2,1)S(1)}, bf16[4,96,384]{2,1,0:T(8,128)(2,1)S(1)}, u32[]{:S(2)}, u32[]{:S(2)}) collective-permute-start(bf16[4,96,384]{2,1,0:T(8,128)(2,1)S(1)} %collective-permute-done.14.rest_0_), channel_id=1, source_target_pairs={{0,1},{1,0},{2,3},{3,2},{4,5},{5,4},{6,7},{7,6},{8,9},{9,8},{10,11... | collective-permute-start | bytes 884744 | tf_op jit(solution)/shard_map/ppermute | solution.py:242
  98.9 45.9 %copy-start = (bf16[4,96,384]{2,1,0:T(8,128)(2,1)}, bf16[4,96,384]{2,1,0:T(8,128)(2,1)S(1)}, u32[]{:S(2)}) copy-start(bf16[4,96,384]{2,1,0:T(8,128)(2,1)S(1)} %collective-permute-done.10.rest_1_) | copy-start | bytes 884740
  98.9 18.6 %collective-permute-start.17 = (bf16[4,96,384]{2,1,0:T(8,128)(2,1)S(1)}, bf16[4,96,384]{2,1,0:T(8,128)(2,1)S(1)}, u32[]{:S(2)}, u32[]{:S(2)}) collective-permute-start(bf16[4,96,384]{2,1,0:T(8,128)(2,1)S(1)} %collective-permute-done.16.rest_1_), channel_id=1, source_target_pairs={{0,1},{1,0},{2,3},{3,2},{4,5},{5,4},{6,7},{7,6},{8,9},{9,8},{10,11... | collective-permute-start | bytes 884744 | tf_op jit(solution)/shard_map/ppermute | solution.py:242
  100.9 20.3 %collective-permute-start.19 = (bf16[4,96,384]{2,1,0:T(8,128)(2,1)}, bf16[4,96,384]{2,1,0:T(8,128)(2,1)S(1)}, u32[]{:S(2)}, u32[]{:S(2)}) collective-permute-start(bf16[4,96,384]{2,1,0:T(8,128)(2,1)} %collective-permute-done.18.rest_2_), channel_id=1, source_target_pairs={{0,1},{1,0},{2,3},{3,2},{4,5},{5,4},{6,7},{7,6},{8,9},{9,8},{10,11... | collective-permute-start | bytes 884744 | tf_op jit(solution)/shard_map/ppermute | solution.py:242
  103.3 22.8 %collective-permute-start.11 = (bf16[4,96,384]{2,1,0:T(8,128)(2,1)S(1)}, bf16[4,96,384]{2,1,0:T(8,128)(2,1)S(1)}, u32[]{:S(2)}, u32[]{:S(2)}) collective-permute-start(bf16[4,96,384]{2,1,0:T(8,128)(2,1)S(1)} %collective-permute-done.10.rest_1_), channel_id=1, source_target_pairs={{0,1},{1,0},{2,3},{3,2},{4,5},{5,4},{6,7},{7,6},{8,9},{9,8},{10,11... | collective-permute-start | bytes 884744 | tf_op jit(solution)/shard_map/ppermute | solution.py:242
  105.3 39.5 %collective-permute-start.13 = (bf16[4,96,384]{2,1,0:T(8,128)(2,1)S(1)}, bf16[4,96,384]{2,1,0:T(8,128)(2,1)S(1)}, u32[]{:S(2)}, u32[]{:S(2)}) collective-permute-start(bf16[4,96,384]{2,1,0:T(8,128)(2,1)S(1)} %collective-permute-done.12.rest_2_), channel_id=1, source_target_pairs={{0,1},{1,0},{2,3},{3,2},{4,5},{5,4},{6,7},{7,6},{8,9},{9,8},{10,11... | collective-permute-start | bytes 884744 | tf_op jit(solution)/shard_map/ppermute | solution.py:242
  115.6 45.6 %collective-permute-start.9 = (bf16[4,96,384]{2,1,0:T(8,128)(2,1)S(1)}, bf16[4,96,384]{2,1,0:T(8,128)(2,1)S(1)}, u32[]{:S(2)}, u32[]{:S(2)}) collective-permute-start(bf16[4,96,384]{2,1,0:T(8,128)(2,1)S(1)} %collective-permute-done.8.rest_0_), channel_id=1, source_target_pairs={{0,1},{1,0},{2,3},{3,2},{4,5},{5,4},{6,7},{7,6},{8,9},{9,8},{10,11... | collective-permute-start | bytes 884744 | tf_op jit(solution)/shard_map/ppermute | solution.py:242
  117.5 29.2 %collective-permute-start.2 = (bf16[192,384]{1,0:T(8,128)(2,1)}, bf16[192,384]{1,0:T(8,128)(2,1)S(1)}, u32[]{:S(2)}, u32[]{:S(2)}) collective-permute-start(bf16[192,384]{1,0:T(8,128)(2,1)} %unpack.1.refs_0_), channel_id=1, source_target_pairs={{0,2},{2,4},{4,6},{6,0},{1,3},{3,5},{5,7},{7,1},{8,10},{10,12},{12... | collective-permute-start | bytes 442376 | tf_op jit(solution)/shard_map/ppermute | solution.py:242
  121.1 28.1 %collective-permute-start.4 = (bf16[192,384]{1,0:T(8,128)(2,1)}, bf16[192,384]{1,0:T(8,128)(2,1)}, u32[]{:S(2)}, u32[]{:S(2)}) collective-permute-start(bf16[192,384]{1,0:T(8,128)(2,1)} %unpack.1.refs_0_), channel_id=1, source_target_pairs={{0,4},{2,6},{4,0},{6,2},{1,5},{3,7},{5,1},{7,3},{8,12},{10,14},{12... | collective-permute-start | bytes 442376 | tf_op jit(solution)/shard_map/ppermute | solution.py:242
  126.1 25.1 %collective-permute-start.6 = (bf16[192,384]{1,0:T(8,128)(2,1)}, bf16[192,384]{1,0:T(8,128)(2,1)}, u32[]{:S(2)}, u32[]{:S(2)}) collective-permute-start(bf16[192,384]{1,0:T(8,128)(2,1)} %unpack.1.refs_0_), channel_id=1, source_target_pairs={{0,6},{2,0},{4,2},{6,4},{1,7},{3,1},{5,3},{7,5},{8,14},{10,8},{12,... | collective-permute-start | bytes 442376 | tf_op jit(solution)/shard_map/ppermute | solution.py:242
  144.8 24.7 %collective-permute-start.1 = (bf16[192,384]{1,0:T(8,128)(2,1)S(1)}, bf16[192,384]{1,0:T(8,128)(2,1)S(1)}, u32[]{:S(2)}, u32[]{:S(2)}) collective-permute-start(bf16[192,384]{1,0:T(8,128)(2,1)S(1)} %copy-done.12), channel_id=1, source_target_pairs={{0,1},{1,0},{2,3},{3,2},{4,5},{5,4},{6,7},{7,6},{8,9},{9,8},{10,11... | collective-permute-start | bytes 442376 | tf_op jit(solution)/shard_map/ppermute | solution.py:242
  146.8 22.7 %collective-permute-start.3 = (bf16[192,384]{1,0:T(8,128)(2,1)S(1)}, bf16[192,384]{1,0:T(8,128)(2,1)S(1)}, u32[]{:S(2)}, u32[]{:S(2)}) collective-permute-start(bf16[192,384]{1,0:T(8,128)(2,1)S(1)} %collective-permute-done.2.refs_2_), channel_id=1, source_target_pairs={{0,1},{1,0},{2,3},{3,2},{4,5},{5,4},{6,7},{7,6},{8,9},{9,8},{10,11... | collective-permute-start | bytes 442376 | tf_op jit(solution)/shard_map/ppermute | solution.py:242
  149.2 20.3 %collective-permute-start.5 = (bf16[192,384]{1,0:T(8,128)(2,1)}, bf16[192,384]{1,0:T(8,128)(2,1)S(1)}, u32[]{:S(2)}, u32[]{:S(2)}) collective-permute-start(bf16[192,384]{1,0:T(8,128)(2,1)} %collective-permute-done.4.refs_4_), channel_id=1, source_target_pairs={{0,1},{1,0},{2,3},{3,2},{4,5},{5,4},{6,7},{7,6},{8,9},{9,8},{10,11... | collective-permute-start | bytes 442376 | tf_op jit(solution)/shard_map/ppermute | solution.py:242
  151.2 18.4 %collective-permute-start.7 = (bf16[192,384]{1,0:T(8,128)(2,1)}, bf16[192,384]{1,0:T(8,128)(2,1)S(1)}, u32[]{:S(2)}, u32[]{:S(2)}) collective-permute-start(bf16[192,384]{1,0:T(8,128)(2,1)} %collective-permute-done.6.refs_6_), channel_id=1, source_target_pairs={{0,1},{1,0},{2,3},{3,2},{4,5},{5,4},{6,7},{7,6},{8,9},{9,8},{10,11... | collective-permute-start | bytes 442376 | tf_op jit(solution)/shard_map/ppermute | solution.py:242
  (15 other events, 221.2 us)

commit v2 on v1

v2 whole, which is shorter than its diff:
```python
import functools

import jax
import jax.numpy as jnp
from jax import lax
from jax.experimental import pallas as pl
from jax.experimental.pallas import tpu as pltpu
from jax.sharding import PartitionSpec as P


F32 = jnp.float32
BF16 = jnp.bfloat16


def iota(shape, dim):
    return lax.broadcasted_iota(jnp.int32, shape, dim)


def onehot(condition):
    return jnp.where(condition, F32(1.0), F32(0.0)).astype(BF16)


def dot(a, b):
    return lax.dot_general(a, b, (((1,), (0,)), ((), ())), preferred_element_type=F32)


def dot_t(a, b):
    return lax.dot_general(a, b, (((1,), (1,)), ((), ())), preferred_element_type=F32)


def vmem(n):
    return [pl.BlockSpec(memory_space=pltpu.VMEM)] * n


SMEM = pl.BlockSpec(memory_space=pltpu.SMEM)


def pack_kernel(capacity, tile, rows, ids_ref, map_ref, held_ref, out_ref, spread_ref):
    me, plane = ids_ref[0], ids_ref[1]
    sectors, tiles = map_ref.shape
    count, width = held_ref.shape
    pool = count // tile
    blocks = width // 128
    local = map_ref[...] - me * pool
    mine = (local >= 0) & (local < pool)
    upto = onehot(iota((tiles, tiles), 0) <= iota((tiles, tiles), 1))
    rank = dot(onehot(mine), upto)
    slots = jnp.zeros((sectors, 128), F32)
    lane = iota((sectors, 128), 1)
    for s in range(capacity):
        hit = mine & (rank == F32(s + 1))
        value = jnp.sum(jnp.where(hit, local, 0).astype(F32), axis=1, keepdims=True)
        slots = slots + jnp.where(lane == s, value, F32(0.0))
    group = capacity * rows
    message = blocks * group
    total = sectors * group
    inner = iota((total, 1), 0) % group
    sector = iota((total, sectors), 0) // group
    spread = dot(onehot(sector == iota((total, sectors), 1)), slots.astype(BF16))
    slot = jnp.sum(jnp.where(iota((total, 128), 1) == inner // rows, spread, F32(0.0)), axis=1, keepdims=True)
    source = slot.astype(jnp.int32) * tile + plane * rows + inner % rows
    result = dot(onehot(source == iota((total, count), 1)), held_ref[...])
    for t in range(sectors):
        for b in range(blocks):
            at = t * message + b * group
            spread_ref[at : at + group, :] = result[t * group : (t + 1) * group, b * 128 : (b + 1) * 128]
    out_ref[...] = spread_ref[...].astype(BF16)


def unpack_kernel(capacity, pool, cores, rows, ids_ref, map_ref, own_ref, peer_ref, out_ref):
    core = ids_ref[2]
    tiles = map_ref.shape[1]
    width = out_ref.shape[1]
    blocks = width // 128
    group = capacity * rows
    message = blocks * group
    owner_row = jnp.broadcast_to(map_ref[...], (tiles, tiles)) // pool
    eye = iota((tiles, tiles), 0) == iota((tiles, tiles), 1)
    owner = jnp.sum(jnp.where(eye, owner_row, 0).astype(F32), axis=1, keepdims=True).astype(jnp.int32)
    before = (owner == owner_row) & (iota((tiles, tiles), 1) < iota((tiles, tiles), 0))
    rank = jnp.sum(jnp.where(before, F32(1.0), F32(0.0)), axis=1, keepdims=True).astype(jnp.int32)
    place = (owner // cores) * message + rank * rows + core
    own = jnp.where(owner % cores == core, place, -2 * message)
    peer = jnp.where(owner % cores == core, -2 * message, place)
    column = iota((tiles, own_ref.shape[0]), 1)
    for b in range(blocks):
        value = dot(onehot(column == own + b * group), own_ref[...])
        value = value + dot(onehot(column == peer + b * group), peer_ref[...])
        out_ref[:, b * 128 : (b + 1) * 128] = value.astype(BF16)


def fold_kernel(ids_ref, fields_ref, tensor_ref, mask_ref, own_ref, got_ref, out_ref, weight_ref):
    plane = ids_ref[1]
    slab, step_rows, width = own_ref.shape
    slots = slab + got_ref.shape[0]
    planes = slots // slab
    states = out_ref.shape[2] // width
    pairs = out_ref.shape[0]
    cols = slots * states * states
    half = 8
    rows = pairs * half
    total = states * rows
    deep = slots * half

    @pl.when(pl.program_id(0) == 0)
    def _():
        mask = mask_ref[...].astype(BF16)
        lanes_v = onehot(iota((slots, cols), 1) // (states * states) == iota((slots, cols), 0))
        base = tensor_ref[...] * dot(mask, lanes_v)
        w = iota((slots, cols), 0)
        lane = iota((slots, cols), 1)
        q, s = lane // states, lane % states
        first = F32(0.5) - (s // 2).astype(F32)
        second = F32(0.5) - (s % 2).astype(F32)
        onsite = fields_ref[0] * first + fields_ref[1] * second
        bond = ids_ref[3]
        base = base + jnp.where((w == bond - 1) & (q == s) & (lane < states * states), onsite, F32(0.0))
        high = base.astype(BF16)
        low = (base - high.astype(F32)).astype(BF16)
        row = iota((total, cols), 0)
        pair = (row // half) % pairs
        state = row // rows
        wanted = (plane * (pairs // states) + pair // states) * (states * states) + (pair % states) * states + state
        choose = onehot(wanted == iota((total, cols), 1))
        slot = iota((slots, deep), 1) // half
        slot = (plane - slot // slab + planes) % planes * slab + slot % slab
        widen = onehot(slot == iota((slots, deep), 0))
        diagonal = iota((total, deep), 0) % half == iota((total, deep), 1) % half
        for part, value in ((0, high), (1, low)):
            tall = dot_t(choose, value).astype(BF16)
            weight_ref[:, part * deep : (part + 1) * deep] = jnp.where(diagonal, dot(tall, widen), F32(0.0)).astype(BF16)

    for at in range(0, step_rows, 16):
        env = jnp.concatenate([own_ref[:, at : at + 16, :], got_ref[:, at : at + 16, :]], axis=0).astype(F32)
        side = jnp.concatenate([env[:, h * half : (h + 1) * half, :].reshape(deep, width) for h in range(2)], axis=1)
        side = side.astype(BF16)
        value = dot(weight_ref[...], jnp.concatenate([side, side], axis=0))
        for s in range(states):
            part = [
                value[s * rows : (s + 1) * rows, h * width : (h + 1) * width].reshape(pairs, half, width)
                for h in range(2)
            ]
            out_ref[:, at : at + 16, s * width : (s + 1) * width] = jnp.concatenate(part, axis=1).astype(BF16)


def apply_kernel(tile, ids_ref, kept_ref, mine_ref, twin_ref, near_ref, far_ref, out_ref, ordered, halves, own, turned):
    core = ids_ref[2]
    planes, tiles, width = mine_ref.shape
    states = tiles * tile // width
    per_state = tiles // states
    share = own.shape[1]

    @pl.when(pl.program_id(0) == 0)
    def _():
        keep = iota((tiles, width), 1) < kept_ref[0]
        for p in range(planes):
            for other, ref in ((0, mine_ref), (1, twin_ref)):
                ordered[p * 2 + (core + other) % 2] = jnp.where(keep, ref[p], jnp.zeros((), BF16))
        n, k = iota((width, width), 0), iota((width, width), 1)
        turn = onehot((n % tile) * per_state + n // tile == k)
        for s in range(states):
            mixed = ordered[:, s * per_state : (s + 1) * per_state, :].reshape(width, width)
            value = dot(turn, mixed)
            own[s * width : (s + 1) * width, :] = jnp.where(core == 0, value[:, :share], value[:, share:]).astype(BF16)
            first = pl.multiple_of(s * width + core * share, share)
            second = pl.multiple_of(s * width + (1 - core) * share, share)
            halves[pl.ds(first, share), :] = value[:share].astype(BF16)
            halves[pl.ds(second, share), :] = value[share:].astype(BF16)

    for q in range(states):
        mid = dot(jnp.concatenate([near_ref[q], far_ref[q]], axis=0), own[...])
        turned[:, q * width : (q + 1) * width] = jnp.swapaxes(mid, 0, 1).astype(BF16)
    out_ref[0, 0] = dot(turned[...], halves[...])


def fold(ids, fields, tensor, mask, own, got, half, states):
    others, count, width = got.shape
    slab = own.shape[0]
    slots, pairs = slab + others, slab * states
    step = 48
    steps = count // step
    fixed = lambda shape: pl.BlockSpec(shape, lambda i, ids: (0,) * len(shape))
    return pl.pallas_call(
        fold_kernel,
        grid_spec=pltpu.PrefetchScalarGridSpec(
            num_scalar_prefetch=1,
            grid=(steps,),
            in_specs=[
                SMEM,
                fixed(tensor.shape),
                fixed(mask.shape),
                pl.BlockSpec((slab, step, width), lambda i, ids: (0, ((ids[2] + half) % 2) * steps + i, 0)),
                pl.BlockSpec((others, step, width), lambda i, ids: (0, i, 0)),
            ],
            out_specs=pl.BlockSpec((pairs, step, states * width), lambda i, ids: (0, i, 0)),
            scratch_shapes=[pltpu.VMEM((states * pairs * 8, slots * 16), BF16)],
        ),
        out_shape=jax.ShapeDtypeStruct((pairs, count, states * width), BF16),
        cost_estimate=pl.CostEstimate(flops=2 * steps * 1024 * 256 * width, bytes_accessed=12 << 20, transcendentals=0),
    )(ids, fields, tensor, mask, own, got)


def call_pack(ids, owner_map, held, capacity, tile, rows):
    sectors, width = owner_map.shape[0], held.shape[1]
    count = sectors * rows * capacity * width // 128
    return pl.pallas_call(
        functools.partial(pack_kernel, capacity, tile, rows),
        in_specs=[SMEM] + vmem(2),
        out_specs=pl.BlockSpec(memory_space=pltpu.VMEM),
        out_shape=jax.ShapeDtypeStruct((count, 128), BF16),
        scratch_shapes=[pltpu.VMEM((count, 128), F32)],
        cost_estimate=pl.CostEstimate(flops=1 << 29, bytes_accessed=2 << 20, transcendentals=0),
        name="pack",
    )(ids, owner_map, held)


def call_unpack(ids, map_here, arrived, swapped, capacity, pool, cores, rows):
    tiles = map_here.shape[1]
    width = arrived.size // (tiles * rows)
    return pl.pallas_call(
        functools.partial(unpack_kernel, capacity, pool, cores, rows),
        in_specs=[SMEM] + vmem(3),
        out_specs=pl.BlockSpec(memory_space=pltpu.VMEM),
        out_shape=jax.ShapeDtypeStruct((tiles, width), BF16),
        cost_estimate=pl.CostEstimate(flops=2 * 384 * 1152 * 384, bytes_accessed=1 << 20, transcendentals=0),
        name="unpack",
    )(ids, map_here, arrived, swapped)


def call_apply(ids, kept, by_plane, by_twin, near, far, tile):
    planes, tiles, width = by_plane.shape
    pairs, share, deep = near.shape
    states = deep // width
    slab = pairs // states
    whole = lambda v, *_: (0, 0, 0)
    return pl.pallas_call(
        functools.partial(apply_kernel, tile),
        grid_spec=pltpu.PrefetchScalarGridSpec(
            num_scalar_prefetch=2,
            grid=(slab,),
            in_specs=[pl.BlockSpec((planes, tiles, width), whole)] * 2
            + [pl.BlockSpec((states, share, deep), lambda v, *_: (v, 0, 0))] * 2,
            out_specs=pl.BlockSpec((1, 1, share, width), lambda v, *_: (v, 0, 0, 0)),
            scratch_shapes=[
                pltpu.VMEM((tile, tiles, width), BF16),
                pltpu.VMEM((deep, width), BF16),
                pltpu.VMEM((deep, share), BF16),
                pltpu.VMEM((share, deep), BF16),
            ],
        ),
        out_shape=jax.ShapeDtypeStruct((slab, 1, share, width), F32),
        cost_estimate=pl.CostEstimate(flops=9 << 29, bytes_accessed=22 << 20, transcendentals=0),
        name="apply",
    )(ids, kept, by_plane, by_twin, near, far)


def on_device(held, owner_map, kept, left_env, mpo_tensor, mpo_mask, fields):
    env_count = lax.axis_size("env")
    cores = lax.axis_size("col")
    planes = lax.axis_size("mpo")
    env_row = lax.axis_index("env")
    core = lax.axis_index("col")
    plane = lax.axis_index("mpo")
    pool, tile, width = held.shape
    tiles = owner_map.shape[1]
    states = tiles * tile // width
    capacity = 2 * tiles // (env_count * cores)
    rows = tile // planes
    slab = left_env.shape[0]
    slots = slab * planes
    bond = mpo_tensor.shape[0]
    ids = jnp.stack([env_row * cores + core, plane, core, jnp.int32(bond)]).astype(jnp.int32)

    def twin(x):
        return lax.ppermute(x, "col", [(0, 1), (1, 0)])

    def gather(x):
        return lax.all_to_all(jnp.broadcast_to(x, (planes, *x.shape)), "mpo", 0, 0, tiled=True)

    message = rows * capacity * width // 128
    packed = call_pack(ids, owner_map, held.reshape(pool * tile, width), capacity, tile, rows)
    arrived = lax.all_to_all(packed.reshape(env_count, message // 4, 4, 128), "env", 0, 0, tiled=True)

    share = width // cores
    env_own = left_env[:, 0]
    env_half = lax.dynamic_slice_in_dim(env_own, core * share, share, 1)
    step = lambda x, d: lax.ppermute(x, "mpo", [(i, (i + d) % planes) for i in range(planes)])
    from_left, from_right = step(env_half, 1), step(env_half, -1)
    ring = [(i * cores + c, (i + 1 - 2 * c) % planes * cores + c) for i in range(planes) for c in range(cores)]
    from_far = lax.ppermute(jnp.where(core == 0, from_left, from_right), ("mpo", "col"), ring)
    env_got = jnp.concatenate([from_left, from_far, from_right], axis=0)

    tensor = jnp.pad(
        mpo_tensor.reshape(bond, bond * states * states), ((0, slots - bond), (0, (slots - bond) * states * states))
    )
    mask = jnp.pad(mpo_mask.astype(F32), ((0, slots - bond), (0, slots - bond)))
    map_here = lax.dynamic_slice_in_dim(owner_map, env_row, 1, 0)
    env_got, tensor, mask, map_here = lax.optimization_barrier((env_got, tensor, mask, map_here))
    env_twin = twin(env_got)
    folded_mine = fold(ids, fields, tensor, mask, env_own, env_got, 0, states)
    folded_twin = fold(ids, fields, tensor, mask, env_own, env_twin, 1, states)

    arrived = arrived.reshape(env_count * message, 128)
    swapped = twin(arrived)
    mine = call_unpack(ids, map_here, arrived, swapped, capacity, pool, cores, rows)
    by_plane = gather(mine)
    by_twin = twin(by_plane)

    result = call_apply(ids, kept, by_plane, by_twin, folded_mine, folded_twin, tile)
    return jnp.swapaxes(result, 2, 3)


def solution(mesh):
    return jax.shard_map(
        on_device,
        mesh=mesh,
        in_specs=(
            P(("real", "env", "col"), None, None),
            P("real", None),
            P(("real", "env")),
            P("mpo", ("real", "env"), None, None),
            P(),
            P(),
            P("real"),
        ),
        out_specs=P("mpo", ("real", "env"), None, "col"),
        check_vma=False,
    )
```

time: 195 us -> 153 us (0.78)
  starting transfers between devices: 102 us -> 62.4 us
  Pallas kernels: 57.2 us -> 36.1 us
  blocking collectives: 0 us -> 14.9 us
  waiting for transfers between devices: 22.7 us -> 30.7 us
    ppermute x20 -> x6, starting transfers between devices: 56.6 us -> 16.5 us  [the longest x2 7.11 us: on_device(): lax.ppermute(x, 'mpo', [(i, (i + d) % planes) for i in range(planes)])]
    ppermute x20 -> x6, waiting for transfers between devices: 0.05 us -> 21.3 us  [the longest x2 12.9 us: on_device(): lax.ppermute(x, 'mpo', [(i, (i + d) % planes) for i in range(planes)])]
    all_to_all x0 -> x1, blocking collectives: none -> 14.9 us  [gather(): lax.all_to_all(jnp.broadcast_to(x, (planes, *x.shape)), 'mpo', 0, 0, tile...]
    pallas_call x4 -> x2, Pallas kernels: 30.5 us -> 17.2 us  [fold(): pl.pallas_call(fold_kernel, grid_spec=pltpu.PrefetchScalarGridSpec(num_sc...]
    all_to_all x1, waiting for transfers between devices: 22.6 us -> 9.41 us  [on_device(): lax.all_to_all(packed.reshape(env_count, message // 4, 4, 128), 'env', 0,...]
    pallas_call x3, Pallas kernels: 26.7 us -> 18.9 us  [the longest x1 12.9 us: call_apply(): pl.pallas_call(functools.partial(apply_kernel, tile), grid_spec=pltpu.Pre...]
  transfers between devices with their start and end apart: 21 -> 7, of which waited for: 1 -> 5; matrix products, arithmetic and copies ran while one was open for 3% -> 3% of each run, Pallas kernels for 17% -> 13%
where the time goes in v2:
time: 153 us; the launch traced here: 151 us
  starting transfers between devices  62.4 us (41%)
  Pallas kernels  36.1 us (24%)
  waiting for transfers between devices  30.7 us (20%)
  blocking collectives  14.9 us (10%)
  local copies, waits for them, and re-layouts  5.4 us (4%)
    all_to_all x1, starting transfers between devices, on_device(): lax.all_to_all(packed.reshape(env_count, message // 4, 4, 128), 'env', 0,...  45.9 us
    pallas_call x2, Pallas kernels, fold(): pl.pallas_call(fold_kernel, grid_spec=pltpu.PrefetchScalarGridSpec(num_sc...  17.2 us
    all_to_all x1, blocking collectives, gather(): lax.all_to_all(jnp.broadcast_to(x, (planes, *x.shape)), 'mpo', 0, 0, tile...  14.9 us
    ppermute x2, waiting for transfers between devices, on_device(): lax.ppermute(x, 'mpo', [(i, (i + d) % planes) for i in range(planes)])  12.9 us
    pallas_call x1, Pallas kernels, call_apply(): pl.pallas_call(functools.partial(apply_kernel, tile), grid_spec=pltpu.Pre...  12.9 us
    all_to_all x1, waiting for transfers between devices, on_device(): lax.all_to_all(packed.reshape(env_count, message // 4, 4, 128), 'env', 0,...  9.41 us
    ppermute x2, starting transfers between devices, on_device(): lax.ppermute(x, 'mpo', [(i, (i + d) % planes) for i in range(planes)])  7.11 us
    ppermute x1, waiting for transfers between devices, on_device(): lax.ppermute(jnp.where(core == 0, from_left, from_right), ('mpo', 'col'),...  6.62 us
  transfers between devices with their start and end apart: 7, of which 5 were waited for; matrix products, arithmetic and copies ran while one was open for 3% of the time, Pallas kernels for 13%

profile of v2, /device:TPU:40, one launch (start us, length us, event | category | flops | bytes accessed | tf_op | source)
XLA Modules:
  0.0 151.2 jit_solution(9074174043349175500)
XLA Ops:
  0.6 3.3 %pack.1 = bf16[1152,128]{1,0:T(8,128)(2,1)} custom-call(s32[4]{0:T(128)} %pad_add_fusion.ids_ref, s32[32,192]{1,0:T(8,128)} %map_ref.1, bf16[1536,384]{1,0:T(8,128)(2,1)} %bitcast.15), custom_call_target="tpu_custom_call" | custom-call | flops 536870912 | bytes 2097152 | tf_op jit(solution)/shard_map/pack/pallas_call | solution.py:206
  3.9 45.9 %all-to-all-start = ((bf16[32,9,4,128]{3,2,1,0:T(4,128)(2,1)}), bf16[32,9,4,128]{3,2,1,0:T(4,128)(2,1)}, u32[]{:S(2)}, u32[]{:S(2)}) async-start(bf16[32,9,4,128]{3,2,1,0:T(4,128)(2,1)} %bitcast.14), calls=%async_computation | async-start | bytes 589824 | tf_op jit(solution)/shard_map/all_to_all | solution.py:282
  49.9 3.6 %collective-permute-start = (bf16[4,192,384]{2,1,0:T(8,128)(2,1)S(1)}, bf16[4,192,384]{2,1,0:T(8,128)(2,1)S(1)}, u32[]{:S(2)}, u32[]{:S(2)}) collective-permute-start(bf16[4,192,384]{2,1,0:T(8,128)(2,1)S(1)} %dynamic-slice_bitcast_fusion), channel_id=1, source_target_pairs={{0,2},{2,4},{4,6},{6,0},{1,3},{3,5},{5,7},{7,1},{8,10},{10,12},{12... | collective-permute-start | bytes 1769480 | tf_op jit(solution)/shard_map/ppermute | solution.py:287
  53.4 3.6 %collective-permute-start.1 = (bf16[4,192,384]{2,1,0:T(8,128)(2,1)S(1)}, bf16[4,192,384]{2,1,0:T(8,128)(2,1)S(1)}, u32[]{:S(2)}, u32[]{:S(2)}) collective-permute-start(bf16[4,192,384]{2,1,0:T(8,128)(2,1)S(1)} %dynamic-slice_bitcast_fusion), channel_id=1, source_target_pairs={{0,6},{2,0},{4,2},{6,4},{1,7},{3,1},{5,3},{7,5},{8,14},{10,8},{12,... | collective-permute-start | bytes 1769480 | tf_op jit(solution)/shard_map/ppermute | solution.py:287
  57.0 11.1 %collective-permute-done = bf16[4,192,384]{2,1,0:T(8,128)(2,1)S(1)} collective-permute-done((bf16[4,192,384]{2,1,0:T(8,128)(2,1)S(1)}, bf16[4,192,384]{2,1,0:T(8,128)(2,1)S(1)}, u32[]{:S(2)}, u32[]{:S(2)}) %collective-permute-start) | collective-permute-done | bytes 589856 | tf_op jit(solution)/shard_map/ppermute | solution.py:287
  68.1 1.9 %collective-permute-done.1 = bf16[4,192,384]{2,1,0:T(8,128)(2,1)S(1)} collective-permute-done((bf16[4,192,384]{2,1,0:T(8,128)(2,1)S(1)}, bf16[4,192,384]{2,1,0:T(8,128)(2,1)S(1)}, u32[]{:S(2)}, u32[]{:S(2)}) %collective-permute-start.1) | collective-permute-done | bytes 589856 | tf_op jit(solution)/shard_map/ppermute | solution.py:287
  70.0 3.6 %collective-permute-start.2 = (bf16[4,192,384]{2,1,0:T(8,128)(2,1)S(1)}, bf16[4,192,384]{2,1,0:T(8,128)(2,1)S(1)}, u32[]{:S(2)}, u32[]{:S(2)}) collective-permute-start(bf16[4,192,384]{2,1,0:T(8,128)(2,1)S(1)} %broadcast_select_fusion), channel_id=1, source_target_pairs={{0,2},{1,7},{2,4},{3,1},{4,6},{5,3},{6,0},{7,5},{8,10},{9,15},{10,... | collective-permute-start | bytes 1769480 | tf_op jit(solution)/shard_map/ppermute | solution.py:290
  73.9 0.6 pad.8.tensor_ref
  74.5 0.6 pad.9.mask_ref
  75.1 1.3 constant_dynamic-slice_fusion.map_ref
  76.4 6.6 %collective-permute-done.2 = bf16[4,192,384]{2,1,0:T(8,128)(2,1)S(1)} collective-permute-done((bf16[4,192,384]{2,1,0:T(8,128)(2,1)S(1)}, bf16[4,192,384]{2,1,0:T(8,128)(2,1)S(1)}, u32[]{:S(2)}, u32[]{:S(2)}) %collective-permute-start.2) | collective-permute-done | bytes 589856 | tf_op jit(solution)/shard_map/ppermute | solution.py:290
  83.3 2.0 %collective-permute-start.5 = (bf16[12,192,384]{2,1,0:T(8,128)(2,1)S(1)}, bf16[12,192,384]{2,1,0:T(8,128)(2,1)}, u32[]{:S(2)}, u32[]{:S(2)}) collective-permute-start(bf16[12,192,384]{2,1,0:T(8,128)(2,1)S(1)} %pad_maximum_fusion.got_ref), channel_id=1, source_target_pairs={{0,1},{1,0},{2,3},{3,2},{4,5},{5,4},{6,7},{7,6},{8,9},{9,8},{10,11... | collective-permute-start | bytes 5308424 | tf_op jit(solution)/shard_map/ppermute | solution.py:275
  85.2 9.4 %all-to-all-done = bf16[32,9,4,128]{3,2,1,0:T(4,128)(2,1)} async-done(((bf16[32,9,4,128]{3,2,1,0:T(4,128)(2,1)}), bf16[32,9,4,128]{3,2,1,0:T(4,128)(2,1)}, u32[]{:S(2)}, u32[]{:S(2)}) %all-to-all-start) | async-done | bytes 294944 | tf_op jit(solution)/shard_map/all_to_all | solution.py:282
  94.7 1.9 %collective-permute-start.3 = (bf16[1152,128]{1,0:T(8,128)(2,1)}, bf16[1152,128]{1,0:T(8,128)(2,1)S(1)}, u32[]{:S(2)}, u32[]{:S(2)}) collective-permute-start(bf16[1152,128]{1,0:T(8,128)(2,1)} %bitcast.7.own_ref), channel_id=1, source_target_pairs={{0,1},{1,0},{2,3},{3,2},{4,5},{5,4},{6,7},{7,6},{8,9},{9,8},{10,11... | collective-permute-start | bytes 884744 | tf_op jit(solution)/shard_map/ppermute | solution.py:275
  96.6 1.8 %collective-permute-done.3.peer_ref = bf16[1152,128]{1,0:T(8,128)(2,1)S(1)} collective-permute-done((bf16[1152,128]{1,0:T(8,128)(2,1)}, bf16[1152,128]{1,0:T(8,128)(2,1)S(1)}, u32[]{:S(2)}, u32[]{:S(2)}) %collective-permute-start.3) | collective-permute-done | bytes 294944 | tf_op jit(solution)/shard_map/ppermute | solution.py:275
  98.4 0.7 copy-done.6
  99.1 2.7 %unpack.1 = bf16[192,384]{1,0:T(8,128)(2,1)} custom-call(s32[4]{0:T(128)} %pad_add_fusion.ids_ref, s32[1,192]{1,0:T(1,128)} %constant_dynamic-slice_fusion.map_ref, bf16[1152,128]{1,0:T(8,128)(2,1)} %bitcast.7.own_ref, bf16[1152,128]{1,0:T(8,128)(2,1)} %copy-done.6), custom_call_target="tpu_custom_call" | custom-call | flops 339738624 | bytes 1048576 | tf_op jit(solution)/shard_map/unpack/pallas_call | solution.py:220
  101.8 1.0 broadcast_in_dim.3
  102.8 14.9 %all_to_all.10.mine_ref = bf16[4,192,384]{2,1,0:T(8,128)(2,1)S(1)} all-to-all(bf16[4,192,384]{2,1,0:T(8,128)(2,1)S(1)} %broadcast_in_dim.3), channel_id=1, replica_groups=mesh['real'=2,'env'=32,'mpo'=4,'col'=2] {'mpo'}, dimensions={0} | all-to-all | bytes 1179648 | tf_op jit(solution)/shard_map/all_to_all | solution.py:278
  117.7 1.9 %collective-permute-start.4 = (bf16[4,192,384]{2,1,0:T(8,128)(2,1)S(1)}, bf16[4,192,384]{2,1,0:T(8,128)(2,1)S(1)}, u32[]{:S(2)}, u32[]{:S(2)}) collective-permute-start(bf16[4,192,384]{2,1,0:T(8,128)(2,1)S(1)} %all_to_all.10.mine_ref), channel_id=1, source_target_pairs={{0,1},{1,0},{2,3},{3,2},{4,5},{5,4},{6,7},{7,6},{8,9},{9,8},{10,11... | collective-permute-start | bytes 1769480 | tf_op jit(solution)/shard_map/ppermute | solution.py:275
  120.3 8.6 %shard_map.73.near_ref = bf16[16,192,1536]{2,1,0:T(8,128)(2,1)} custom-call(s32[4]{0:T(128)} %pad_add_fusion.ids_ref, f32[2]{0:T(128)} %fields_ref.3, f32[16,256]{1,0:T(8,128)} %pad.8.tensor_ref, f32[16,16]{1,0:T(8,128)} %pad.9.mask_ref, bf16[4,384,384]{2,1,0:T(8,128)(2,1)} %bitcast.11, bf16[12,192,384]{2,1,0:T(8,128)(2,1)} %copy-done.1), custom_call_target="tpu_custom_call" | custom-call | flops 805306368 | bytes 12582912 | tf_op jit(solution)/shard_map/pallas_call | solution.py:183
  128.9 8.5 %shard_map.74.far_ref = bf16[16,192,1536]{2,1,0:T(8,128)(2,1)} custom-call(s32[4]{0:T(128)} %pad_add_fusion.ids_ref, f32[2]{0:T(128)} %fields_ref.3, f32[16,256]{1,0:T(8,128)} %pad.8.tensor_ref, f32[16,16]{1,0:T(8,128)} %pad.9.mask_ref, bf16[4,384,384]{2,1,0:T(8,128)(2,1)} %bitcast.12, bf16[12,192,384]{2,1,0:T(8,128)(2,1)} %collective-permute-done.5.got_ref), custom_call_target="tpu_custom_call" | custom-call | flops 805306368 | bytes 12582912 | tf_op jit(solution)/shard_map/pallas_call | solution.py:183
  137.5 0.8 copy-done.3
  138.3 12.9 %apply.1 = f32[4,1,192,384]{3,2,1,0:T(8,128)} custom-call(s32[4]{0:T(128)} %pad_add_fusion.ids_ref, s32[1]{0:T(128)S(6)} %copy.11.kept_ref, bf16[4,192,384]{2,1,0:T(8,128)(2,1)} %copy-done.2, bf16[4,192,384]{2,1,0:T(8,128)(2,1)} %copy-done.3, bf16[16,192,1536]{2,1,0:T(8,128)(2,1)} %shard_map.73.near_ref, bf16[16,192,1536]{2,1,0:T(8,128)(2,1)} %shard_map.74.far_ref), custom_call_target="tpu_custom_call" | custom-call | flops 4831838208 | bytes 23068672 | tf_op jit(solution)/shard_map/apply/pallas_call | solution.py:236
  (21 shorter events, 1.3 us)
Async XLA Ops:
  0.0 49.8 %copy-start = (bf16[4,1,384,384]{3,2,1,0:T(8,128)(2,1)S(1)}, bf16[4,1,384,384]{3,2,1,0:T(8,128)(2,1)}, u32[]{:S(2)}) copy-start(bf16[4,1,384,384]{3,2,1,0:T(8,128)(2,1)} %param.10) | copy-start | bytes 3538948
  3.9 69.7 %copy-start.4 = (f32[14,14,4,4]{1,3,2,0:T(4,128)S(1)}, f32[14,14,4,4]{1,3,2,0:T(4,128)}, u32[]{:S(2)}) copy-start(f32[14,14,4,4]{1,3,2,0:T(4,128)} %param.11) | copy-start | bytes 37636
  3.9 90.8 %all-to-all-start = ((bf16[32,9,4,128]{3,2,1,0:T(4,128)(2,1)}), bf16[32,9,4,128]{3,2,1,0:T(4,128)(2,1)}, u32[]{:S(2)}, u32[]{:S(2)}) async-start(bf16[32,9,4,128]{3,2,1,0:T(4,128)(2,1)} %bitcast.14), calls=%async_computation | async-start | bytes 589824 | tf_op jit(solution)/shard_map/all_to_all | solution.py:282
  49.8 24.1 %copy-start.5 = (s32[14,14]{1,0:T(8,128)S(1)}, s32[14,14]{1,0:T(8,128)}, u32[]{:S(2)}) copy-start(s32[14,14]{1,0:T(8,128)} %param.12) | copy-start | bytes 2356
  49.9 18.2 %collective-permute-start = (bf16[4,192,384]{2,1,0:T(8,128)(2,1)S(1)}, bf16[4,192,384]{2,1,0:T(8,128)(2,1)S(1)}, u32[]{:S(2)}, u32[]{:S(2)}) collective-permute-start(bf16[4,192,384]{2,1,0:T(8,128)(2,1)S(1)} %dynamic-slice_bitcast_fusion), channel_id=1, source_target_pairs={{0,2},{2,4},{4,6},{6,0},{1,3},{3,5},{5,7},{7,1},{8,10},{10,12},{12... | collective-permute-start | bytes 1769480 | tf_op jit(solution)/shard_map/ppermute | solution.py:287
  53.4 16.5 %collective-permute-start.1 = (bf16[4,192,384]{2,1,0:T(8,128)(2,1)S(1)}, bf16[4,192,384]{2,1,0:T(8,128)(2,1)S(1)}, u32[]{:S(2)}, u32[]{:S(2)}) collective-permute-start(bf16[4,192,384]{2,1,0:T(8,128)(2,1)S(1)} %dynamic-slice_bitcast_fusion), channel_id=1, source_target_pairs={{0,6},{2,0},{4,2},{6,4},{1,7},{3,1},{5,3},{7,5},{8,14},{10,8},{12,... | collective-permute-start | bytes 1769480 | tf_op jit(solution)/shard_map/ppermute | solution.py:287
  70.0 13.0 %collective-permute-start.2 = (bf16[4,192,384]{2,1,0:T(8,128)(2,1)S(1)}, bf16[4,192,384]{2,1,0:T(8,128)(2,1)S(1)}, u32[]{:S(2)}, u32[]{:S(2)}) collective-permute-start(bf16[4,192,384]{2,1,0:T(8,128)(2,1)S(1)} %broadcast_select_fusion), channel_id=1, source_target_pairs={{0,2},{1,7},{2,4},{3,1},{4,6},{5,3},{6,0},{7,5},{8,10},{9,15},{10,... | collective-permute-start | bytes 1769480 | tf_op jit(solution)/shard_map/ppermute | solution.py:290
  83.3 37.0 %copy-start.1 = (bf16[12,192,384]{2,1,0:T(8,128)(2,1)}, bf16[12,192,384]{2,1,0:T(8,128)(2,1)S(1)}, u32[]{:S(2)}) copy-start(bf16[12,192,384]{2,1,0:T(8,128)(2,1)S(1)} %pad_maximum_fusion.got_ref) | copy-start | bytes 5308420
  83.3 45.6 %collective-permute-start.5 = (bf16[12,192,384]{2,1,0:T(8,128)(2,1)S(1)}, bf16[12,192,384]{2,1,0:T(8,128)(2,1)}, u32[]{:S(2)}, u32[]{:S(2)}) collective-permute-start(bf16[12,192,384]{2,1,0:T(8,128)(2,1)S(1)} %pad_maximum_fusion.got_ref), channel_id=1, source_target_pairs={{0,1},{1,0},{2,3},{3,2},{4,5},{5,4},{6,7},{7,6},{8,9},{9,8},{10,11... | collective-permute-start | bytes 5308424 | tf_op jit(solution)/shard_map/ppermute | solution.py:275
  94.7 3.7 %collective-permute-start.3 = (bf16[1152,128]{1,0:T(8,128)(2,1)}, bf16[1152,128]{1,0:T(8,128)(2,1)S(1)}, u32[]{:S(2)}, u32[]{:S(2)}) collective-permute-start(bf16[1152,128]{1,0:T(8,128)(2,1)} %bitcast.7.own_ref), channel_id=1, source_target_pairs={{0,1},{1,0},{2,3},{3,2},{4,5},{5,4},{6,7},{7,6},{8,9},{9,8},{10,11... | collective-permute-start | bytes 884744 | tf_op jit(solution)/shard_map/ppermute | solution.py:275
  98.4 0.7 copy-start.6
  117.7 11.3 %copy-start.2 = (bf16[4,192,384]{2,1,0:T(8,128)(2,1)}, bf16[4,192,384]{2,1,0:T(8,128)(2,1)S(1)}, u32[]{:S(2)}) copy-start(bf16[4,192,384]{2,1,0:T(8,128)(2,1)S(1)} %all_to_all.10.mine_ref) | copy-start | bytes 1769476
  117.7 19.8 %collective-permute-start.4 = (bf16[4,192,384]{2,1,0:T(8,128)(2,1)S(1)}, bf16[4,192,384]{2,1,0:T(8,128)(2,1)S(1)}, u32[]{:S(2)}, u32[]{:S(2)}) collective-permute-start(bf16[4,192,384]{2,1,0:T(8,128)(2,1)S(1)} %all_to_all.10.mine_ref), channel_id=1, source_target_pairs={{0,1},{1,0},{2,3},{3,2},{4,5},{5,4},{6,7},{7,6},{8,9},{9,8},{10,11... | collective-permute-start | bytes 1769480 | tf_op jit(solution)/shard_map/ppermute | solution.py:275
  137.4 0.8 copy-start.3

commit v3 on v2

--- a/solution.py
+++ b/solution.py
@@ -10,6 +10,10 @@
 
 F32 = jnp.float32
 BF16 = jnp.bfloat16
+
+
+GROUP = 8
+CHUNKS = 2
 
 
 def iota(shape, dim):
@@ -70,7 +74,7 @@
 def unpack_kernel(capacity, pool, cores, rows, ids_ref, map_ref, own_ref, peer_ref, out_ref):
     core = ids_ref[2]
     tiles = map_ref.shape[1]
-    width = out_ref.shape[1]
+    width = out_ref.shape[2]
     blocks = width // 128
     group = capacity * rows
     message = blocks * group
@@ -86,64 +90,79 @@
     for b in range(blocks):
         value = dot(onehot(column == own + b * group), own_ref[...])
         value = value + dot(onehot(column == peer + b * group), peer_ref[...])
-        out_ref[:, b * 128 : (b + 1) * 128] = value.astype(BF16)
-
-
-def fold_kernel(ids_ref, fields_ref, tensor_ref, mask_ref, own_ref, got_ref, out_ref, weight_ref):
+        for copy in range(out_ref.shape[0]):
+            out_ref[copy, :, b * 128 : (b + 1) * 128] = value.astype(BF16)
+
+
+def weight_kernel(slab, states, group, ids_ref, fields_ref, tensor_ref, mask_ref, out_ref):
     plane = ids_ref[1]
+    slots, cols = tensor_ref.shape
+    planes = slots // slab
+    pairs = slab * states
+    rows = pairs * group
+    total = states * rows
+    deep = slots * group
+    mask = mask_ref[...].astype(BF16)
+    lanes_v = onehot(iota((slots, cols), 1) // (states * states) == iota((slots, cols), 0))
+    base = tensor_ref[...] * dot(mask, lanes_v)
+    w = iota((slots, cols), 0)
+    lane = iota((slots, cols), 1)
+    q, s = lane // states, lane % states
+    first = F32(0.5) - (s // 2).astype(F32)
+    second = F32(0.5) - (s % 2).astype(F32)
+    onsite = fields_ref[0] * first + fields_ref[1] * second
+    base = base + jnp.where((w == ids_ref[3] - 1) & (q == s) & (lane < states * states), onsite, F32(0.0))
+    high = base.astype(BF16)
+    low = (base - high.astype(F32)).astype(BF16)
+    row = iota((total, cols), 0)
+    pair = (row // group) % pairs
+    state = row // rows
+    wanted = (plane * slab + pair // states) * (states * states) + (pair % states) * states + state
+    choose = onehot(wanted == iota((total, cols), 1))
+    slot = iota((slots, deep), 1) // group
+    slot = (plane - slot // slab + planes) % planes * slab + slot % slab
+    widen = onehot(slot == iota((slots, deep), 0))
+    diagonal = iota((total, deep), 0) % group == iota((total, deep), 1) % group
+    for part, value in ((0, high), (1, low)):
+        tall = dot_t(choose, value).astype(BF16)
+        out_ref[:, part * deep : (part + 1) * deep] = jnp.where(diagonal, dot(tall, widen), F32(0.0)).astype(BF16)
+
+
+def call_weights(ids, fields, tensor, mask, slab, states):
+    slots = tensor.shape[0]
+    return pl.pallas_call(
+        functools.partial(weight_kernel, slab, states, GROUP),
+        in_specs=[SMEM] * 2 + vmem(2),
+        out_specs=pl.BlockSpec(memory_space=pltpu.VMEM),
+        out_shape=jax.ShapeDtypeStruct((states * slab * states * GROUP, 2 * slots * GROUP), BF16),
+        cost_estimate=pl.CostEstimate(flops=1 << 28, bytes_accessed=1 << 19, transcendentals=0),
+        name="weights",
+    )(ids, fields, tensor, mask)
+
+
+def fold_kernel(ids_ref, weight_ref, own_ref, got_ref, out_ref):
     slab, step_rows, width = own_ref.shape
     slots = slab + got_ref.shape[0]
-    planes = slots // slab
     states = out_ref.shape[2] // width
     pairs = out_ref.shape[0]
-    cols = slots * states * states
-    half = 8
-    rows = pairs * half
-    total = states * rows
-    deep = slots * half
-
-    @pl.when(pl.program_id(0) == 0)
-    def _():
-        mask = mask_ref[...].astype(BF16)
-        lanes_v = onehot(iota((slots, cols), 1) // (states * states) == iota((slots, cols), 0))
-        base = tensor_ref[...] * dot(mask, lanes_v)
-        w = iota((slots, cols), 0)
-        lane = iota((slots, cols), 1)
-        q, s = lane // states, lane % states
-        first = F32(0.5) - (s // 2).astype(F32)
-        second = F32(0.5) - (s % 2).astype(F32)
-        onsite = fields_ref[0] * first + fields_ref[1] * second
-        bond = ids_ref[3]
-        base = base + jnp.where((w == bond - 1) & (q == s) & (lane < states * states), onsite, F32(0.0))
-        high = base.astype(BF16)
-        low = (base - high.astype(F32)).astype(BF16)
-        row = iota((total, cols), 0)
-        pair = (row // half) % pairs
-        state = row // rows
-        wanted = (plane * (pairs // states) + pair // states) * (states * states) + (pair % states) * states + state
-        choose = onehot(wanted == iota((total, cols), 1))
-        slot = iota((slots, deep), 1) // half
-        slot = (plane - slot // slab + planes) % planes * slab + slot % slab
-        widen = onehot(slot == iota((slots, deep), 0))
-        diagonal = iota((total, deep), 0) % half == iota((total, deep), 1) % half
-        for part, value in ((0, high), (1, low)):
-            tall = dot_t(choose, value).astype(BF16)
-            weight_ref[:, part * deep : (part + 1) * deep] = jnp.where(diagonal, dot(tall, widen), F32(0.0)).astype(BF16)
-
-    for at in range(0, step_rows, 16):
-        env = jnp.concatenate([own_ref[:, at : at + 16, :], got_ref[:, at : at + 16, :]], axis=0).astype(F32)
-        side = jnp.concatenate([env[:, h * half : (h + 1) * half, :].reshape(deep, width) for h in range(2)], axis=1)
-        side = side.astype(BF16)
+    rows = pairs * GROUP
+    for at in range(0, step_rows, 2 * GROUP):
+        here = slice(at, at + 2 * GROUP)
+        env = jnp.concatenate([own_ref[:, here, :], got_ref[:, here, :]], axis=0).astype(F32)
+        side = [env[:, h * GROUP : (h + 1) * GROUP, :].reshape(slots * GROUP, width) for h in range(2)]
+        side = jnp.concatenate(side, axis=1).astype(BF16)
         value = dot(weight_ref[...], jnp.concatenate([side, side], axis=0))
         for s in range(states):
             part = [
-                value[s * rows : (s + 1) * rows, h * width : (h + 1) * width].reshape(pairs, half, width)
+                value[s * rows : (s + 1) * rows, h * width : (h + 1) * width].reshape(pairs, GROUP, width)
                 for h in range(2)
             ]
-            out_ref[:, at : at + 16, s * width : (s + 1) * width] = jnp.concatenate(part, axis=1).astype(BF16)
-
-
-def apply_kernel(tile, ids_ref, kept_ref, mine_ref, twin_ref, near_ref, far_ref, out_ref, ordered, halves, own, turned):
+            out_ref[:, here, s * width : (s + 1) * width] = jnp.concatenate(part, axis=1).astype(BF16)
+
+
+def apply_kernel(tile, ids_ref, kept_ref, mine_ref, twin_ref, *refs):
+    folded = refs[: 2 * CHUNKS]
+    out_ref, ordered, halves, own, turned = refs[2 * CHUNKS :]
     core = ids_ref[2]
     planes, tiles, width = mine_ref.shape
     states = tiles * tile // width
@@ -168,36 +187,34 @@
             halves[pl.ds(second, share), :] = value[share:].astype(BF16)
 
     for q in range(states):
-        mid = dot(jnp.concatenate([near_ref[q], far_ref[q]], axis=0), own[...])
+        mid = dot(jnp.concatenate([ref[q] for ref in folded], axis=0), own[...])
         turned[:, q * width : (q + 1) * width] = jnp.swapaxes(mid, 0, 1).astype(BF16)
     out_ref[0, 0] = dot(turned[...], halves[...])
 
 
-def fold(ids, fields, tensor, mask, own, got, half, states):
+def fold(ids, weights, own, got, half, chunk, states):
     others, count, width = got.shape
     slab = own.shape[0]
-    slots, pairs = slab + others, slab * states
+    pairs = slab * states
     step = 48
     steps = count // step
-    fixed = lambda shape: pl.BlockSpec(shape, lambda i, ids: (0,) * len(shape))
     return pl.pallas_call(
         fold_kernel,
         grid_spec=pltpu.PrefetchScalarGridSpec(
             num_scalar_prefetch=1,
             grid=(steps,),
             in_specs=[
-                SMEM,
-                fixed(tensor.shape),
-                fixed(mask.shape),
-                pl.BlockSpec((slab, step, width), lambda i, ids: (0, ((ids[2] + half) % 2) * steps + i, 0)),
+                pl.BlockSpec(weights.shape, lambda i, ids: (0, 0)),
+                pl.BlockSpec(
+                    (slab, step, width), lambda i, ids: (0, ((ids[2] + half) % 2 * CHUNKS + chunk) * steps + i, 0)
+                ),
                 pl.BlockSpec((others, step, width), lambda i, ids: (0, i, 0)),
             ],
             out_specs=pl.BlockSpec((pairs, step, states * width), lambda i, ids: (0, i, 0)),
-            scratch_shapes=[pltpu.VMEM((states * pairs * 8, slots * 16), BF16)],
         ),
         out_shape=jax.ShapeDtypeStruct((pairs, count, states * width), BF16),
-        cost_estimate=pl.CostEstimate(flops=2 * steps * 1024 * 256 * width, bytes_accessed=12 << 20, transcendentals=0),
-    )(ids, fields, tensor, mask, own, got)
+        cost_estimate=pl.CostEstimate(flops=2 * count * 64 * 256 * width, bytes_accessed=6 << 20, transcendentals=0),
+    )(ids, weights, own, got)
 
 
 def call_pack(ids, owner_map, held, capacity, tile, rows):
@@ -214,22 +231,24 @@
     )(ids, owner_map, held)
 
 
-def call_unpack(ids, map_here, arrived, swapped, capacity, pool, cores, rows):
+def call_unpack(ids, map_here, arrived, swapped, capacity, pool, cores, rows, copies):
     tiles = map_here.shape[1]
     width = arrived.size // (tiles * rows)
     return pl.pallas_call(
         functools.partial(unpack_kernel, capacity, pool, cores, rows),
         in_specs=[SMEM] + vmem(3),
         out_specs=pl.BlockSpec(memory_space=pltpu.VMEM),
-        out_shape=jax.ShapeDtypeStruct((tiles, width), BF16),
+        out_shape=jax.ShapeDtypeStruct((copies, tiles, width), BF16),
         cost_estimate=pl.CostEstimate(flops=2 * 384 * 1152 * 384, bytes_accessed=1 << 20, transcendentals=0),
+        compiler_params=pltpu.CompilerParams(vmem_limit_bytes=16 << 20),
         name="unpack",
     )(ids, map_here, arrived, swapped)
 
 
-def call_apply(ids, kept, by_plane, by_twin, near, far, tile):
+def call_apply(ids, kept, by_plane, by_twin, folded, tile):
     planes, tiles, width = by_plane.shape
-    pairs, share, deep = near.shape
+    pairs, part, deep = folded[0].shape
+    share = width // 2
     states = deep // width
     slab = pairs // states
     whole = lambda v, *_: (0, 0, 0)
@@ -239,7 +258,7 @@
             num_scalar_prefetch=2,
             grid=(slab,),
             in_specs=[pl.BlockSpec((planes, tiles, width), whole)] * 2
-            + [pl.BlockSpec((states, share, deep), lambda v, *_: (v, 0, 0))] * 2,
+            + [pl.BlockSpec((states, part, deep), lambda v, *_: (v, 0, 0))] * len(folded),
             out_specs=pl.BlockSpec((1, 1, share, width), lambda v, *_: (v, 0, 0, 0)),
             scratch_shapes=[
                 pltpu.VMEM((tile, tiles, width), BF16),
@@ -251,7 +270,7 @@
         out_shape=jax.ShapeDtypeStruct((slab, 1, share, width), F32),
         cost_estimate=pl.CostEstimate(flops=9 << 29, bytes_accessed=22 << 20, transcendentals=0),
         name="apply",
-    )(ids, kept, by_plane, by_twin, near, far)
+    )(ids, kept, by_plane, by_twin, *folded)
 
 
 def on_device(held, owner_map, kept, left_env, mpo_tensor, mpo_mask, fields):
@@ -274,39 +293,42 @@
     def twin(x):
         return lax.ppermute(x, "col", [(0, 1), (1, 0)])
 
-    def gather(x):
-        return lax.all_to_all(jnp.broadcast_to(x, (planes, *x.shape)), "mpo", 0, 0, tiled=True)
-
     message = rows * capacity * width // 128
     packed = call_pack(ids, owner_map, held.reshape(pool * tile, width), capacity, tile, rows)
     arrived = lax.all_to_all(packed.reshape(env_count, message // 4, 4, 128), "env", 0, 0, tiled=True)
 
     share = width // cores
     env_own = left_env[:, 0]
-    env_half = lax.dynamic_slice_in_dim(env_own, core * share, share, 1)
     step = lambda x, d: lax.ppermute(x, "mpo", [(i, (i + d) % planes) for i in range(planes)])
-    from_left, from_right = step(env_half, 1), step(env_half, -1)
     ring = [(i * cores + c, (i + 1 - 2 * c) % planes * cores + c) for i in range(planes) for c in range(cores)]
-    from_far = lax.ppermute(jnp.where(core == 0, from_left, from_right), ("mpo", "col"), ring)
-    env_got = jnp.concatenate([from_left, from_far, from_right], axis=0)
+    chunk_rows = share // CHUNKS
+    env_got = []
+    for chunk in range(CHUNKS):
+        part = lax.dynamic_slice_in_dim(env_own, core * share + chunk * chunk_rows, chunk_rows, 1)
+        from_left, from_right = step(part, 1), step(part, -1)
+        from_far = lax.ppermute(jnp.where(core == 0, from_left, from_right), ("mpo", "col"), ring)
+        env_got.append(jnp.concatenate([from_left, from_far, from_right], axis=0))
 
     tensor = jnp.pad(
         mpo_tensor.reshape(bond, bond * states * states), ((0, slots - bond), (0, (slots - bond) * states * states))
     )
     mask = jnp.pad(mpo_mask.astype(F32), ((0, slots - bond), (0, slots - bond)))
+    weights = call_weights(ids, fields, tensor, mask, slab, states)
     map_here = lax.dynamic_slice_in_dim(owner_map, env_row, 1, 0)
-    env_got, tensor, mask, map_here = lax.optimization_barrier((env_got, tensor, mask, map_here))
-    env_twin = twin(env_got)
-    folded_mine = fold(ids, fields, tensor, mask, env_own, env_got, 0, states)
-    folded_twin = fold(ids, fields, tensor, mask, env_own, env_twin, 1, states)
+    env_got[0], weights, map_here = lax.optimization_barrier((env_got[0], weights, map_here))
+    folded = [None] * (2 * CHUNKS)
+    for chunk in range(CHUNKS):
+        env_twin = twin(env_got[chunk])
+        for half, got in ((0, env_got[chunk]), (1, env_twin)):
+            folded[half * CHUNKS + chunk] = fold(ids, weights, env_own, got, half, chunk, states)
 
     arrived = arrived.reshape(env_count * message, 128)
     swapped = twin(arrived)
-    mine = call_unpack(ids, map_here, arrived, swapped, capacity, pool, cores, rows)
-    by_plane = gather(mine)
+    mine = call_unpack(ids, map_here, arrived, swapped, capacity, pool, cores, rows, planes)
+    by_plane = lax.all_to_all(mine, "mpo", 0, 0, tiled=True)
     by_twin = twin(by_plane)
 
-    result = call_apply(ids, kept, by_plane, by_twin, folded_mine, folded_twin, tile)
+    result = call_apply(ids, kept, by_plane, by_twin, folded, tile)
     return jnp.swapaxes(result, 2, 3)
 
 

time: 153 us -> 161 us (1.052)
  blocking collectives: 14.9 us -> 0 us
  starting transfers between devices: 62.4 us -> 76.7 us
  Pallas kernels: 36.1 us -> 40.7 us
  waiting for transfers between devices: 30.7 us -> 33 us
    all_to_all x1 -> x0, blocking collectives: 14.9 us -> none  [gather(): lax.all_to_all(jnp.broadcast_to(x, (planes, *x.shape)), 'mpo', 0, 0, tile...]
    all_to_all x1, waiting for transfers between devices: 9.41 us -> 17.8 us  [on_device(): lax.all_to_all(packed.reshape(env_count, message // 4, 4, 128), 'env', 0,...]
    all_to_all x0 -> x1, waiting for transfers between devices: none -> 8.34 us  [on_device(): by_plane = lax.all_to_all(mine, 'mpo', 0, 0, tiled=True)]
    ppermute x2 -> x4, starting transfers between devices: 7.11 us -> 14.2 us  [on_device(): lax.ppermute(x, 'mpo', [(i, (i + d) % planes) for i in range(planes)])]
    ppermute x1 -> x2, waiting for transfers between devices: 6.62 us -> 0.01 us  [on_device(): lax.ppermute(jnp.where(core == 0, from_left, from_right), ('mpo', 'col'),...]
    ppermute x2 -> x4, waiting for transfers between devices: 12.9 us -> 6.84 us  [on_device(): lax.ppermute(x, 'mpo', [(i, (i + d) % planes) for i in range(planes)])]
    all_to_all x0 -> x1, starting transfers between devices: none -> 4.57 us  [on_device(): by_plane = lax.all_to_all(mine, 'mpo', 0, 0, tiled=True)]
    ppermute x3 -> x4, starting transfers between devices: 5.83 us -> 8.27 us  [twin(): return lax.ppermute(x, 'col', [(0, 1), (1, 0)])]
  transfers between devices with their start and end apart: 7 -> 12, of which waited for: 5 -> 4; matrix products, arithmetic and copies ran while one was open for 3% -> 3% of each run, Pallas kernels for 13% -> 15%
where the time goes in v3:
time: 161 us; the launch traced here: 158 us
  starting transfers between devices  76.7 us (48%)
  Pallas kernels  40.7 us (25%)
  waiting for transfers between devices  33 us (20%)
  local copies, waits for them, and re-layouts  5.35 us (3%)
  other arithmetic  1.62 us (1%)
    all_to_all x1, starting transfers between devices, on_device(): lax.all_to_all(packed.reshape(env_count, message // 4, 4, 128), 'env', 0,...  45.8 us
    pallas_call x4, Pallas kernels, fold(): pl.pallas_call(fold_kernel, grid_spec=pltpu.PrefetchScalarGridSpec(num_sc...  19.6 us
    all_to_all x1, waiting for transfers between devices, on_device(): lax.all_to_all(packed.reshape(env_count, message // 4, 4, 128), 'env', 0,...  17.8 us
    ppermute x4, starting transfers between devices, on_device(): lax.ppermute(x, 'mpo', [(i, (i + d) % planes) for i in range(planes)])  14.2 us
    pallas_call x1, Pallas kernels, call_apply(): pl.pallas_call(functools.partial(apply_kernel, tile), grid_spec=pltpu.Pre...  13.2 us
    all_to_all x1, waiting for transfers between devices, on_device(): by_plane = lax.all_to_all(mine, 'mpo', 0, 0, tiled=True)  8.34 us
    ppermute x4, starting transfers between devices, twin(): return lax.ppermute(x, 'col', [(0, 1), (1, 0)])  8.27 us
    ppermute x4, waiting for transfers between devices, on_device(): lax.ppermute(x, 'mpo', [(i, (i + d) % planes) for i in range(planes)])  6.84 us
  transfers between devices with their start and end apart: 12, of which 4 were waited for; matrix products, arithmetic and copies ran while one was open for 3% of the time, Pallas kernels for 15%

profile of v3, /device:TPU:40, one launch (start us, length us, event | category | flops | bytes accessed | tf_op | source)
XLA Modules:
  0.0 158.2 jit_solution(9791193490069538181)
XLA Ops:
  0.6 3.3 %pack.1 = bf16[1152,128]{1,0:T(8,128)(2,1)} custom-call(s32[4]{0:T(128)} %pad_add_fusion.ids_ref, s32[32,192]{1,0:T(8,128)} %map_ref.1, bf16[1536,384]{1,0:T(8,128)(2,1)} %bitcast.21), custom_call_target="tpu_custom_call" | custom-call | flops 536870912 | bytes 2097152 | tf_op jit(solution)/shard_map/pack/pallas_call | solution.py:223
  3.9 45.8 %all-to-all-start = ((bf16[32,9,4,128]{3,2,1,0:T(4,128)(2,1)}), bf16[32,9,4,128]{3,2,1,0:T(4,128)(2,1)S(1)}, u32[]{:S(2)}, u32[]{:S(2)}) async-start(bf16[32,9,4,128]{3,2,1,0:T(4,128)(2,1)} %bitcast.20), calls=%async_computation | async-start | bytes 589824 | tf_op jit(solution)/shard_map/all_to_all | solution.py:298
  50.8 5.1 %collective-permute-start.1 = (bf16[4,96,384]{2,1,0:T(8,128)(2,1)S(1)}, bf16[4,96,384]{2,1,0:T(8,128)(2,1)S(1)}, u32[]{:S(2)}, u32[]{:S(2)}) collective-permute-start(bf16[4,96,384]{2,1,0:T(8,128)(2,1)S(1)} %get-tuple-element.12), channel_id=1, source_target_pairs={{0,6},{2,0},{4,2},{6,4},{1,7},{3,1},{5,3},{7,5},{8,14},{10,8},{12,... | collective-permute-start | bytes 884744 | tf_op jit(solution)/shard_map/ppermute | solution.py:302
  56.0 2.0 %collective-permute-start = (bf16[4,96,384]{2,1,0:T(8,128)(2,1)S(1)}, bf16[4,96,384]{2,1,0:T(8,128)(2,1)S(1)}, u32[]{:S(2)}, u32[]{:S(2)}) collective-permute-start(bf16[4,96,384]{2,1,0:T(8,128)(2,1)S(1)} %get-tuple-element.12), channel_id=1, source_target_pairs={{0,2},{2,4},{4,6},{6,0},{1,3},{3,5},{5,7},{7,1},{8,10},{10,12},{12... | collective-permute-start | bytes 884744 | tf_op jit(solution)/shard_map/ppermute | solution.py:302
  57.9 5.2 %collective-permute-start.6 = (bf16[4,96,384]{2,1,0:T(8,128)(2,1)S(1)}, bf16[4,96,384]{2,1,0:T(8,128)(2,1)S(1)}, u32[]{:S(2)}, u32[]{:S(2)}) collective-permute-start(bf16[4,96,384]{2,1,0:T(8,128)(2,1)S(1)} %get-tuple-element.11), channel_id=1, source_target_pairs={{0,6},{2,0},{4,2},{6,4},{1,7},{3,1},{5,3},{7,5},{8,14},{10,8},{12,... | collective-permute-start | bytes 884744 | tf_op jit(solution)/shard_map/ppermute | solution.py:302
  63.1 2.0 %collective-permute-start.5 = (bf16[4,96,384]{2,1,0:T(8,128)(2,1)S(1)}, bf16[4,96,384]{2,1,0:T(8,128)(2,1)S(1)}, u32[]{:S(2)}, u32[]{:S(2)}) collective-permute-start(bf16[4,96,384]{2,1,0:T(8,128)(2,1)S(1)} %get-tuple-element.11), channel_id=1, source_target_pairs={{0,2},{2,4},{4,6},{6,0},{1,3},{3,5},{5,7},{7,1},{8,10},{10,12},{12... | collective-permute-start | bytes 884744 | tf_op jit(solution)/shard_map/ppermute | solution.py:302
  65.1 2.3 %collective-permute-done = bf16[4,96,384]{2,1,0:T(8,128)(2,1)S(1)} collective-permute-done((bf16[4,96,384]{2,1,0:T(8,128)(2,1)S(1)}, bf16[4,96,384]{2,1,0:T(8,128)(2,1)S(1)}, u32[]{:S(2)}, u32[]{:S(2)}) %collective-permute-start) | collective-permute-done | bytes 294944 | tf_op jit(solution)/shard_map/ppermute | solution.py:302
  67.4 2.0 %collective-permute-start.2 = (bf16[4,96,384]{2,1,0:T(8,128)(2,1)S(1)}, bf16[4,96,384]{2,1,0:T(8,128)(2,1)S(1)}, u32[]{:S(2)}, u32[]{:S(2)}) collective-permute-start(bf16[4,96,384]{2,1,0:T(8,128)(2,1)S(1)} %broadcast_select_fusion.1), channel_id=1, source_target_pairs={{0,2},{1,7},{2,4},{3,1},{4,6},{5,3},{6,0},{7,5},{8,10},{9,15},{10,... | collective-permute-start | bytes 884744 | tf_op jit(solution)/shard_map/ppermute | solution.py:309
  69.3 4.6 %collective-permute-done.5 = bf16[4,96,384]{2,1,0:T(8,128)(2,1)S(1)} collective-permute-done((bf16[4,96,384]{2,1,0:T(8,128)(2,1)S(1)}, bf16[4,96,384]{2,1,0:T(8,128)(2,1)S(1)}, u32[]{:S(2)}, u32[]{:S(2)}) %collective-permute-start.5) | collective-permute-done | bytes 294944 | tf_op jit(solution)/shard_map/ppermute | solution.py:302
  74.7 1.9 %collective-permute-start.7 = (bf16[4,96,384]{2,1,0:T(8,128)(2,1)}, bf16[4,96,384]{2,1,0:T(8,128)(2,1)}, u32[]{:S(2)}, u32[]{:S(2)}) collective-permute-start(bf16[4,96,384]{2,1,0:T(8,128)(2,1)} %get-tuple-element.13), channel_id=1, source_target_pairs={{0,2},{1,7},{2,4},{3,1},{4,6},{5,3},{6,0},{7,5},{8,10},{9,15},{10,... | collective-permute-start | bytes 884744 | tf_op jit(solution)/shard_map/ppermute | solution.py:309
  76.7 17.8 %all-to-all-done = bf16[32,9,4,128]{3,2,1,0:T(4,128)(2,1)S(1)} async-done(((bf16[32,9,4,128]{3,2,1,0:T(4,128)(2,1)}), bf16[32,9,4,128]{3,2,1,0:T(4,128)(2,1)S(1)}, u32[]{:S(2)}, u32[]{:S(2)}) %all-to-all-start) | async-done | bytes 294944 | tf_op jit(solution)/shard_map/all_to_all | solution.py:298
  94.5 1.9 %collective-permute-start.3 = (bf16[1152,128]{1,0:T(8,128)(2,1)S(1)}, bf16[1152,128]{1,0:T(8,128)(2,1)S(1)}, u32[]{:S(2)}, u32[]{:S(2)}) collective-permute-start(bf16[1152,128]{1,0:T(8,128)(2,1)S(1)} %bitcast.13), channel_id=1, source_target_pairs={{0,1},{1,0},{2,3},{3,2},{4,5},{5,4},{6,7},{7,6},{8,9},{9,8},{10,11... | collective-permute-start | bytes 884744 | tf_op jit(solution)/shard_map/ppermute | solution.py:294
  98.7 2.2 %weights.1.weight_ref = bf16[512,256]{1,0:T(8,128)(2,1)} custom-call(s32[4]{0:T(128)} %pad_add_fusion.ids_ref, f32[2]{0:T(128)} %fields_ref.1, f32[16,256]{1,0:T(8,128)} %pad.8.tensor_ref, f32[16,16]{1,0:T(8,128)} %pad.9.mask_ref), custom_call_target="tpu_custom_call" | custom-call | flops 268435456 | bytes 524288 | tf_op jit(solution)/shard_map/weights/pallas_call | solution.py:133
  101.1 2.4 %collective-permute-start.8 = (bf16[12,96,384]{2,1,0:T(8,128)(2,1)S(1)}, bf16[12,96,384]{2,1,0:T(8,128)(2,1)}, u32[]{:S(2)}, u32[]{:S(2)}) collective-permute-start(bf16[12,96,384]{2,1,0:T(8,128)(2,1)S(1)} %pad_maximum_fusion.got_ref), channel_id=1, source_target_pairs={{0,1},{1,0},{2,3},{3,2},{4,5},{5,4},{6,7},{7,6},{8,9},{9,8},{10,11... | collective-permute-start | bytes 2654216 | tf_op jit(solution)/shard_map/ppermute | solution.py:294
  104.5 2.4 %unpack.1 = bf16[4,192,384]{2,1,0:T(8,128)(2,1)} custom-call(s32[4]{0:T(128)S(1)} %copy-done, s32[1,192]{1,0:T(1,128)S(1)} %constant_dynamic-slice_fusion.map_ref, bf16[1152,128]{1,0:T(8,128)(2,1)S(1)} %bitcast.14, bf16[1152,128]{1,0:T(8,128)(2,1)S(1)} %collective-permute-done.3.peer_ref), custom_call_target="tpu_custom_call" | custom-call | flops 339738624 | bytes 1048576 | tf_op jit(solution)/shard_map/unpack/pallas_call | solution.py:237
  107.0 4.6 %all-to-all-start.1 = ((bf16[4,192,384]{2,1,0:T(8,128)(2,1)}), bf16[4,192,384]{2,1,0:T(8,128)(2,1)S(1)}, u32[]{:S(2)}, u32[]{:S(2)}) async-start(bf16[4,192,384]{2,1,0:T(8,128)(2,1)} %unpack.1), calls=%async_computation.1 | async-start | bytes 1179648 | tf_op jit(solution)/shard_map/all_to_all | solution.py:328
  111.6 2.0 %collective-permute-start.9 = (bf16[12,96,384]{2,1,0:T(8,128)(2,1)S(1)}, bf16[12,96,384]{2,1,0:T(8,128)(2,1)S(1)}, u32[]{:S(2)}, u32[]{:S(2)}) collective-permute-start(bf16[12,96,384]{2,1,0:T(8,128)(2,1)S(1)} %constant_dynamic-update-slice_fusion.got_ref), channel_id=1, source_target_pairs={{0,1},{1,0},{2,3},{3,2},{4,5},{5,4},{6,7},{7,6},{8,9},{9,8},{10,11... | collective-permute-start | bytes 2654216 | tf_op jit(solution)/shard_map/ppermute | solution.py:294
  113.5 8.3 %all-to-all-done.1.mine_ref = bf16[4,192,384]{2,1,0:T(8,128)(2,1)S(1)} async-done(((bf16[4,192,384]{2,1,0:T(8,128)(2,1)}), bf16[4,192,384]{2,1,0:T(8,128)(2,1)S(1)}, u32[]{:S(2)}, u32[]{:S(2)}) %all-to-all-start.1) | async-done | bytes 589856 | tf_op jit(solution)/shard_map/all_to_all | solution.py:328
  121.9 1.9 %collective-permute-start.4 = (bf16[4,192,384]{2,1,0:T(8,128)(2,1)S(1)}, bf16[4,192,384]{2,1,0:T(8,128)(2,1)}, u32[]{:S(2)}, u32[]{:S(2)}) collective-permute-start(bf16[4,192,384]{2,1,0:T(8,128)(2,1)S(1)} %all-to-all-done.1.mine_ref), channel_id=1, source_target_pairs={{0,1},{1,0},{2,3},{3,2},{4,5},{5,4},{6,7},{7,6},{8,9},{9,8},{10,11... | collective-permute-start | bytes 1769480 | tf_op jit(solution)/shard_map/ppermute | solution.py:294
  124.5 4.9 %shard_map.74.refs_1_ = bf16[16,96,1536]{2,1,0:T(8,128)(2,1)} custom-call(s32[4]{0:T(128)} %pad_add_fusion.ids_ref, bf16[512,256]{1,0:T(8,128)(2,1)} %weights.1.weight_ref, bf16[4,384,384]{2,1,0:T(8,128)(2,1)} %bitcast.15, bf16[12,96,384]{2,1,0:T(8,128)(2,1)} %copy-done.3), custom_call_target="tpu_custom_call" | custom-call | flops 1207959552 | bytes 6291456 | tf_op jit(solution)/shard_map/pallas_call | solution.py:201
  129.4 4.9 %shard_map.73.refs_0_ = bf16[16,96,1536]{2,1,0:T(8,128)(2,1)} custom-call(s32[4]{0:T(128)} %pad_add_fusion.ids_ref, bf16[512,256]{1,0:T(8,128)(2,1)} %weights.1.weight_ref, bf16[4,384,384]{2,1,0:T(8,128)(2,1)} %bitcast.16, bf16[12,96,384]{2,1,0:T(8,128)(2,1)} %copy-done.1), custom_call_target="tpu_custom_call" | custom-call | flops 1207959552 | bytes 6291456 | tf_op jit(solution)/shard_map/pallas_call | solution.py:201
  134.3 4.9 %shard_map.75.refs_2_ = bf16[16,96,1536]{2,1,0:T(8,128)(2,1)} custom-call(s32[4]{0:T(128)} %pad_add_fusion.ids_ref, bf16[512,256]{1,0:T(8,128)(2,1)} %weights.1.weight_ref, bf16[4,384,384]{2,1,0:T(8,128)(2,1)} %bitcast.17, bf16[12,96,384]{2,1,0:T(8,128)(2,1)} %collective-permute-done.8.got_ref), custom_call_target="tpu_custom_call" | custom-call | flops 1207959552 | bytes 6291456 | tf_op jit(solution)/shard_map/pallas_call | solution.py:201
  140.2 4.9 %shard_map.76.refs_3_ = bf16[16,96,1536]{2,1,0:T(8,128)(2,1)} custom-call(s32[4]{0:T(128)} %pad_add_fusion.ids_ref, bf16[512,256]{1,0:T(8,128)(2,1)} %weights.1.weight_ref, bf16[4,384,384]{2,1,0:T(8,128)(2,1)} %bitcast.18, bf16[12,96,384]{2,1,0:T(8,128)(2,1)} %copy-done.4), custom_call_target="tpu_custom_call" | custom-call | flops 1207959552 | bytes 6291456 | tf_op jit(solution)/shard_map/pallas_call | solution.py:201
  145.0 13.2 %apply.1 = f32[4,1,192,384]{3,2,1,0:T(8,128)} custom-call(s32[4]{0:T(128)} %pad_add_fusion.ids_ref, s32[1]{0:T(128)S(6)} %copy.13.kept_ref, bf16[4,192,384]{2,1,0:T(8,128)(2,1)} %copy-done.2, bf16[4,192,384]{2,1,0:T(8,128)(2,1)} %collective-permute-done.4.twin_ref, bf16[16,96,1536]{2,1,0:T(8,128)(2,1)} %shard_map.73.refs_0_, ...), custom_call_target="tpu_custom_call" | custom-call | flops 4831838208 | bytes 23068672 | tf_op jit(solution)/shard_map/apply/pallas_call | solution.py:255
  (35 shorter events, 7.0 us)
Async XLA Ops:
  0.0 97.2 %copy-start.6 = (s32[14,14]{1,0:T(8,128)S(1)}, s32[14,14]{1,0:T(8,128)}, u32[]{:S(2)}) copy-start(s32[14,14]{1,0:T(8,128)} %param.12) | copy-start | bytes 2356
  0.0 97.2 %copy-start.5 = (f32[14,14,4,4]{1,3,2,0:T(4,128)S(1)}, f32[14,14,4,4]{1,3,2,0:T(4,128)}, u32[]{:S(2)}) copy-start(f32[14,14,4,4]{1,3,2,0:T(4,128)} %param.11) | copy-start | bytes 37636
  0.6 103.9 %copy-start = (s32[4]{0:T(128)S(1)}, s32[4]{0:T(128)}, u32[]{:S(2)}) copy-start(s32[4]{0:T(128)} %pad_add_fusion.ids_ref) | copy-start | bytes 52
  3.9 90.6 %all-to-all-start = ((bf16[32,9,4,128]{3,2,1,0:T(4,128)(2,1)}), bf16[32,9,4,128]{3,2,1,0:T(4,128)(2,1)S(1)}, u32[]{:S(2)}, u32[]{:S(2)}) async-start(bf16[32,9,4,128]{3,2,1,0:T(4,128)(2,1)} %bitcast.20), calls=%async_computation | async-start | bytes 589824 | tf_op jit(solution)/shard_map/all_to_all | solution.py:298
  50.8 14.2 %collective-permute-start.1 = (bf16[4,96,384]{2,1,0:T(8,128)(2,1)S(1)}, bf16[4,96,384]{2,1,0:T(8,128)(2,1)S(1)}, u32[]{:S(2)}, u32[]{:S(2)}) collective-permute-start(bf16[4,96,384]{2,1,0:T(8,128)(2,1)S(1)} %get-tuple-element.12), channel_id=1, source_target_pairs={{0,6},{2,0},{4,2},{6,4},{1,7},{3,1},{5,3},{7,5},{8,14},{10,8},{12,... | collective-permute-start | bytes 884744 | tf_op jit(solution)/shard_map/ppermute | solution.py:302
  56.0 11.4 %collective-permute-start = (bf16[4,96,384]{2,1,0:T(8,128)(2,1)S(1)}, bf16[4,96,384]{2,1,0:T(8,128)(2,1)S(1)}, u32[]{:S(2)}, u32[]{:S(2)}) collective-permute-start(bf16[4,96,384]{2,1,0:T(8,128)(2,1)S(1)} %get-tuple-element.12), channel_id=1, source_target_pairs={{0,2},{2,4},{4,6},{6,0},{1,3},{3,5},{5,7},{7,1},{8,10},{10,12},{12... | collective-permute-start | bytes 884744 | tf_op jit(solution)/shard_map/ppermute | solution.py:302
  57.9 11.4 %collective-permute-start.6 = (bf16[4,96,384]{2,1,0:T(8,128)(2,1)S(1)}, bf16[4,96,384]{2,1,0:T(8,128)(2,1)S(1)}, u32[]{:S(2)}, u32[]{:S(2)}) collective-permute-start(bf16[4,96,384]{2,1,0:T(8,128)(2,1)S(1)} %get-tuple-element.11), channel_id=1, source_target_pairs={{0,6},{2,0},{4,2},{6,4},{1,7},{3,1},{5,3},{7,5},{8,14},{10,8},{12,... | collective-permute-start | bytes 884744 | tf_op jit(solution)/shard_map/ppermute | solution.py:302
  63.1 10.8 %collective-permute-start.5 = (bf16[4,96,384]{2,1,0:T(8,128)(2,1)S(1)}, bf16[4,96,384]{2,1,0:T(8,128)(2,1)S(1)}, u32[]{:S(2)}, u32[]{:S(2)}) collective-permute-start(bf16[4,96,384]{2,1,0:T(8,128)(2,1)S(1)} %get-tuple-element.11), channel_id=1, source_target_pairs={{0,2},{2,4},{4,6},{6,0},{1,3},{3,5},{5,7},{7,1},{8,10},{10,12},{12... | collective-permute-start | bytes 884744 | tf_op jit(solution)/shard_map/ppermute | solution.py:302
  67.4 33.5 %collective-permute-start.2 = (bf16[4,96,384]{2,1,0:T(8,128)(2,1)S(1)}, bf16[4,96,384]{2,1,0:T(8,128)(2,1)S(1)}, u32[]{:S(2)}, u32[]{:S(2)}) collective-permute-start(bf16[4,96,384]{2,1,0:T(8,128)(2,1)S(1)} %broadcast_select_fusion.1), channel_id=1, source_target_pairs={{0,2},{1,7},{2,4},{3,1},{4,6},{5,3},{6,0},{7,5},{8,10},{9,15},{10,... | collective-permute-start | bytes 884744 | tf_op jit(solution)/shard_map/ppermute | solution.py:309
  74.7 28.8 %collective-permute-start.7 = (bf16[4,96,384]{2,1,0:T(8,128)(2,1)}, bf16[4,96,384]{2,1,0:T(8,128)(2,1)}, u32[]{:S(2)}, u32[]{:S(2)}) collective-permute-start(bf16[4,96,384]{2,1,0:T(8,128)(2,1)} %get-tuple-element.13), channel_id=1, source_target_pairs={{0,2},{1,7},{2,4},{3,1},{4,6},{5,3},{6,0},{7,5},{8,10},{9,15},{10,... | collective-permute-start | bytes 884744 | tf_op jit(solution)/shard_map/ppermute | solution.py:309
  94.5 10.0 %collective-permute-start.3 = (bf16[1152,128]{1,0:T(8,128)(2,1)S(1)}, bf16[1152,128]{1,0:T(8,128)(2,1)S(1)}, u32[]{:S(2)}, u32[]{:S(2)}) collective-permute-start(bf16[1152,128]{1,0:T(8,128)(2,1)S(1)} %bitcast.13), channel_id=1, source_target_pairs={{0,1},{1,0},{2,3},{3,2},{4,5},{5,4},{6,7},{7,6},{8,9},{9,8},{10,11... | collective-permute-start | bytes 884744 | tf_op jit(solution)/shard_map/ppermute | solution.py:294
  101.0 28.4 %copy-start.1 = (bf16[12,96,384]{2,1,0:T(8,128)(2,1)}, bf16[12,96,384]{2,1,0:T(8,128)(2,1)S(1)}, u32[]{:S(2)}) copy-start(bf16[12,96,384]{2,1,0:T(8,128)(2,1)S(1)} %pad_maximum_fusion.got_ref) | copy-start | bytes 2654212
  101.1 33.3 %collective-permute-start.8 = (bf16[12,96,384]{2,1,0:T(8,128)(2,1)S(1)}, bf16[12,96,384]{2,1,0:T(8,128)(2,1)}, u32[]{:S(2)}, u32[]{:S(2)}) collective-permute-start(bf16[12,96,384]{2,1,0:T(8,128)(2,1)S(1)} %pad_maximum_fusion.got_ref), channel_id=1, source_target_pairs={{0,1},{1,0},{2,3},{3,2},{4,5},{5,4},{6,7},{7,6},{8,9},{9,8},{10,11... | collective-permute-start | bytes 2654216 | tf_op jit(solution)/shard_map/ppermute | solution.py:294
  107.0 14.9 %all-to-all-start.1 = ((bf16[4,192,384]{2,1,0:T(8,128)(2,1)}), bf16[4,192,384]{2,1,0:T(8,128)(2,1)S(1)}, u32[]{:S(2)}, u32[]{:S(2)}) async-start(bf16[4,192,384]{2,1,0:T(8,128)(2,1)} %unpack.1), calls=%async_computation.1 | async-start | bytes 1179648 | tf_op jit(solution)/shard_map/all_to_all | solution.py:328
  111.6 12.9 %copy-start.3 = (bf16[12,96,384]{2,1,0:T(8,128)(2,1)}, bf16[12,96,384]{2,1,0:T(8,128)(2,1)S(1)}, u32[]{:S(2)}) copy-start(bf16[12,96,384]{2,1,0:T(8,128)(2,1)S(1)} %constant_dynamic-update-slice_fusion.got_ref) | copy-start | bytes 2654212
  111.6 27.7 %collective-permute-start.9 = (bf16[12,96,384]{2,1,0:T(8,128)(2,1)S(1)}, bf16[12,96,384]{2,1,0:T(8,128)(2,1)S(1)}, u32[]{:S(2)}, u32[]{:S(2)}) collective-permute-start(bf16[12,96,384]{2,1,0:T(8,128)(2,1)S(1)} %constant_dynamic-update-slice_fusion.got_ref), channel_id=1, source_target_pairs={{0,1},{1,0},{2,3},{3,2},{4,5},{5,4},{6,7},{7,6},{8,9},{9,8},{10,11... | collective-permute-start | bytes 2654216 | tf_op jit(solution)/shard_map/ppermute | solution.py:294
  121.9 12.4 %copy-start.2 = (bf16[4,192,384]{2,1,0:T(8,128)(2,1)}, bf16[4,192,384]{2,1,0:T(8,128)(2,1)S(1)}, u32[]{:S(2)}) copy-start(bf16[4,192,384]{2,1,0:T(8,128)(2,1)S(1)} %all-to-all-done.1.mine_ref) | copy-start | bytes 1769476
  121.9 23.1 %collective-permute-start.4 = (bf16[4,192,384]{2,1,0:T(8,128)(2,1)S(1)}, bf16[4,192,384]{2,1,0:T(8,128)(2,1)}, u32[]{:S(2)}, u32[]{:S(2)}) collective-permute-start(bf16[4,192,384]{2,1,0:T(8,128)(2,1)S(1)} %all-to-all-done.1.mine_ref), channel_id=1, source_target_pairs={{0,1},{1,0},{2,3},{3,2},{4,5},{5,4},{6,7},{7,6},{8,9},{9,8},{10,11... | collective-permute-start | bytes 1769480 | tf_op jit(solution)/shard_map/ppermute | solution.py:294
  139.2 0.9 copy-start.4

commit v4 on v3

--- a/solution.py
+++ b/solution.py
@@ -13,7 +13,7 @@
 
 
 GROUP = 8
-CHUNKS = 2
+CHUNKS = 1
 
 
 def iota(shape, dim):
@@ -56,42 +56,35 @@
         value = jnp.sum(jnp.where(hit, local, 0).astype(F32), axis=1, keepdims=True)
         slots = slots + jnp.where(lane == s, value, F32(0.0))
     group = capacity * rows
-    message = blocks * group
     total = sectors * group
     inner = iota((total, 1), 0) % group
     sector = iota((total, sectors), 0) // group
     spread = dot(onehot(sector == iota((total, sectors), 1)), slots.astype(BF16))
-    slot = jnp.sum(jnp.where(iota((total, 128), 1) == inner // rows, spread, F32(0.0)), axis=1, keepdims=True)
-    source = slot.astype(jnp.int32) * tile + plane * rows + inner % rows
+    slot = jnp.sum(jnp.where(iota((total, 128), 1) == inner % capacity, spread, F32(0.0)), axis=1, keepdims=True)
+    source = slot.astype(jnp.int32) * tile + plane * rows + inner // capacity
     result = dot(onehot(source == iota((total, count), 1)), held_ref[...])
-    for t in range(sectors):
+    for t in range(sectors * rows):
         for b in range(blocks):
-            at = t * message + b * group
-            spread_ref[at : at + group, :] = result[t * group : (t + 1) * group, b * 128 : (b + 1) * 128]
+            at = (t * blocks + b) * capacity
+            spread_ref[at : at + capacity, :] = result[t * capacity : (t + 1) * capacity, b * 128 : (b + 1) * 128]
     out_ref[...] = spread_ref[...].astype(BF16)
 
 
-def unpack_kernel(capacity, pool, cores, rows, ids_ref, map_ref, own_ref, peer_ref, out_ref):
-    core = ids_ref[2]
+def unpack_kernel(capacity, pool, map_ref, got_ref, out_ref):
     tiles = map_ref.shape[1]
     width = out_ref.shape[2]
     blocks = width // 128
-    group = capacity * rows
-    message = blocks * group
     owner_row = jnp.broadcast_to(map_ref[...], (tiles, tiles)) // pool
     eye = iota((tiles, tiles), 0) == iota((tiles, tiles), 1)
     owner = jnp.sum(jnp.where(eye, owner_row, 0).astype(F32), axis=1, keepdims=True).astype(jnp.int32)
     before = (owner == owner_row) & (iota((tiles, tiles), 1) < iota((tiles, tiles), 0))
     rank = jnp.sum(jnp.where(before, F32(1.0), F32(0.0)), axis=1, keepdims=True).astype(jnp.int32)
-    place = (owner // cores) * message + rank * rows + core
-    own = jnp.where(owner % cores == core, place, -2 * message)
-    peer = jnp.where(owner % cores == core, -2 * message, place)
-    column = iota((tiles, own_ref.shape[0]), 1)
+    place = owner * (blocks * capacity) + rank
+    column = iota((tiles, got_ref.shape[0]), 1)
     for b in range(blocks):
-        value = dot(onehot(column == own + b * group), own_ref[...])
-        value = value + dot(onehot(column == peer + b * group), peer_ref[...])
+        value = dot(onehot(column == place + b * capacity), got_ref[...]).astype(BF16)
         for copy in range(out_ref.shape[0]):
-            out_ref[copy, :, b * 128 : (b + 1) * 128] = value.astype(BF16)
+            out_ref[copy, :, b * 128 : (b + 1) * 128] = value
 
 
 def weight_kernel(slab, states, group, ids_ref, fields_ref, tensor_ref, mask_ref, out_ref):
@@ -160,26 +153,23 @@
             out_ref[:, here, s * width : (s + 1) * width] = jnp.concatenate(part, axis=1).astype(BF16)
 
 
-def apply_kernel(tile, ids_ref, kept_ref, mine_ref, twin_ref, *refs):
+def apply_kernel(tile, ids_ref, kept_ref, rows_ref, *refs):
     folded = refs[: 2 * CHUNKS]
-    out_ref, ordered, halves, own, turned = refs[2 * CHUNKS :]
+    out_ref, halves, own, turned = refs[2 * CHUNKS :]
     core = ids_ref[2]
-    planes, tiles, width = mine_ref.shape
+    _, tiles, width = rows_ref.shape
     states = tiles * tile // width
     per_state = tiles // states
     share = own.shape[1]
 
     @pl.when(pl.program_id(0) == 0)
     def _():
-        keep = iota((tiles, width), 1) < kept_ref[0]
-        for p in range(planes):
-            for other, ref in ((0, mine_ref), (1, twin_ref)):
-                ordered[p * 2 + (core + other) % 2] = jnp.where(keep, ref[p], jnp.zeros((), BF16))
+        keep = iota((width, width), 1) < kept_ref[0]
         n, k = iota((width, width), 0), iota((width, width), 1)
         turn = onehot((n % tile) * per_state + n // tile == k)
         for s in range(states):
-            mixed = ordered[:, s * per_state : (s + 1) * per_state, :].reshape(width, width)
-            value = dot(turn, mixed)
+            mixed = rows_ref[:, s * per_state : (s + 1) * per_state, :].reshape(width, width)
+            value = jnp.where(keep, dot(turn, mixed), F32(0.0))
             own[s * width : (s + 1) * width, :] = jnp.where(core == 0, value[:, :share], value[:, share:]).astype(BF16)
             first = pl.multiple_of(s * width + core * share, share)
             second = pl.multiple_of(s * width + (1 - core) * share, share)
@@ -231,22 +221,22 @@
     )(ids, owner_map, held)
 
 
-def call_unpack(ids, map_here, arrived, swapped, capacity, pool, cores, rows, copies):
+def call_unpack(map_here, arrived, capacity, pool, copies):
     tiles = map_here.shape[1]
-    width = arrived.size // (tiles * rows)
-    return pl.pallas_call(
-        functools.partial(unpack_kernel, capacity, pool, cores, rows),
-        in_specs=[SMEM] + vmem(3),
+    width = arrived.size // tiles // 2
+    return pl.pallas_call(
+        functools.partial(unpack_kernel, capacity, pool),
+        in_specs=vmem(2),
         out_specs=pl.BlockSpec(memory_space=pltpu.VMEM),
         out_shape=jax.ShapeDtypeStruct((copies, tiles, width), BF16),
-        cost_estimate=pl.CostEstimate(flops=2 * 384 * 1152 * 384, bytes_accessed=1 << 20, transcendentals=0),
+        cost_estimate=pl.CostEstimate(flops=1 << 28, bytes_accessed=2 << 20, transcendentals=0),
         compiler_params=pltpu.CompilerParams(vmem_limit_bytes=16 << 20),
         name="unpack",
-    )(ids, map_here, arrived, swapped)
-
-
-def call_apply(ids, kept, by_plane, by_twin, folded, tile):
-    planes, tiles, width = by_plane.shape
+    )(map_here, arrived)
+
+
+def call_apply(ids, kept, rows, folded, tile):
+    _, tiles, width = rows.shape
     pairs, part, deep = folded[0].shape
     share = width // 2
     states = deep // width
@@ -257,11 +247,10 @@
         grid_spec=pltpu.PrefetchScalarGridSpec(
             num_scalar_prefetch=2,
             grid=(slab,),
-            in_specs=[pl.BlockSpec((planes, tiles, width), whole)] * 2
+            in_specs=[pl.BlockSpec((tile, tiles, width), whole)]
             + [pl.BlockSpec((states, part, deep), lambda v, *_: (v, 0, 0))] * len(folded),
             out_specs=pl.BlockSpec((1, 1, share, width), lambda v, *_: (v, 0, 0, 0)),
             scratch_shapes=[
-                pltpu.VMEM((tile, tiles, width), BF16),
                 pltpu.VMEM((deep, width), BF16),
                 pltpu.VMEM((deep, share), BF16),
                 pltpu.VMEM((share, deep), BF16),
@@ -270,7 +259,7 @@
         out_shape=jax.ShapeDtypeStruct((slab, 1, share, width), F32),
         cost_estimate=pl.CostEstimate(flops=9 << 29, bytes_accessed=22 << 20, transcendentals=0),
         name="apply",
-    )(ids, kept, by_plane, by_twin, *folded)
+    )(ids, kept, rows, *folded)
 
 
 def on_device(held, owner_map, kept, left_env, mpo_tensor, mpo_mask, fields):
@@ -293,42 +282,35 @@
     def twin(x):
         return lax.ppermute(x, "col", [(0, 1), (1, 0)])
 
-    message = rows * capacity * width // 128
+    members = env_count * cores
+    message = capacity * width // 128
     packed = call_pack(ids, owner_map, held.reshape(pool * tile, width), capacity, tile, rows)
-    arrived = lax.all_to_all(packed.reshape(env_count, message // 4, 4, 128), "env", 0, 0, tiled=True)
+    arrived = lax.all_to_all(packed.reshape(members, message // 2, 2, 128), ("env", "col"), 0, 0, tiled=True)
 
     share = width // cores
     env_own = left_env[:, 0]
     step = lambda x, d: lax.ppermute(x, "mpo", [(i, (i + d) % planes) for i in range(planes)])
     ring = [(i * cores + c, (i + 1 - 2 * c) % planes * cores + c) for i in range(planes) for c in range(cores)]
-    chunk_rows = share // CHUNKS
-    env_got = []
-    for chunk in range(CHUNKS):
-        part = lax.dynamic_slice_in_dim(env_own, core * share + chunk * chunk_rows, chunk_rows, 1)
-        from_left, from_right = step(part, 1), step(part, -1)
-        from_far = lax.ppermute(jnp.where(core == 0, from_left, from_right), ("mpo", "col"), ring)
-        env_got.append(jnp.concatenate([from_left, from_far, from_right], axis=0))
-
+    part = lax.dynamic_slice_in_dim(env_own, core * share, share, 1)
+    from_left, from_right = step(part, 1), step(part, -1)
     tensor = jnp.pad(
         mpo_tensor.reshape(bond, bond * states * states), ((0, slots - bond), (0, (slots - bond) * states * states))
     )
     mask = jnp.pad(mpo_mask.astype(F32), ((0, slots - bond), (0, slots - bond)))
     weights = call_weights(ids, fields, tensor, mask, slab, states)
     map_here = lax.dynamic_slice_in_dim(owner_map, env_row, 1, 0)
-    env_got[0], weights, map_here = lax.optimization_barrier((env_got[0], weights, map_here))
-    folded = [None] * (2 * CHUNKS)
-    for chunk in range(CHUNKS):
-        env_twin = twin(env_got[chunk])
-        for half, got in ((0, env_got[chunk]), (1, env_twin)):
-            folded[half * CHUNKS + chunk] = fold(ids, weights, env_own, got, half, chunk, states)
-
-    arrived = arrived.reshape(env_count * message, 128)
-    swapped = twin(arrived)
-    mine = call_unpack(ids, map_here, arrived, swapped, capacity, pool, cores, rows, planes)
-    by_plane = lax.all_to_all(mine, "mpo", 0, 0, tiled=True)
-    by_twin = twin(by_plane)
-
-    result = call_apply(ids, kept, by_plane, by_twin, folded, tile)
+    onward = jnp.where(core == 0, from_left, from_right)
+    onward, weights, map_here = lax.optimization_barrier((onward, weights, map_here))
+    from_far = lax.ppermute(onward, ("mpo", "col"), ring)
+    env_got = jnp.concatenate([from_left, from_far, from_right], axis=0)
+    env_twin = twin(env_got)
+    folded = []
+    for half, got in ((0, env_got), (1, env_twin)):
+        folded.append(fold(ids, weights, env_own, got, half, 0, states))
+
+    mine = call_unpack(map_here, arrived.reshape(members * message, 128), capacity, pool, planes * cores)
+    tile_rows = lax.all_to_all(mine, ("mpo", "col"), 0, 0, tiled=True)
+    result = call_apply(ids, kept, tile_rows, folded, tile)
     return jnp.swapaxes(result, 2, 3)
 
 

time: 161 us -> 143 us (0.89)
  starting transfers between devices: 76.7 us -> 63.3 us
  Pallas kernels: 40.7 us -> 35.8 us
  waiting for transfers between devices: 33 us -> 36.2 us
    ppermute x2 -> x1, waiting for transfers between devices: 0.01 us -> 10.6 us  [on_device(): from_far = lax.ppermute(onward, ('mpo', 'col'), ring)]
    ppermute x4 -> x2, starting transfers between devices: 14.2 us -> 7.06 us  [on_device(): lax.ppermute(x, 'mpo', [(i, (i + d) % planes) for i in range(planes)])]
    ppermute x4 -> x2, waiting for transfers between devices: 6.84 us -> 0.01 us  [on_device(): lax.ppermute(x, 'mpo', [(i, (i + d) % planes) for i in range(planes)])]
    ppermute x4 -> x1, starting transfers between devices: 8.27 us -> 1.95 us  [twin(): return lax.ppermute(x, 'col', [(0, 1), (1, 0)])]
    pallas_call x4 -> x2, Pallas kernels: 19.6 us -> 15.7 us  [fold(): pl.pallas_call(fold_kernel, grid_spec=pltpu.PrefetchScalarGridSpec(num_sc...]
    ppermute x2 -> x1, starting transfers between devices: 3.89 us -> 2.41 us  [on_device(): from_far = lax.ppermute(onward, ('mpo', 'col'), ring)]
  transfers between devices with their start and end apart: 12 -> 6, of which waited for: 4 -> 3; matrix products, arithmetic and copies ran while one was open for 3% -> 2% of each run, Pallas kernels for 15% -> 16%
where the time goes in v4:
time: 143 us; the launch traced here: 142 us
  starting transfers between devices  63.3 us (44%)
  waiting for transfers between devices  36.2 us (25%)
  Pallas kernels  35.8 us (25%)
  local copies, waits for them, and re-layouts  4.61 us (3%)
    all_to_all x1, starting transfers between devices, on_device(): lax.all_to_all(packed.reshape(members, message // 2, 2, 128), ('env', 'co...  47.3 us
    all_to_all x1, waiting for transfers between devices, on_device(): lax.all_to_all(packed.reshape(members, message // 2, 2, 128), ('env', 'co...  24.6 us
    pallas_call x2, Pallas kernels, fold(): pl.pallas_call(fold_kernel, grid_spec=pltpu.PrefetchScalarGridSpec(num_sc...  15.7 us
    pallas_call x1, Pallas kernels, call_apply(): pl.pallas_call(functools.partial(apply_kernel, tile), grid_spec=pltpu.Pre...  12.8 us
    ppermute x1, waiting for transfers between devices, on_device(): from_far = lax.ppermute(onward, ('mpo', 'col'), ring)  10.6 us
    ppermute x2, starting transfers between devices, on_device(): lax.ppermute(x, 'mpo', [(i, (i + d) % planes) for i in range(planes)])  7.06 us
    all_to_all x1, starting transfers between devices, on_device(): tile_rows = lax.all_to_all(mine, ('mpo', 'col'), 0, 0, tiled=True)  4.51 us
    pallas_call x1, Pallas kernels, call_pack(): pl.pallas_call(functools.partial(pack_kernel, capacity, tile, rows), in_s...  3.27 us
  transfers between devices with their start and end apart: 6, of which 3 were waited for; matrix products, arithmetic and copies ran while one was open for 2% of the time, Pallas kernels for 16%

profile of v4, /device:TPU:40, one launch (start us, length us, event | category | flops | bytes accessed | tf_op | source)
XLA Modules:
  0.0 141.5 jit_solution(4837996757983193752)
XLA Ops:
  0.0 1.2 dynamic-slice_bitcast_fusion
  1.2 5.1 %collective-permute-start.1 = (bf16[4,192,384]{2,1,0:T(8,128)(2,1)S(1)}, bf16[4,192,384]{2,1,0:T(8,128)(2,1)S(1)}, u32[]{:S(2)}, u32[]{:S(2)}) collective-permute-start(bf16[4,192,384]{2,1,0:T(8,128)(2,1)S(1)} %dynamic-slice_bitcast_fusion), channel_id=1, source_target_pairs={{0,6},{2,0},{4,2},{6,4},{1,7},{3,1},{5,3},{7,5},{8,14},{10,8},{12,... | collective-permute-start | bytes 1769480 | tf_op jit(solution)/shard_map/ppermute | solution.py:292
  6.3 2.0 %collective-permute-start = (bf16[4,192,384]{2,1,0:T(8,128)(2,1)S(1)}, bf16[4,192,384]{2,1,0:T(8,128)(2,1)S(1)}, u32[]{:S(2)}, u32[]{:S(2)}) collective-permute-start(bf16[4,192,384]{2,1,0:T(8,128)(2,1)S(1)} %dynamic-slice_bitcast_fusion), channel_id=1, source_target_pairs={{0,2},{2,4},{4,6},{6,0},{1,3},{3,5},{5,7},{7,1},{8,10},{10,12},{12... | collective-permute-start | bytes 1769480 | tf_op jit(solution)/shard_map/ppermute | solution.py:292
  8.3 0.7 pad_add_fusion.ids_ref
  8.9 3.3 %pack.1 = bf16[1152,128]{1,0:T(8,128)(2,1)} custom-call(s32[4]{0:T(128)} %pad_add_fusion.ids_ref, s32[32,192]{1,0:T(8,128)} %map_ref.1, bf16[1536,384]{1,0:T(8,128)(2,1)} %bitcast.16), custom_call_target="tpu_custom_call" | custom-call | flops 536870912 | bytes 2097152 | tf_op jit(solution)/shard_map/pack/pallas_call | solution.py:213
  12.2 47.3 %all-to-all-start = ((bf16[64,9,2,128]{3,2,1,0:T(2,128)(2,1)}), bf16[64,9,2,128]{3,2,1,0:T(2,128)(2,1)S(1)}, u32[]{:S(2)}, u32[]{:S(2)}) async-start(bf16[64,9,2,128]{3,2,1,0:T(2,128)(2,1)} %bitcast.15), calls=%async_computation | async-start | bytes 589824 | tf_op jit(solution)/shard_map/all_to_all | solution.py:288
  59.5 0.2 copy.9
  59.9 0.6 pad.8.tensor_ref
  60.5 0.6 pad.9.mask_ref
  61.1 2.2 %weights.1.weight_ref = bf16[512,256]{1,0:T(8,128)(2,1)} custom-call(s32[4]{0:T(128)} %pad_add_fusion.ids_ref, f32[2]{0:T(128)} %fields_ref.1, f32[16,256]{1,0:T(8,128)} %pad.8.tensor_ref, f32[16,16]{1,0:T(8,128)} %pad.9.mask_ref), custom_call_target="tpu_custom_call" | custom-call | flops 268435456 | bytes 524288 | tf_op jit(solution)/shard_map/weights/pallas_call | solution.py:126
  63.3 0.7 constant_dynamic-slice_fusion.map_ref
  64.0 0.2 constant_dynamic-update-slice_fusion.2
  64.2 2.4 %collective-permute-start.2 = (bf16[4,192,384]{2,1,0:T(8,128)(2,1)S(1)}, bf16[4,192,384]{2,1,0:T(8,128)(2,1)S(1)}, u32[]{:S(2)}, u32[]{:S(2)}) collective-permute-start(bf16[4,192,384]{2,1,0:T(8,128)(2,1)S(1)} %get-tuple-element.10), channel_id=1, source_target_pairs={{0,2},{1,7},{2,4},{3,1},{4,6},{5,3},{6,0},{7,5},{8,10},{9,15},{10,... | collective-permute-start | bytes 1769480 | tf_op jit(solution)/shard_map/ppermute | solution.py:304
  66.6 10.6 %collective-permute-done.2 = bf16[4,192,384]{2,1,0:T(8,128)(2,1)S(1)} collective-permute-done((bf16[4,192,384]{2,1,0:T(8,128)(2,1)S(1)}, bf16[4,192,384]{2,1,0:T(8,128)(2,1)S(1)}, u32[]{:S(2)}, u32[]{:S(2)}) %collective-permute-start.2) | collective-permute-done | bytes 589856 | tf_op jit(solution)/shard_map/ppermute | solution.py:304
  77.3 0.1 constant_dynamic-update-slice_fusion.got_ref
  77.4 2.0 %collective-permute-start.3 = (bf16[12,192,384]{2,1,0:T(8,128)(2,1)S(1)}, bf16[12,192,384]{2,1,0:T(8,128)(2,1)}, u32[]{:S(2)}, u32[]{:S(2)}) collective-permute-start(bf16[12,192,384]{2,1,0:T(8,128)(2,1)S(1)} %constant_dynamic-update-slice_fusion.got_ref), channel_id=1, source_target_pairs={{0,1},{1,0},{2,3},{3,2},{4,5},{5,4},{6,7},{7,6},{8,9},{9,8},{10,11... | collective-permute-start | bytes 5308424 | tf_op jit(solution)/shard_map/ppermute | solution.py:283
  79.4 24.6 %all-to-all-done = bf16[64,9,2,128]{3,2,1,0:T(2,128)(2,1)S(1)} async-done(((bf16[64,9,2,128]{3,2,1,0:T(2,128)(2,1)}), bf16[64,9,2,128]{3,2,1,0:T(2,128)(2,1)S(1)}, u32[]{:S(2)}, u32[]{:S(2)}) %all-to-all-start) | async-done | bytes 294944 | tf_op jit(solution)/shard_map/all_to_all | solution.py:288
  104.0 1.8 %unpack.1 = bf16[8,192,384]{2,1,0:T(8,128)(2,1)} custom-call(s32[1,192]{1,0:T(1,128)S(1)} %constant_dynamic-slice_fusion.map_ref, bf16[1152,128]{1,0:T(8,128)(2,1)S(1)} %bitcast.11), custom_call_target="tpu_custom_call" | custom-call | flops 268435456 | bytes 2097152 | tf_op jit(solution)/shard_map/unpack/pallas_call | solution.py:227
  105.9 4.5 %all-to-all-start.1 = ((bf16[8,192,384]{2,1,0:T(8,128)(2,1)}), bf16[8,192,384]{2,1,0:T(8,128)(2,1)S(1)}, u32[]{:S(2)}, u32[]{:S(2)}) async-start(bf16[8,192,384]{2,1,0:T(8,128)(2,1)} %unpack.1), calls=%async_computation.1 | async-start | bytes 2359296 | tf_op jit(solution)/shard_map/all_to_all | solution.py:312
  111.0 7.9 %shard_map.73.refs_0_ = bf16[16,192,1536]{2,1,0:T(8,128)(2,1)} custom-call(s32[4]{0:T(128)} %pad_add_fusion.ids_ref, bf16[512,256]{1,0:T(8,128)(2,1)} %weights.1.weight_ref, bf16[4,384,384]{2,1,0:T(8,128)(2,1)} %bitcast.12, bf16[12,192,384]{2,1,0:T(8,128)(2,1)} %copy-done.1), custom_call_target="tpu_custom_call" | custom-call | flops 2415919104 | bytes 6291456 | tf_op jit(solution)/shard_map/pallas_call | solution.py:191
  118.9 7.8 %shard_map.74.refs_1_ = bf16[16,192,1536]{2,1,0:T(8,128)(2,1)} custom-call(s32[4]{0:T(128)} %pad_add_fusion.ids_ref, bf16[512,256]{1,0:T(8,128)(2,1)} %weights.1.weight_ref, bf16[4,384,384]{2,1,0:T(8,128)(2,1)} %bitcast.13, bf16[12,192,384]{2,1,0:T(8,128)(2,1)} %collective-permute-done.3.got_ref), custom_call_target="tpu_custom_call" | custom-call | flops 2415919104 | bytes 6291456 | tf_op jit(solution)/shard_map/pallas_call | solution.py:191
  126.7 1.0 all-to-all-done.1.rows_ref
  127.7 1.0 copy-done
  128.7 12.8 %apply.1 = f32[4,1,192,384]{3,2,1,0:T(8,128)} custom-call(s32[4]{0:T(128)} %pad_add_fusion.ids_ref, s32[1]{0:T(128)S(6)} %copy.13.kept_ref, bf16[8,192,384]{2,1,0:T(8,128)(2,1)} %copy-done, bf16[16,192,1536]{2,1,0:T(8,128)(2,1)} %shard_map.73.refs_0_, bf16[16,192,1536]{2,1,0:T(8,128)(2,1)} %shard_map.74.refs_1_), custom_call_target="tpu_custom_call" | custom-call | flops 4831838208 | bytes 23068672 | tf_op jit(solution)/shard_map/apply/pallas_call | solution.py:245
  (13 shorter events, 0.2 us)
Async XLA Ops:
  0.0 59.5 %copy-start.2 = (f32[14,14,4,4]{1,3,2,0:T(4,128)S(1)}, f32[14,14,4,4]{1,3,2,0:T(4,128)}, u32[]{:S(2)}) copy-start(f32[14,14,4,4]{1,3,2,0:T(4,128)} %param.11) | copy-start | bytes 37636
  1.2 58.7 %copy-start.3 = (s32[14,14]{1,0:T(8,128)S(1)}, s32[14,14]{1,0:T(8,128)}, u32[]{:S(2)}) copy-start(s32[14,14]{1,0:T(8,128)} %param.12) | copy-start | bytes 2356
  1.2 62.8 %collective-permute-start.1 = (bf16[4,192,384]{2,1,0:T(8,128)(2,1)S(1)}, bf16[4,192,384]{2,1,0:T(8,128)(2,1)S(1)}, u32[]{:S(2)}, u32[]{:S(2)}) collective-permute-start(bf16[4,192,384]{2,1,0:T(8,128)(2,1)S(1)} %dynamic-slice_bitcast_fusion), channel_id=1, source_target_pairs={{0,6},{2,0},{4,2},{6,4},{1,7},{3,1},{5,3},{7,5},{8,14},{10,8},{12,... | collective-permute-start | bytes 1769480 | tf_op jit(solution)/shard_map/ppermute | solution.py:292
  6.3 57.7 %collective-permute-start = (bf16[4,192,384]{2,1,0:T(8,128)(2,1)S(1)}, bf16[4,192,384]{2,1,0:T(8,128)(2,1)S(1)}, u32[]{:S(2)}, u32[]{:S(2)}) collective-permute-start(bf16[4,192,384]{2,1,0:T(8,128)(2,1)S(1)} %dynamic-slice_bitcast_fusion), channel_id=1, source_target_pairs={{0,2},{2,4},{4,6},{6,0},{1,3},{3,5},{5,7},{7,1},{8,10},{10,12},{12... | collective-permute-start | bytes 1769480 | tf_op jit(solution)/shard_map/ppermute | solution.py:292
  12.2 91.8 %all-to-all-start = ((bf16[64,9,2,128]{3,2,1,0:T(2,128)(2,1)}), bf16[64,9,2,128]{3,2,1,0:T(2,128)(2,1)S(1)}, u32[]{:S(2)}, u32[]{:S(2)}) async-start(bf16[64,9,2,128]{3,2,1,0:T(2,128)(2,1)} %bitcast.15), calls=%async_computation | async-start | bytes 589824 | tf_op jit(solution)/shard_map/all_to_all | solution.py:288
  64.2 13.0 %collective-permute-start.2 = (bf16[4,192,384]{2,1,0:T(8,128)(2,1)S(1)}, bf16[4,192,384]{2,1,0:T(8,128)(2,1)S(1)}, u32[]{:S(2)}, u32[]{:S(2)}) collective-permute-start(bf16[4,192,384]{2,1,0:T(8,128)(2,1)S(1)} %get-tuple-element.10), channel_id=1, source_target_pairs={{0,2},{1,7},{2,4},{3,1},{4,6},{5,3},{6,0},{7,5},{8,10},{9,15},{10,... | collective-permute-start | bytes 1769480 | tf_op jit(solution)/shard_map/ppermute | solution.py:304
  77.4 28.4 %copy-start.1 = (bf16[12,192,384]{2,1,0:T(8,128)(2,1)}, bf16[12,192,384]{2,1,0:T(8,128)(2,1)S(1)}, u32[]{:S(2)}) copy-start(bf16[12,192,384]{2,1,0:T(8,128)(2,1)S(1)} %constant_dynamic-update-slice_fusion.got_ref) | copy-start | bytes 5308420
  77.4 41.4 %collective-permute-start.3 = (bf16[12,192,384]{2,1,0:T(8,128)(2,1)S(1)}, bf16[12,192,384]{2,1,0:T(8,128)(2,1)}, u32[]{:S(2)}, u32[]{:S(2)}) collective-permute-start(bf16[12,192,384]{2,1,0:T(8,128)(2,1)S(1)} %constant_dynamic-update-slice_fusion.got_ref), channel_id=1, source_target_pairs={{0,1},{1,0},{2,3},{3,2},{4,5},{5,4},{6,7},{7,6},{8,9},{9,8},{10,11... | collective-permute-start | bytes 5308424 | tf_op jit(solution)/shard_map/ppermute | solution.py:283
  105.9 21.9 %all-to-all-start.1 = ((bf16[8,192,384]{2,1,0:T(8,128)(2,1)}), bf16[8,192,384]{2,1,0:T(8,128)(2,1)S(1)}, u32[]{:S(2)}, u32[]{:S(2)}) async-start(bf16[8,192,384]{2,1,0:T(8,128)(2,1)} %unpack.1), calls=%async_computation.1 | async-start | bytes 2359296 | tf_op jit(solution)/shard_map/all_to_all | solution.py:312
  127.7 1.0 copy-start

commit v5 on v4

--- a/solution.py
+++ b/solution.py
@@ -70,7 +70,8 @@
     out_ref[...] = spread_ref[...].astype(BF16)
 
 
-def unpack_kernel(capacity, pool, map_ref, got_ref, out_ref):
+def unpack_kernel(capacity, pool, cores, ids_ref, map_ref, own_ref, peer_ref, out_ref):
+    core = ids_ref[2]
     tiles = map_ref.shape[1]
     width = out_ref.shape[2]
     blocks = width // 128
@@ -79,12 +80,15 @@
     owner = jnp.sum(jnp.where(eye, owner_row, 0).astype(F32), axis=1, keepdims=True).astype(jnp.int32)
     before = (owner == owner_row) & (iota((tiles, tiles), 1) < iota((tiles, tiles), 0))
     rank = jnp.sum(jnp.where(before, F32(1.0), F32(0.0)), axis=1, keepdims=True).astype(jnp.int32)
-    place = owner * (blocks * capacity) + rank
-    column = iota((tiles, got_ref.shape[0]), 1)
+    place = (owner // cores * cores + core) * (blocks * capacity) + rank
+    own = jnp.where(owner % cores == core, place, -own_ref.shape[0])
+    peer = jnp.where(owner % cores == core, -own_ref.shape[0], place)
+    column = iota((tiles, own_ref.shape[0]), 1)
     for b in range(blocks):
-        value = dot(onehot(column == place + b * capacity), got_ref[...]).astype(BF16)
+        value = dot(onehot(column == own + b * capacity), own_ref[...])
+        value = value + dot(onehot(column == peer + b * capacity), peer_ref[...])
         for copy in range(out_ref.shape[0]):
-            out_ref[copy, :, b * 128 : (b + 1) * 128] = value
+            out_ref[copy, :, b * 128 : (b + 1) * 128] = value.astype(BF16)
 
 
 def weight_kernel(slab, states, group, ids_ref, fields_ref, tensor_ref, mask_ref, out_ref):
@@ -221,18 +225,18 @@
     )(ids, owner_map, held)
 
 
-def call_unpack(map_here, arrived, capacity, pool, copies):
+def call_unpack(ids, map_here, arrived, swapped, capacity, pool, cores, copies):
     tiles = map_here.shape[1]
     width = arrived.size // tiles // 2
     return pl.pallas_call(
-        functools.partial(unpack_kernel, capacity, pool),
-        in_specs=vmem(2),
+        functools.partial(unpack_kernel, capacity, pool, cores),
+        in_specs=[SMEM] + vmem(3),
         out_specs=pl.BlockSpec(memory_space=pltpu.VMEM),
         out_shape=jax.ShapeDtypeStruct((copies, tiles, width), BF16),
         cost_estimate=pl.CostEstimate(flops=1 << 28, bytes_accessed=2 << 20, transcendentals=0),
         compiler_params=pltpu.CompilerParams(vmem_limit_bytes=16 << 20),
         name="unpack",
-    )(map_here, arrived)
+    )(ids, map_here, arrived, swapped)
 
 
 def call_apply(ids, kept, rows, folded, tile):
@@ -282,10 +286,9 @@
     def twin(x):
         return lax.ppermute(x, "col", [(0, 1), (1, 0)])
 
-    members = env_count * cores
-    message = capacity * width // 128
+    message = rows * capacity * width // 128
     packed = call_pack(ids, owner_map, held.reshape(pool * tile, width), capacity, tile, rows)
-    arrived = lax.all_to_all(packed.reshape(members, message // 2, 2, 128), ("env", "col"), 0, 0, tiled=True)
+    arrived = lax.all_to_all(packed.reshape(env_count, message // 4, 4, 128), "env", 0, 0, tiled=True)
 
     share = width // cores
     env_own = left_env[:, 0]
@@ -308,7 +311,9 @@
     for half, got in ((0, env_got), (1, env_twin)):
         folded.append(fold(ids, weights, env_own, got, half, 0, states))
 
-    mine = call_unpack(map_here, arrived.reshape(members * message, 128), capacity, pool, planes * cores)
+    arrived = arrived.reshape(env_count * message, 128)
+    swapped = twin(arrived)
+    mine = call_unpack(ids, map_here, arrived, swapped, capacity, pool, cores, planes * cores)
     tile_rows = lax.all_to_all(mine, ("mpo", "col"), 0, 0, tiled=True)
     result = call_apply(ids, kept, tile_rows, folded, tile)
     return jnp.swapaxes(result, 2, 3)

time: 143 us -> 145 us (1.014)
  waiting for transfers between devices: 36.2 us -> 37.7 us
    ppermute x1 -> x2, starting transfers between devices: 1.95 us -> 3.89 us  [twin(): return lax.ppermute(x, 'col', [(0, 1), (1, 0)])]
    all_to_all x1, starting transfers between devices: 47.3 us -> 45.8 us  [on_device(): lax.all_to_all(packed.reshape(env_count, message // 4, 4, 128), 'env', 0,...]
    ppermute x1 -> x2, waiting for transfers between devices: 0.01 us -> 1.55 us  [twin(): return lax.ppermute(x, 'col', [(0, 1), (1, 0)])]
  transfers between devices with their start and end apart: 6 -> 7, of which waited for: 3 -> 4; matrix products, arithmetic and copies ran while one was open for 2% -> 2% of each run, Pallas kernels for 16% -> 17%
where the time goes in v5:
time: 145 us; the launch traced here: 144 us
  starting transfers between devices  63.3 us (44%)
  waiting for transfers between devices  37.7 us (26%)
  Pallas kernels  36.7 us (25%)
  local copies, waits for them, and re-layouts  4.63 us (3%)
    all_to_all x1, starting transfers between devices, on_device(): lax.all_to_all(packed.reshape(env_count, message // 4, 4, 128), 'env', 0,...  45.8 us
    all_to_all x1, waiting for transfers between devices, on_device(): lax.all_to_all(packed.reshape(env_count, message // 4, 4, 128), 'env', 0,...  24.6 us
    pallas_call x2, Pallas kernels, fold(): pl.pallas_call(fold_kernel, grid_spec=pltpu.PrefetchScalarGridSpec(num_sc...  15.7 us
    pallas_call x1, Pallas kernels, call_apply(): pl.pallas_call(functools.partial(apply_kernel, tile), grid_spec=pltpu.Pre...  12.8 us
    ppermute x1, waiting for transfers between devices, on_device(): from_far = lax.ppermute(onward, ('mpo', 'col'), ring)  10.6 us
    ppermute x2, starting transfers between devices, on_device(): lax.ppermute(x, 'mpo', [(i, (i + d) % planes) for i in range(planes)])  7.06 us
    all_to_all x1, starting transfers between devices, on_device(): tile_rows = lax.all_to_all(mine, ('mpo', 'col'), 0, 0, tiled=True)  4.2 us
    ppermute x2, starting transfers between devices, twin(): return lax.ppermute(x, 'col', [(0, 1), (1, 0)])  3.89 us
  transfers between devices with their start and end apart: 7, of which 4 were waited for; matrix products, arithmetic and copies ran while one was open for 2% of the time, Pallas kernels for 17%

profile of v5, /device:TPU:40, one launch (start us, length us, event | category | flops | bytes accessed | tf_op | source)
XLA Modules:
  0.0 144.0 jit_solution(8854823515545091347)
XLA Ops:
  0.0 1.2 dynamic-slice_bitcast_fusion
  1.2 5.1 %collective-permute-start.1 = (bf16[4,192,384]{2,1,0:T(8,128)(2,1)S(1)}, bf16[4,192,384]{2,1,0:T(8,128)(2,1)S(1)}, u32[]{:S(2)}, u32[]{:S(2)}) collective-permute-start(bf16[4,192,384]{2,1,0:T(8,128)(2,1)S(1)} %dynamic-slice_bitcast_fusion), channel_id=1, source_target_pairs={{0,6},{2,0},{4,2},{6,4},{1,7},{3,1},{5,3},{7,5},{8,14},{10,8},{12,... | collective-permute-start | bytes 1769480 | tf_op jit(solution)/shard_map/ppermute | solution.py:295
  6.3 2.0 %collective-permute-start = (bf16[4,192,384]{2,1,0:T(8,128)(2,1)S(1)}, bf16[4,192,384]{2,1,0:T(8,128)(2,1)S(1)}, u32[]{:S(2)}, u32[]{:S(2)}) collective-permute-start(bf16[4,192,384]{2,1,0:T(8,128)(2,1)S(1)} %dynamic-slice_bitcast_fusion), channel_id=1, source_target_pairs={{0,2},{2,4},{4,6},{6,0},{1,3},{3,5},{5,7},{7,1},{8,10},{10,12},{12... | collective-permute-start | bytes 1769480 | tf_op jit(solution)/shard_map/ppermute | solution.py:295
  8.3 0.6 pad_add_fusion.ids_ref
  8.8 3.3 %pack.1 = bf16[1152,128]{1,0:T(8,128)(2,1)} custom-call(s32[4]{0:T(128)} %pad_add_fusion.ids_ref, s32[32,192]{1,0:T(8,128)} %map_ref.1, bf16[1536,384]{1,0:T(8,128)(2,1)} %bitcast.17), custom_call_target="tpu_custom_call" | custom-call | flops 536870912 | bytes 2097152 | tf_op jit(solution)/shard_map/pack/pallas_call | solution.py:217
  12.1 45.8 %all-to-all-start = ((bf16[32,9,4,128]{3,2,1,0:T(4,128)(2,1)}), bf16[32,9,4,128]{3,2,1,0:T(4,128)(2,1)S(1)}, u32[]{:S(2)}, u32[]{:S(2)}) async-start(bf16[32,9,4,128]{3,2,1,0:T(4,128)(2,1)} %bitcast.16), calls=%async_computation | async-start | bytes 589824 | tf_op jit(solution)/shard_map/all_to_all | solution.py:291
  57.9 0.2 copy.9
  58.2 0.6 pad.8.tensor_ref
  58.8 0.6 pad.9.mask_ref
  59.4 2.2 %weights.1.weight_ref = bf16[512,256]{1,0:T(8,128)(2,1)} custom-call(s32[4]{0:T(128)} %pad_add_fusion.ids_ref, f32[2]{0:T(128)} %fields_ref.1, f32[16,256]{1,0:T(8,128)} %pad.8.tensor_ref, f32[16,16]{1,0:T(8,128)} %pad.9.mask_ref), custom_call_target="tpu_custom_call" | custom-call | flops 268435456 | bytes 524288 | tf_op jit(solution)/shard_map/weights/pallas_call | solution.py:130
  61.6 0.7 constant_dynamic-slice_fusion.map_ref
  62.6 2.4 %collective-permute-start.3 = (bf16[4,192,384]{2,1,0:T(8,128)(2,1)S(1)}, bf16[4,192,384]{2,1,0:T(8,128)(2,1)S(1)}, u32[]{:S(2)}, u32[]{:S(2)}) collective-permute-start(bf16[4,192,384]{2,1,0:T(8,128)(2,1)S(1)} %get-tuple-element.10), channel_id=1, source_target_pairs={{0,2},{1,7},{2,4},{3,1},{4,6},{5,3},{6,0},{7,5},{8,10},{9,15},{10,... | collective-permute-start | bytes 1769480 | tf_op jit(solution)/shard_map/ppermute | solution.py:307
  65.0 10.6 %collective-permute-done.3 = bf16[4,192,384]{2,1,0:T(8,128)(2,1)S(1)} collective-permute-done((bf16[4,192,384]{2,1,0:T(8,128)(2,1)S(1)}, bf16[4,192,384]{2,1,0:T(8,128)(2,1)S(1)}, u32[]{:S(2)}, u32[]{:S(2)}) %collective-permute-start.3) | collective-permute-done | bytes 589856 | tf_op jit(solution)/shard_map/ppermute | solution.py:307
  75.8 2.0 %collective-permute-start.4 = (bf16[12,192,384]{2,1,0:T(8,128)(2,1)S(1)}, bf16[12,192,384]{2,1,0:T(8,128)(2,1)}, u32[]{:S(2)}, u32[]{:S(2)}) collective-permute-start(bf16[12,192,384]{2,1,0:T(8,128)(2,1)S(1)} %constant_dynamic-update-slice_fusion.got_ref), channel_id=1, source_target_pairs={{0,1},{1,0},{2,3},{3,2},{4,5},{5,4},{6,7},{7,6},{8,9},{9,8},{10,11... | collective-permute-start | bytes 5308424 | tf_op jit(solution)/shard_map/ppermute | solution.py:287
  77.8 24.6 %all-to-all-done = bf16[32,9,4,128]{3,2,1,0:T(4,128)(2,1)S(1)} async-done(((bf16[32,9,4,128]{3,2,1,0:T(4,128)(2,1)}), bf16[32,9,4,128]{3,2,1,0:T(4,128)(2,1)S(1)}, u32[]{:S(2)}, u32[]{:S(2)}) %all-to-all-start) | async-done | bytes 294944 | tf_op jit(solution)/shard_map/all_to_all | solution.py:291
  102.4 1.9 %collective-permute-start.2 = (bf16[1152,128]{1,0:T(8,128)(2,1)S(1)}, bf16[1152,128]{1,0:T(8,128)(2,1)S(1)}, u32[]{:S(2)}, u32[]{:S(2)}) collective-permute-start(bf16[1152,128]{1,0:T(8,128)(2,1)S(1)} %bitcast.11), channel_id=1, source_target_pairs={{0,1},{1,0},{2,3},{3,2},{4,5},{5,4},{6,7},{7,6},{8,9},{9,8},{10,11... | collective-permute-start | bytes 884744 | tf_op jit(solution)/shard_map/ppermute | solution.py:287
  104.3 1.5 %collective-permute-done.2.peer_ref = bf16[1152,128]{1,0:T(8,128)(2,1)S(1)} collective-permute-done((bf16[1152,128]{1,0:T(8,128)(2,1)S(1)}, bf16[1152,128]{1,0:T(8,128)(2,1)S(1)}, u32[]{:S(2)}, u32[]{:S(2)}) %collective-permute-start.2) | collective-permute-done | bytes 294944 | tf_op jit(solution)/shard_map/ppermute | solution.py:287
  105.9 2.7 %unpack.1 = bf16[8,192,384]{2,1,0:T(8,128)(2,1)} custom-call(s32[4]{0:T(128)S(1)} %copy-done, s32[1,192]{1,0:T(1,128)S(1)} %constant_dynamic-slice_fusion.map_ref, bf16[1152,128]{1,0:T(8,128)(2,1)S(1)} %bitcast.12, bf16[1152,128]{1,0:T(8,128)(2,1)S(1)} %collective-permute-done.2.peer_ref), custom_call_target="tpu_custom_call" | custom-call | flops 268435456 | bytes 2097152 | tf_op jit(solution)/shard_map/unpack/pallas_call | solution.py:231
  108.6 4.2 %all-to-all-start.1 = ((bf16[8,192,384]{2,1,0:T(8,128)(2,1)}), bf16[8,192,384]{2,1,0:T(8,128)(2,1)S(1)}, u32[]{:S(2)}, u32[]{:S(2)}) async-start(bf16[8,192,384]{2,1,0:T(8,128)(2,1)} %unpack.1), calls=%async_computation.1 | async-start | bytes 2359296 | tf_op jit(solution)/shard_map/all_to_all | solution.py:317
  113.4 7.9 %shard_map.73.refs_0_ = bf16[16,192,1536]{2,1,0:T(8,128)(2,1)} custom-call(s32[4]{0:T(128)} %pad_add_fusion.ids_ref, bf16[512,256]{1,0:T(8,128)(2,1)} %weights.1.weight_ref, bf16[4,384,384]{2,1,0:T(8,128)(2,1)} %bitcast.13, bf16[12,192,384]{2,1,0:T(8,128)(2,1)} %copy-done.2), custom_call_target="tpu_custom_call" | custom-call | flops 2415919104 | bytes 6291456 | tf_op jit(solution)/shard_map/pallas_call | solution.py:195
  121.3 7.8 %shard_map.74.refs_1_ = bf16[16,192,1536]{2,1,0:T(8,128)(2,1)} custom-call(s32[4]{0:T(128)} %pad_add_fusion.ids_ref, bf16[512,256]{1,0:T(8,128)(2,1)} %weights.1.weight_ref, bf16[4,384,384]{2,1,0:T(8,128)(2,1)} %bitcast.14, bf16[12,192,384]{2,1,0:T(8,128)(2,1)} %collective-permute-done.4.got_ref), custom_call_target="tpu_custom_call" | custom-call | flops 2415919104 | bytes 6291456 | tf_op jit(solution)/shard_map/pallas_call | solution.py:195
  129.1 1.0 all-to-all-done.1.rows_ref
  130.1 1.0 copy-done.1
  131.2 12.8 %apply.1 = f32[4,1,192,384]{3,2,1,0:T(8,128)} custom-call(s32[4]{0:T(128)} %pad_add_fusion.ids_ref, s32[1]{0:T(128)S(6)} %copy.13.kept_ref, bf16[8,192,384]{2,1,0:T(8,128)(2,1)} %copy-done.1, bf16[16,192,1536]{2,1,0:T(8,128)(2,1)} %shard_map.73.refs_0_, bf16[16,192,1536]{2,1,0:T(8,128)(2,1)} %shard_map.74.refs_1_), custom_call_target="tpu_custom_call" | custom-call | flops 4831838208 | bytes 23068672 | tf_op jit(solution)/shard_map/apply/pallas_call | solution.py:249
  (17 shorter events, 0.5 us)
Async XLA Ops:
  0.0 57.9 %copy-start.3 = (f32[14,14,4,4]{1,3,2,0:T(4,128)S(1)}, f32[14,14,4,4]{1,3,2,0:T(4,128)}, u32[]{:S(2)}) copy-start(f32[14,14,4,4]{1,3,2,0:T(4,128)} %param.11) | copy-start | bytes 37636
  1.2 57.0 %copy-start.4 = (s32[14,14]{1,0:T(8,128)S(1)}, s32[14,14]{1,0:T(8,128)}, u32[]{:S(2)}) copy-start(s32[14,14]{1,0:T(8,128)} %param.12) | copy-start | bytes 2356
  1.2 61.1 %collective-permute-start.1 = (bf16[4,192,384]{2,1,0:T(8,128)(2,1)S(1)}, bf16[4,192,384]{2,1,0:T(8,128)(2,1)S(1)}, u32[]{:S(2)}, u32[]{:S(2)}) collective-permute-start(bf16[4,192,384]{2,1,0:T(8,128)(2,1)S(1)} %dynamic-slice_bitcast_fusion), channel_id=1, source_target_pairs={{0,6},{2,0},{4,2},{6,4},{1,7},{3,1},{5,3},{7,5},{8,14},{10,8},{12,... | collective-permute-start | bytes 1769480 | tf_op jit(solution)/shard_map/ppermute | solution.py:295
  6.3 56.0 %collective-permute-start = (bf16[4,192,384]{2,1,0:T(8,128)(2,1)S(1)}, bf16[4,192,384]{2,1,0:T(8,128)(2,1)S(1)}, u32[]{:S(2)}, u32[]{:S(2)}) collective-permute-start(bf16[4,192,384]{2,1,0:T(8,128)(2,1)S(1)} %dynamic-slice_bitcast_fusion), channel_id=1, source_target_pairs={{0,2},{2,4},{4,6},{6,0},{1,3},{3,5},{5,7},{7,1},{8,10},{10,12},{12... | collective-permute-start | bytes 1769480 | tf_op jit(solution)/shard_map/ppermute | solution.py:295
  12.1 90.3 %all-to-all-start = ((bf16[32,9,4,128]{3,2,1,0:T(4,128)(2,1)}), bf16[32,9,4,128]{3,2,1,0:T(4,128)(2,1)S(1)}, u32[]{:S(2)}, u32[]{:S(2)}) async-start(bf16[32,9,4,128]{3,2,1,0:T(4,128)(2,1)} %bitcast.16), calls=%async_computation | async-start | bytes 589824 | tf_op jit(solution)/shard_map/all_to_all | solution.py:291
  62.6 43.3 %copy-start = (s32[4]{0:T(128)S(1)}, s32[4]{0:T(128)}, u32[]{:S(2)}) copy-start(s32[4]{0:T(128)} %pad_add_fusion.ids_ref) | copy-start | bytes 52
  62.6 13.0 %collective-permute-start.3 = (bf16[4,192,384]{2,1,0:T(8,128)(2,1)S(1)}, bf16[4,192,384]{2,1,0:T(8,128)(2,1)S(1)}, u32[]{:S(2)}, u32[]{:S(2)}) collective-permute-start(bf16[4,192,384]{2,1,0:T(8,128)(2,1)S(1)} %get-tuple-element.10), channel_id=1, source_target_pairs={{0,2},{1,7},{2,4},{3,1},{4,6},{5,3},{6,0},{7,5},{8,10},{9,15},{10,... | collective-permute-start | bytes 1769480 | tf_op jit(solution)/shard_map/ppermute | solution.py:307
  75.8 32.8 %copy-start.2 = (bf16[12,192,384]{2,1,0:T(8,128)(2,1)}, bf16[12,192,384]{2,1,0:T(8,128)(2,1)S(1)}, u32[]{:S(2)}) copy-start(bf16[12,192,384]{2,1,0:T(8,128)(2,1)S(1)} %constant_dynamic-update-slice_fusion.got_ref) | copy-start | bytes 5308420
  75.8 45.5 %collective-permute-start.4 = (bf16[12,192,384]{2,1,0:T(8,128)(2,1)S(1)}, bf16[12,192,384]{2,1,0:T(8,128)(2,1)}, u32[]{:S(2)}, u32[]{:S(2)}) collective-permute-start(bf16[12,192,384]{2,1,0:T(8,128)(2,1)S(1)} %constant_dynamic-update-slice_fusion.got_ref), channel_id=1, source_target_pairs={{0,1},{1,0},{2,3},{3,2},{4,5},{5,4},{6,7},{7,6},{8,9},{9,8},{10,11... | collective-permute-start | bytes 5308424 | tf_op jit(solution)/shard_map/ppermute | solution.py:287
  102.4 3.5 %collective-permute-start.2 = (bf16[1152,128]{1,0:T(8,128)(2,1)S(1)}, bf16[1152,128]{1,0:T(8,128)(2,1)S(1)}, u32[]{:S(2)}, u32[]{:S(2)}) collective-permute-start(bf16[1152,128]{1,0:T(8,128)(2,1)S(1)} %bitcast.11), channel_id=1, source_target_pairs={{0,1},{1,0},{2,3},{3,2},{4,5},{5,4},{6,7},{7,6},{8,9},{9,8},{10,11... | collective-permute-start | bytes 884744 | tf_op jit(solution)/shard_map/ppermute | solution.py:287
  108.6 21.5 %all-to-all-start.1 = ((bf16[8,192,384]{2,1,0:T(8,128)(2,1)}), bf16[8,192,384]{2,1,0:T(8,128)(2,1)S(1)}, u32[]{:S(2)}, u32[]{:S(2)}) async-start(bf16[8,192,384]{2,1,0:T(8,128)(2,1)} %unpack.1), calls=%async_computation.1 | async-start | bytes 2359296 | tf_op jit(solution)/shard_map/all_to_all | solution.py:317
  130.1 1.0 copy-start.1

commit v6 on v5

--- a/solution.py
+++ b/solution.py
@@ -137,6 +137,30 @@
     )(ids, fields, tensor, mask)
 
 
+def turn_kernel(tile, ids_ref, env_ref, out_ref):
+    core = ids_ref[2]
+    slab, share, width = out_ref.shape
+    runs = width // tile
+    row = iota((share, width), 0) + core * share
+    rows = onehot(row % runs * tile + row // runs == iota((share, width), 1))
+    column = iota((width, width), 1)
+    columns = onehot(column % runs * tile + column // runs == iota((width, width), 0))
+    for w in range(slab):
+        out_ref[w] = dot(dot(rows, env_ref[w]).astype(BF16), columns).astype(BF16)
+
+
+def call_turn(ids, env, tile):
+    slab, width, _ = env.shape
+    return pl.pallas_call(
+        functools.partial(turn_kernel, tile),
+        in_specs=[SMEM] + vmem(1),
+        out_specs=pl.BlockSpec(memory_space=pltpu.VMEM),
+        out_shape=jax.ShapeDtypeStruct((slab, width // 2, width), BF16),
+        cost_estimate=pl.CostEstimate(flops=1 << 28, bytes_accessed=2 << 20, transcendentals=0),
+        name="turn",
+    )(ids, env)
+
+
 def fold_kernel(ids_ref, weight_ref, own_ref, got_ref, out_ref):
     slab, step_rows, width = own_ref.shape
     slots = slab + got_ref.shape[0]
@@ -157,23 +181,23 @@
             out_ref[:, here, s * width : (s + 1) * width] = jnp.concatenate(part, axis=1).astype(BF16)
 
 
-def apply_kernel(tile, ids_ref, kept_ref, rows_ref, *refs):
+def apply_kernel(tile, ids_ref, kept_ref, mine_ref, twin_ref, *refs):
     folded = refs[: 2 * CHUNKS]
-    out_ref, halves, own, turned = refs[2 * CHUNKS :]
+    out_ref, ordered, halves, own, turned = refs[2 * CHUNKS :]
     core = ids_ref[2]
-    _, tiles, width = rows_ref.shape
+    planes, tiles, width = mine_ref.shape
     states = tiles * tile // width
     per_state = tiles // states
     share = own.shape[1]
 
     @pl.when(pl.program_id(0) == 0)
     def _():
-        keep = iota((width, width), 1) < kept_ref[0]
-        n, k = iota((width, width), 0), iota((width, width), 1)
-        turn = onehot((n % tile) * per_state + n // tile == k)
+        keep = iota((tiles, width), 1) < kept_ref[0]
+        for p in range(planes):
+            for other, ref in ((0, mine_ref), (1, twin_ref)):
+                ordered[p * 2 + (core + other) % 2] = jnp.where(keep, ref[p], jnp.zeros((), BF16))
         for s in range(states):
-            mixed = rows_ref[:, s * per_state : (s + 1) * per_state, :].reshape(width, width)
-            value = jnp.where(keep, dot(turn, mixed), F32(0.0))
+            value = ordered[:, s * per_state : (s + 1) * per_state, :].reshape(width, width).astype(F32)
             own[s * width : (s + 1) * width, :] = jnp.where(core == 0, value[:, :share], value[:, share:]).astype(BF16)
             first = pl.multiple_of(s * width + core * share, share)
             second = pl.multiple_of(s * width + (1 - core) * share, share)
@@ -186,7 +210,7 @@
     out_ref[0, 0] = dot(turned[...], halves[...])
 
 
-def fold(ids, weights, own, got, half, chunk, states):
+def fold(ids, weights, own, got, states):
     others, count, width = got.shape
     slab = own.shape[0]
     pairs = slab * states
@@ -199,9 +223,7 @@
             grid=(steps,),
             in_specs=[
                 pl.BlockSpec(weights.shape, lambda i, ids: (0, 0)),
-                pl.BlockSpec(
-                    (slab, step, width), lambda i, ids: (0, ((ids[2] + half) % 2 * CHUNKS + chunk) * steps + i, 0)
-                ),
+                pl.BlockSpec((slab, step, width), lambda i, ids: (0, i, 0)),
                 pl.BlockSpec((others, step, width), lambda i, ids: (0, i, 0)),
             ],
             out_specs=pl.BlockSpec((pairs, step, states * width), lambda i, ids: (0, i, 0)),
@@ -239,8 +261,8 @@
     )(ids, map_here, arrived, swapped)
 
 
-def call_apply(ids, kept, rows, folded, tile):
-    _, tiles, width = rows.shape
+def call_apply(ids, kept, by_plane, by_twin, folded, tile):
+    planes, tiles, width = by_plane.shape
     pairs, part, deep = folded[0].shape
     share = width // 2
     states = deep // width
@@ -251,10 +273,11 @@
         grid_spec=pltpu.PrefetchScalarGridSpec(
             num_scalar_prefetch=2,
             grid=(slab,),
-            in_specs=[pl.BlockSpec((tile, tiles, width), whole)]
+            in_specs=[pl.BlockSpec((planes, tiles, width), whole)] * 2
             + [pl.BlockSpec((states, part, deep), lambda v, *_: (v, 0, 0))] * len(folded),
             out_specs=pl.BlockSpec((1, 1, share, width), lambda v, *_: (v, 0, 0, 0)),
             scratch_shapes=[
+                pltpu.VMEM((tile, tiles, width), BF16),
                 pltpu.VMEM((deep, width), BF16),
                 pltpu.VMEM((deep, share), BF16),
                 pltpu.VMEM((share, deep), BF16),
@@ -263,7 +286,7 @@
         out_shape=jax.ShapeDtypeStruct((slab, 1, share, width), F32),
         cost_estimate=pl.CostEstimate(flops=9 << 29, bytes_accessed=22 << 20, transcendentals=0),
         name="apply",
-    )(ids, kept, rows, *folded)
+    )(ids, kept, by_plane, by_twin, *folded)
 
 
 def on_device(held, owner_map, kept, left_env, mpo_tensor, mpo_mask, fields):
@@ -290,11 +313,10 @@
     packed = call_pack(ids, owner_map, held.reshape(pool * tile, width), capacity, tile, rows)
     arrived = lax.all_to_all(packed.reshape(env_count, message // 4, 4, 128), "env", 0, 0, tiled=True)
 
-    share = width // cores
     env_own = left_env[:, 0]
     step = lambda x, d: lax.ppermute(x, "mpo", [(i, (i + d) % planes) for i in range(planes)])
     ring = [(i * cores + c, (i + 1 - 2 * c) % planes * cores + c) for i in range(planes) for c in range(cores)]
-    part = lax.dynamic_slice_in_dim(env_own, core * share, share, 1)
+    part = call_turn(ids, env_own, tile)
     from_left, from_right = step(part, 1), step(part, -1)
     tensor = jnp.pad(
         mpo_tensor.reshape(bond, bond * states * states), ((0, slots - bond), (0, (slots - bond) * states * states))
@@ -306,16 +328,18 @@
     onward, weights, map_here = lax.optimization_barrier((onward, weights, map_here))
     from_far = lax.ppermute(onward, ("mpo", "col"), ring)
     env_got = jnp.concatenate([from_left, from_far, from_right], axis=0)
+    part_twin = twin(part)
     env_twin = twin(env_got)
     folded = []
-    for half, got in ((0, env_got), (1, env_twin)):
-        folded.append(fold(ids, weights, env_own, got, half, 0, states))
+    for own, got in ((part, env_got), (part_twin, env_twin)):
+        folded.append(fold(ids, weights, own, got, states))
 
     arrived = arrived.reshape(env_count * message, 128)
     swapped = twin(arrived)
-    mine = call_unpack(ids, map_here, arrived, swapped, capacity, pool, cores, planes * cores)
-    tile_rows = lax.all_to_all(mine, ("mpo", "col"), 0, 0, tiled=True)
-    result = call_apply(ids, kept, tile_rows, folded, tile)
+    mine = call_unpack(ids, map_here, arrived, swapped, capacity, pool, cores, planes)
+    by_plane = lax.all_to_all(mine, "mpo", 0, 0, tiled=True)
+    by_twin = twin(by_plane)
+    result = call_apply(ids, kept, by_plane, by_twin, folded, tile)
     return jnp.swapaxes(result, 2, 3)
 
 

time: 145 us -> 158 us (1.090)
  waiting for transfers between devices: 37.7 us -> 45.2 us
  starting transfers between devices: 63.3 us -> 67.4 us
  Pallas kernels: 36.7 us -> 39.5 us
  local copies, waits for them, and re-layouts: 4.63 us -> 2.45 us
    all_to_all x1, waiting for transfers between devices: 0.98 us -> 8.53 us  [on_device(): by_plane = lax.all_to_all(mine, 'mpo', 0, 0, tiled=True)]
    ppermute x2 -> x4, starting transfers between devices: 3.89 us -> 7.9 us  [twin(): return lax.ppermute(x, 'col', [(0, 1), (1, 0)])]
    pallas_call x0 -> x1, Pallas kernels: none -> 3.49 us  [call_turn(): pl.pallas_call(functools.partial(turn_kernel, tile), in_specs=[SMEM] + vm...]
  transfers between devices with their start and end apart: 7 -> 9, of which waited for: 4 -> 4; matrix products, arithmetic and copies ran while one was open for 2% -> 2% of each run, Pallas kernels for 17% -> 15%
where the time goes in v6:
time: 158 us; the launch traced here: 156 us
  starting transfers between devices  67.4 us (43%)
  waiting for transfers between devices  45.2 us (29%)
  Pallas kernels  39.5 us (25%)
  local copies, waits for them, and re-layouts  2.45 us (2%)
    all_to_all x1, starting transfers between devices, on_device(): lax.all_to_all(packed.reshape(env_count, message // 4, 4, 128), 'env', 0,...  45.8 us
    all_to_all x1, waiting for transfers between devices, on_device(): lax.all_to_all(packed.reshape(env_count, message // 4, 4, 128), 'env', 0,...  24.5 us
    pallas_call x2, Pallas kernels, fold(): pl.pallas_call(fold_kernel, grid_spec=pltpu.PrefetchScalarGridSpec(num_sc...  15.7 us
    pallas_call x1, Pallas kernels, call_apply(): pl.pallas_call(functools.partial(apply_kernel, tile), grid_spec=pltpu.Pre...  12.4 us
    ppermute x1, waiting for transfers between devices, on_device(): from_far = lax.ppermute(onward, ('mpo', 'col'), ring)  10.6 us
    all_to_all x1, waiting for transfers between devices, on_device(): by_plane = lax.all_to_all(mine, 'mpo', 0, 0, tiled=True)  8.53 us
    ppermute x4, starting transfers between devices, twin(): return lax.ppermute(x, 'col', [(0, 1), (1, 0)])  7.9 us
    ppermute x2, starting transfers between devices, on_device(): lax.ppermute(x, 'mpo', [(i, (i + d) % planes) for i in range(planes)])  7.17 us
  transfers between devices with their start and end apart: 9, of which 4 were waited for; matrix products, arithmetic and copies ran while one was open for 2% of the time, Pallas kernels for 15%

profile of v6, /device:TPU:40, one launch (start us, length us, event | category | flops | bytes accessed | tf_op | source)
XLA Modules:
  0.0 156.2 jit_solution(4061910262799145135)
XLA Ops:
  0.0 0.7 pad_add_fusion.ids_ref
  0.7 3.5 %turn.1.own_ref = bf16[4,192,384]{2,1,0:T(8,128)(2,1)} custom-call(s32[4]{0:T(128)} %pad_add_fusion.ids_ref, bf16[4,384,384]{2,1,0:T(8,128)(2,1)} %bitcast.11), custom_call_target="tpu_custom_call" | custom-call | flops 268435456 | bytes 2097152 | tf_op jit(solution)/shard_map/turn/pallas_call | solution.py:154
  4.1 5.2 %collective-permute-start.1 = (bf16[4,192,384]{2,1,0:T(8,128)(2,1)}, bf16[4,192,384]{2,1,0:T(8,128)(2,1)S(1)}, u32[]{:S(2)}, u32[]{:S(2)}) collective-permute-start(bf16[4,192,384]{2,1,0:T(8,128)(2,1)} %turn.1.own_ref), channel_id=1, source_target_pairs={{0,6},{2,0},{4,2},{6,4},{1,7},{3,1},{5,3},{7,5},{8,14},{10,8},{12,... | collective-permute-start | bytes 1769480 | tf_op jit(solution)/shard_map/ppermute | solution.py:317
  9.4 2.0 %collective-permute-start = (bf16[4,192,384]{2,1,0:T(8,128)(2,1)}, bf16[4,192,384]{2,1,0:T(8,128)(2,1)S(1)}, u32[]{:S(2)}, u32[]{:S(2)}) collective-permute-start(bf16[4,192,384]{2,1,0:T(8,128)(2,1)} %turn.1.own_ref), channel_id=1, source_target_pairs={{0,2},{2,4},{4,6},{6,0},{1,3},{3,5},{5,7},{7,1},{8,10},{10,12},{12... | collective-permute-start | bytes 1769480 | tf_op jit(solution)/shard_map/ppermute | solution.py:317
  11.3 3.3 %pack.1 = bf16[1152,128]{1,0:T(8,128)(2,1)} custom-call(s32[4]{0:T(128)} %pad_add_fusion.ids_ref, s32[32,192]{1,0:T(8,128)} %map_ref.1, bf16[1536,384]{1,0:T(8,128)(2,1)} %bitcast.14), custom_call_target="tpu_custom_call" | custom-call | flops 536870912 | bytes 2097152 | tf_op jit(solution)/shard_map/pack/pallas_call | solution.py:239
  14.6 45.8 %all-to-all-start = ((bf16[32,9,4,128]{3,2,1,0:T(4,128)(2,1)}), bf16[32,9,4,128]{3,2,1,0:T(4,128)(2,1)S(1)}, u32[]{:S(2)}, u32[]{:S(2)}) async-start(bf16[32,9,4,128]{3,2,1,0:T(4,128)(2,1)} %bitcast.13), calls=%async_computation | async-start | bytes 589824 | tf_op jit(solution)/shard_map/all_to_all | solution.py:314
  60.7 0.6 pad.8.tensor_ref
  61.3 0.6 pad.9.mask_ref
  61.9 2.2 %weights.1.weight_ref = bf16[512,256]{1,0:T(8,128)(2,1)} custom-call(s32[4]{0:T(128)} %pad_add_fusion.ids_ref, f32[2]{0:T(128)} %fields_ref.1, f32[16,256]{1,0:T(8,128)} %pad.8.tensor_ref, f32[16,16]{1,0:T(8,128)} %pad.9.mask_ref), custom_call_target="tpu_custom_call" | custom-call | flops 268435456 | bytes 524288 | tf_op jit(solution)/shard_map/weights/pallas_call | solution.py:130
  64.1 0.7 constant_dynamic-slice_fusion.map_ref
  65.1 2.4 %collective-permute-start.4 = (bf16[4,192,384]{2,1,0:T(8,128)(2,1)S(1)}, bf16[4,192,384]{2,1,0:T(8,128)(2,1)S(1)}, u32[]{:S(2)}, u32[]{:S(2)}) collective-permute-start(bf16[4,192,384]{2,1,0:T(8,128)(2,1)S(1)} %get-tuple-element.10), channel_id=1, source_target_pairs={{0,2},{1,7},{2,4},{3,1},{4,6},{5,3},{6,0},{7,5},{8,10},{9,15},{10,... | collective-permute-start | bytes 1769480 | tf_op jit(solution)/shard_map/ppermute | solution.py:329
  67.5 10.6 %collective-permute-done.4 = bf16[4,192,384]{2,1,0:T(8,128)(2,1)S(1)} collective-permute-done((bf16[4,192,384]{2,1,0:T(8,128)(2,1)S(1)}, bf16[4,192,384]{2,1,0:T(8,128)(2,1)S(1)}, u32[]{:S(2)}, u32[]{:S(2)}) %collective-permute-start.4) | collective-permute-done | bytes 589856 | tf_op jit(solution)/shard_map/ppermute | solution.py:329
  78.3 2.1 %collective-permute-start.6 = (bf16[12,192,384]{2,1,0:T(8,128)(2,1)S(1)}, bf16[12,192,384]{2,1,0:T(8,128)(2,1)}, u32[]{:S(2)}, u32[]{:S(2)}) collective-permute-start(bf16[12,192,384]{2,1,0:T(8,128)(2,1)S(1)} %constant_dynamic-update-slice_fusion.got_ref), channel_id=1, source_target_pairs={{0,1},{1,0},{2,3},{3,2},{4,5},{5,4},{6,7},{7,6},{8,9},{9,8},{10,11... | collective-permute-start | bytes 5308424 | tf_op jit(solution)/shard_map/ppermute | solution.py:310
  80.4 24.5 %all-to-all-done = bf16[32,9,4,128]{3,2,1,0:T(4,128)(2,1)S(1)} async-done(((bf16[32,9,4,128]{3,2,1,0:T(4,128)(2,1)}), bf16[32,9,4,128]{3,2,1,0:T(4,128)(2,1)S(1)}, u32[]{:S(2)}, u32[]{:S(2)}) %all-to-all-start) | async-done | bytes 294944 | tf_op jit(solution)/shard_map/all_to_all | solution.py:314
  104.9 1.9 %collective-permute-start.2 = (bf16[1152,128]{1,0:T(8,128)(2,1)S(1)}, bf16[1152,128]{1,0:T(8,128)(2,1)S(1)}, u32[]{:S(2)}, u32[]{:S(2)}) collective-permute-start(bf16[1152,128]{1,0:T(8,128)(2,1)S(1)} %bitcast.9), channel_id=1, source_target_pairs={{0,1},{1,0},{2,3},{3,2},{4,5},{5,4},{6,7},{7,6},{8,9},{9,8},{10,11... | collective-permute-start | bytes 884744 | tf_op jit(solution)/shard_map/ppermute | solution.py:310
  106.8 1.5 collective-permute-done.2.peer_ref
  108.4 2.4 %unpack.1 = bf16[4,192,384]{2,1,0:T(8,128)(2,1)} custom-call(s32[4]{0:T(128)S(1)} %copy-done, s32[1,192]{1,0:T(1,128)S(1)} %constant_dynamic-slice_fusion.map_ref, bf16[1152,128]{1,0:T(8,128)(2,1)S(1)} %bitcast.10, bf16[1152,128]{1,0:T(8,128)(2,1)S(1)} %collective-permute-done.2.peer_ref), custom_call_target="tpu_custom_call" | custom-call | flops 268435456 | bytes 2097152 | tf_op jit(solution)/shard_map/unpack/pallas_call | solution.py:253
  110.8 4.2 %all-to-all-start.1 = ((bf16[4,192,384]{2,1,0:T(8,128)(2,1)}), bf16[4,192,384]{2,1,0:T(8,128)(2,1)S(1)}, u32[]{:S(2)}, u32[]{:S(2)}) async-start(bf16[4,192,384]{2,1,0:T(8,128)(2,1)} %unpack.1), calls=%async_computation.1 | async-start | bytes 1179648 | tf_op jit(solution)/shard_map/all_to_all | solution.py:340
  115.0 1.9 %collective-permute-start.5 = (bf16[4,192,384]{2,1,0:T(8,128)(2,1)S(1)}, bf16[4,192,384]{2,1,0:T(8,128)(2,1)}, u32[]{:S(2)}, u32[]{:S(2)}) collective-permute-start(bf16[4,192,384]{2,1,0:T(8,128)(2,1)S(1)} %copy-done.3), channel_id=1, source_target_pairs={{0,1},{1,0},{2,3},{3,2},{4,5},{5,4},{6,7},{7,6},{8,9},{9,8},{10,11... | collective-permute-start | bytes 1769480 | tf_op jit(solution)/shard_map/ppermute | solution.py:310
  116.9 8.5 %all-to-all-done.1.mine_ref = bf16[4,192,384]{2,1,0:T(8,128)(2,1)S(1)} async-done(((bf16[4,192,384]{2,1,0:T(8,128)(2,1)}), bf16[4,192,384]{2,1,0:T(8,128)(2,1)S(1)}, u32[]{:S(2)}, u32[]{:S(2)}) %all-to-all-start.1) | async-done | bytes 589856 | tf_op jit(solution)/shard_map/all_to_all | solution.py:340
  125.5 1.9 %collective-permute-start.3 = (bf16[4,192,384]{2,1,0:T(8,128)(2,1)S(1)}, bf16[4,192,384]{2,1,0:T(8,128)(2,1)}, u32[]{:S(2)}, u32[]{:S(2)}) collective-permute-start(bf16[4,192,384]{2,1,0:T(8,128)(2,1)S(1)} %all-to-all-done.1.mine_ref), channel_id=1, source_target_pairs={{0,1},{1,0},{2,3},{3,2},{4,5},{5,4},{6,7},{7,6},{8,9},{9,8},{10,11... | collective-permute-start | bytes 1769480 | tf_op jit(solution)/shard_map/ppermute | solution.py:310
  128.1 7.8 %shard_map.73.refs_0_ = bf16[16,192,1536]{2,1,0:T(8,128)(2,1)} custom-call(s32[4]{0:T(128)} %pad_add_fusion.ids_ref, bf16[512,256]{1,0:T(8,128)(2,1)} %weights.1.weight_ref, bf16[4,192,384]{2,1,0:T(8,128)(2,1)} %turn.1.own_ref, bf16[12,192,384]{2,1,0:T(8,128)(2,1)} %copy-done.1), custom_call_target="tpu_custom_call" | custom-call | flops 2415919104 | bytes 6291456 | tf_op jit(solution)/shard_map/pallas_call | solution.py:219
  135.9 7.9 %shard_map.74.refs_1_ = bf16[16,192,1536]{2,1,0:T(8,128)(2,1)} custom-call(s32[4]{0:T(128)} %pad_add_fusion.ids_ref, bf16[512,256]{1,0:T(8,128)(2,1)} %weights.1.weight_ref, bf16[4,192,384]{2,1,0:T(8,128)(2,1)} %collective-permute-done.5.own_ref, bf16[12,192,384]{2,1,0:T(8,128)(2,1)} %collective-permute-done.6.got_ref), custom_call_target="tpu_custom_call" | custom-call | flops 2415919104 | bytes 6291456 | tf_op jit(solution)/shard_map/pallas_call | solution.py:219
  143.8 12.4 %apply.1 = f32[4,1,192,384]{3,2,1,0:T(8,128)} custom-call(s32[4]{0:T(128)} %pad_add_fusion.ids_ref, s32[1]{0:T(128)S(6)} %copy.13.kept_ref, bf16[4,192,384]{2,1,0:T(8,128)(2,1)} %copy-done.2, bf16[4,192,384]{2,1,0:T(8,128)(2,1)} %collective-permute-done.3.twin_ref, bf16[16,192,1536]{2,1,0:T(8,128)(2,1)} %shard_map.73.refs_0_, ...), custom_call_target="tpu_custom_call" | custom-call | flops 4831838208 | bytes 23068672 | tf_op jit(solution)/shard_map/apply/pallas_call | solution.py:271
  (23 shorter events, 0.7 us)
Async XLA Ops:
  0.7 59.7 %copy-start.4 = (f32[14,14,4,4]{1,3,2,0:T(4,128)S(1)}, f32[14,14,4,4]{1,3,2,0:T(4,128)}, u32[]{:S(2)}) copy-start(f32[14,14,4,4]{1,3,2,0:T(4,128)} %param.11) | copy-start | bytes 37636
  4.1 56.6 %copy-start.5 = (s32[14,14]{1,0:T(8,128)S(1)}, s32[14,14]{1,0:T(8,128)}, u32[]{:S(2)}) copy-start(s32[14,14]{1,0:T(8,128)} %param.12) | copy-start | bytes 2356
  4.1 60.7 %collective-permute-start.1 = (bf16[4,192,384]{2,1,0:T(8,128)(2,1)}, bf16[4,192,384]{2,1,0:T(8,128)(2,1)S(1)}, u32[]{:S(2)}, u32[]{:S(2)}) collective-permute-start(bf16[4,192,384]{2,1,0:T(8,128)(2,1)} %turn.1.own_ref), channel_id=1, source_target_pairs={{0,6},{2,0},{4,2},{6,4},{1,7},{3,1},{5,3},{7,5},{8,14},{10,8},{12,... | collective-permute-start | bytes 1769480 | tf_op jit(solution)/shard_map/ppermute | solution.py:317
  9.4 55.5 %collective-permute-start = (bf16[4,192,384]{2,1,0:T(8,128)(2,1)}, bf16[4,192,384]{2,1,0:T(8,128)(2,1)S(1)}, u32[]{:S(2)}, u32[]{:S(2)}) collective-permute-start(bf16[4,192,384]{2,1,0:T(8,128)(2,1)} %turn.1.own_ref), channel_id=1, source_target_pairs={{0,2},{2,4},{4,6},{6,0},{1,3},{3,5},{5,7},{7,1},{8,10},{10,12},{12... | collective-permute-start | bytes 1769480 | tf_op jit(solution)/shard_map/ppermute | solution.py:317
  14.6 90.3 %all-to-all-start = ((bf16[32,9,4,128]{3,2,1,0:T(4,128)(2,1)}), bf16[32,9,4,128]{3,2,1,0:T(4,128)(2,1)S(1)}, u32[]{:S(2)}, u32[]{:S(2)}) async-start(bf16[32,9,4,128]{3,2,1,0:T(4,128)(2,1)} %bitcast.13), calls=%async_computation | async-start | bytes 589824 | tf_op jit(solution)/shard_map/all_to_all | solution.py:314
  65.0 43.3 %copy-start = (s32[4]{0:T(128)S(1)}, s32[4]{0:T(128)}, u32[]{:S(2)}) copy-start(s32[4]{0:T(128)} %pad_add_fusion.ids_ref) | copy-start | bytes 52
  65.1 13.0 %collective-permute-start.4 = (bf16[4,192,384]{2,1,0:T(8,128)(2,1)S(1)}, bf16[4,192,384]{2,1,0:T(8,128)(2,1)S(1)}, u32[]{:S(2)}, u32[]{:S(2)}) collective-permute-start(bf16[4,192,384]{2,1,0:T(8,128)(2,1)S(1)} %get-tuple-element.10), channel_id=1, source_target_pairs={{0,2},{1,7},{2,4},{3,1},{4,6},{5,3},{6,0},{7,5},{8,10},{9,15},{10,... | collective-permute-start | bytes 1769480 | tf_op jit(solution)/shard_map/ppermute | solution.py:329
  78.2 36.8 %copy-start.3 = (bf16[4,192,384]{2,1,0:T(8,128)(2,1)S(1)}, bf16[4,192,384]{2,1,0:T(8,128)(2,1)}, u32[]{:S(2)}) copy-start(bf16[4,192,384]{2,1,0:T(8,128)(2,1)} %turn.1.own_ref) | copy-start | bytes 1769476
  78.3 49.8 %copy-start.1 = (bf16[12,192,384]{2,1,0:T(8,128)(2,1)}, bf16[12,192,384]{2,1,0:T(8,128)(2,1)S(1)}, u32[]{:S(2)}) copy-start(bf16[12,192,384]{2,1,0:T(8,128)(2,1)S(1)} %constant_dynamic-update-slice_fusion.got_ref) | copy-start | bytes 5308420
  78.3 57.6 %collective-permute-start.6 = (bf16[12,192,384]{2,1,0:T(8,128)(2,1)S(1)}, bf16[12,192,384]{2,1,0:T(8,128)(2,1)}, u32[]{:S(2)}, u32[]{:S(2)}) collective-permute-start(bf16[12,192,384]{2,1,0:T(8,128)(2,1)S(1)} %constant_dynamic-update-slice_fusion.got_ref), channel_id=1, source_target_pairs={{0,1},{1,0},{2,3},{3,2},{4,5},{5,4},{6,7},{7,6},{8,9},{9,8},{10,11... | collective-permute-start | bytes 5308424 | tf_op jit(solution)/shard_map/ppermute | solution.py:310
  104.9 3.5 %collective-permute-start.2 = (bf16[1152,128]{1,0:T(8,128)(2,1)S(1)}, bf16[1152,128]{1,0:T(8,128)(2,1)S(1)}, u32[]{:S(2)}, u32[]{:S(2)}) collective-permute-start(bf16[1152,128]{1,0:T(8,128)(2,1)S(1)} %bitcast.9), channel_id=1, source_target_pairs={{0,1},{1,0},{2,3},{3,2},{4,5},{5,4},{6,7},{7,6},{8,9},{9,8},{10,11... | collective-permute-start | bytes 884744 | tf_op jit(solution)/shard_map/ppermute | solution.py:310
  110.8 14.7 %all-to-all-start.1 = ((bf16[4,192,384]{2,1,0:T(8,128)(2,1)}), bf16[4,192,384]{2,1,0:T(8,128)(2,1)S(1)}, u32[]{:S(2)}, u32[]{:S(2)}) async-start(bf16[4,192,384]{2,1,0:T(8,128)(2,1)} %unpack.1), calls=%async_computation.1 | async-start | bytes 1179648 | tf_op jit(solution)/shard_map/all_to_all | solution.py:340
  115.0 20.9 %collective-permute-start.5 = (bf16[4,192,384]{2,1,0:T(8,128)(2,1)S(1)}, bf16[4,192,384]{2,1,0:T(8,128)(2,1)}, u32[]{:S(2)}, u32[]{:S(2)}) collective-permute-start(bf16[4,192,384]{2,1,0:T(8,128)(2,1)S(1)} %copy-done.3), channel_id=1, source_target_pairs={{0,1},{1,0},{2,3},{3,2},{4,5},{5,4},{6,7},{7,6},{8,9},{9,8},{10,11... | collective-permute-start | bytes 1769480 | tf_op jit(solution)/shard_map/ppermute | solution.py:310
  125.5 10.4 %copy-start.2 = (bf16[4,192,384]{2,1,0:T(8,128)(2,1)}, bf16[4,192,384]{2,1,0:T(8,128)(2,1)S(1)}, u32[]{:S(2)}) copy-start(bf16[4,192,384]{2,1,0:T(8,128)(2,1)S(1)} %all-to-all-done.1.mine_ref) | copy-start | bytes 1769476
  125.5 18.3 %collective-permute-start.3 = (bf16[4,192,384]{2,1,0:T(8,128)(2,1)S(1)}, bf16[4,192,384]{2,1,0:T(8,128)(2,1)}, u32[]{:S(2)}, u32[]{:S(2)}) collective-permute-start(bf16[4,192,384]{2,1,0:T(8,128)(2,1)S(1)} %all-to-all-done.1.mine_ref), channel_id=1, source_target_pairs={{0,1},{1,0},{2,3},{3,2},{4,5},{5,4},{6,7},{7,6},{8,9},{9,8},{10,11... | collective-permute-start | bytes 1769480 | tf_op jit(solution)/shard_map/ppermute | solution.py:310

commit v7 on v5

--- a/solution.py
+++ b/solution.py
@@ -13,7 +13,6 @@
 
 
 GROUP = 8
-CHUNKS = 1
 
 
 def iota(shape, dim):
@@ -158,8 +157,8 @@
 
 
 def apply_kernel(tile, ids_ref, kept_ref, rows_ref, *refs):
-    folded = refs[: 2 * CHUNKS]
-    out_ref, halves, own, turned = refs[2 * CHUNKS :]
+    folded = refs[:-4]
+    out_ref, halves, own, turned = refs[-4:]
     core = ids_ref[2]
     _, tiles, width = rows_ref.shape
     states = tiles * tile // width
@@ -186,23 +185,21 @@
     out_ref[0, 0] = dot(turned[...], halves[...])
 
 
-def fold(ids, weights, own, got, half, chunk, states):
-    others, count, width = got.shape
+def fold(ids, weights, own, got, half, begin, count, states):
+    others, share, width = got.shape
     slab = own.shape[0]
     pairs = slab * states
     step = 48
-    steps = count // step
+    first, whole = begin // step, share // step
     return pl.pallas_call(
         fold_kernel,
         grid_spec=pltpu.PrefetchScalarGridSpec(
             num_scalar_prefetch=1,
-            grid=(steps,),
+            grid=(count // step,),
             in_specs=[
                 pl.BlockSpec(weights.shape, lambda i, ids: (0, 0)),
-                pl.BlockSpec(
-                    (slab, step, width), lambda i, ids: (0, ((ids[2] + half) % 2 * CHUNKS + chunk) * steps + i, 0)
-                ),
-                pl.BlockSpec((others, step, width), lambda i, ids: (0, i, 0)),
+                pl.BlockSpec((slab, step, width), lambda i, ids: (0, (ids[2] + half) % 2 * whole + first + i, 0)),
+                pl.BlockSpec((others, step, width), lambda i, ids: (0, first + i, 0)),
             ],
             out_specs=pl.BlockSpec((pairs, step, states * width), lambda i, ids: (0, i, 0)),
         ),
@@ -241,7 +238,7 @@
 
 def call_apply(ids, kept, rows, folded, tile):
     _, tiles, width = rows.shape
-    pairs, part, deep = folded[0].shape
+    pairs, _, deep = folded[0].shape
     share = width // 2
     states = deep // width
     slab = pairs // states
@@ -252,7 +249,7 @@
             num_scalar_prefetch=2,
             grid=(slab,),
             in_specs=[pl.BlockSpec((tile, tiles, width), whole)]
-            + [pl.BlockSpec((states, part, deep), lambda v, *_: (v, 0, 0))] * len(folded),
+            + [pl.BlockSpec((states, part.shape[1], deep), lambda v, *_: (v, 0, 0)) for part in folded],
             out_specs=pl.BlockSpec((1, 1, share, width), lambda v, *_: (v, 0, 0, 0)),
             scratch_shapes=[
                 pltpu.VMEM((deep, width), BF16),
@@ -308,8 +305,11 @@
     env_got = jnp.concatenate([from_left, from_far, from_right], axis=0)
     env_twin = twin(env_got)
     folded = []
-    for half, got in ((0, env_got), (1, env_twin)):
-        folded.append(fold(ids, weights, env_own, got, half, 0, states))
+    early = share // 2
+    for half, got, begin, count in (
+        (0, env_got, 0, early), (0, env_got, early, share - early), (1, env_twin, 0, share)
+    ):
+        folded.append(fold(ids, weights, env_own, got, half, begin, count, states))
 
     arrived = arrived.reshape(env_count * message, 128)
     swapped = twin(arrived)

time: 145 us -> 148 us (1.021); the launches traced: 144 us -> 145 us
  Pallas kernels: 36.7 us -> 39 us
    pallas_call x2 -> x3, Pallas kernels: 15.7 us -> 17.7 us  [fold(): pl.pallas_call(fold_kernel, grid_spec=pltpu.PrefetchScalarGridSpec(num_sc...]
  transfers between devices with their start and end apart: 7 -> 7, of which waited for: 4 -> 3; matrix products, arithmetic and copies ran while one was open for 2% -> 2% of each run, Pallas kernels for 17% -> 18%
where the time goes in v7:
time: 148 us; the launch traced here: 145 us
  starting transfers between devices  63.3 us (43%)
  Pallas kernels  39 us (26%)
  waiting for transfers between devices  36.8 us (25%)
  local copies, waits for them, and re-layouts  4.62 us (3%)
    all_to_all x1, starting transfers between devices, on_device(): lax.all_to_all(packed.reshape(env_count, message // 4, 4, 128), 'env', 0,...  45.8 us
    all_to_all x1, waiting for transfers between devices, on_device(): lax.all_to_all(packed.reshape(env_count, message // 4, 4, 128), 'env', 0,...  24.6 us
    pallas_call x3, Pallas kernels, fold(): pl.pallas_call(fold_kernel, grid_spec=pltpu.PrefetchScalarGridSpec(num_sc...  17.7 us
    pallas_call x1, Pallas kernels, call_apply(): pl.pallas_call(functools.partial(apply_kernel, tile), grid_spec=pltpu.Pre...  13.2 us
    ppermute x1, waiting for transfers between devices, on_device(): from_far = lax.ppermute(onward, ('mpo', 'col'), ring)  10.6 us
    ppermute x2, starting transfers between devices, on_device(): lax.ppermute(x, 'mpo', [(i, (i + d) % planes) for i in range(planes)])  7.06 us
    all_to_all x1, starting transfers between devices, on_device(): tile_rows = lax.all_to_all(mine, ('mpo', 'col'), 0, 0, tiled=True)  4.2 us
    ppermute x2, starting transfers between devices, twin(): return lax.ppermute(x, 'col', [(0, 1), (1, 0)])  3.89 us
  transfers between devices with their start and end apart: 7, of which 3 were waited for; matrix products, arithmetic and copies ran while one was open for 2% of the time, Pallas kernels for 18%

profile of v7, /device:TPU:40, one launch (start us, length us, event | category | flops | bytes accessed | tf_op | source)
XLA Modules:
  0.0 145.3 jit_solution(8121908723832899275)
XLA Ops:
  0.0 1.2 dynamic-slice_bitcast_fusion
  1.2 5.1 %collective-permute-start.1 = (bf16[4,192,384]{2,1,0:T(8,128)(2,1)S(1)}, bf16[4,192,384]{2,1,0:T(8,128)(2,1)S(1)}, u32[]{:S(2)}, u32[]{:S(2)}) collective-permute-start(bf16[4,192,384]{2,1,0:T(8,128)(2,1)S(1)} %dynamic-slice_bitcast_fusion), channel_id=1, source_target_pairs={{0,6},{2,0},{4,2},{6,4},{1,7},{3,1},{5,3},{7,5},{8,14},{10,8},{12,... | collective-permute-start | bytes 1769480 | tf_op jit(solution)/shard_map/ppermute | solution.py:292
  6.3 2.0 %collective-permute-start = (bf16[4,192,384]{2,1,0:T(8,128)(2,1)S(1)}, bf16[4,192,384]{2,1,0:T(8,128)(2,1)S(1)}, u32[]{:S(2)}, u32[]{:S(2)}) collective-permute-start(bf16[4,192,384]{2,1,0:T(8,128)(2,1)S(1)} %dynamic-slice_bitcast_fusion), channel_id=1, source_target_pairs={{0,2},{2,4},{4,6},{6,0},{1,3},{3,5},{5,7},{7,1},{8,10},{10,12},{12... | collective-permute-start | bytes 1769480 | tf_op jit(solution)/shard_map/ppermute | solution.py:292
  8.3 0.6 pad_add_fusion.ids_ref
  8.8 3.3 %pack.1 = bf16[1152,128]{1,0:T(8,128)(2,1)} custom-call(s32[4]{0:T(128)} %pad_add_fusion.ids_ref, s32[32,192]{1,0:T(8,128)} %map_ref.1, bf16[1536,384]{1,0:T(8,128)(2,1)} %bitcast.18), custom_call_target="tpu_custom_call" | custom-call | flops 536870912 | bytes 2097152 | tf_op jit(solution)/shard_map/pack/pallas_call | solution.py:214
  12.1 45.8 %all-to-all-start = ((bf16[32,9,4,128]{3,2,1,0:T(4,128)(2,1)}), bf16[32,9,4,128]{3,2,1,0:T(4,128)(2,1)S(1)}, u32[]{:S(2)}, u32[]{:S(2)}) async-start(bf16[32,9,4,128]{3,2,1,0:T(4,128)(2,1)} %bitcast.17), calls=%async_computation | async-start | bytes 589824 | tf_op jit(solution)/shard_map/all_to_all | solution.py:288
  57.9 0.2 copy.9
  58.2 0.6 pad.8.tensor_ref
  58.8 0.6 pad.9.mask_ref
  59.4 2.2 %weights.1.weight_ref = bf16[512,256]{1,0:T(8,128)(2,1)} custom-call(s32[4]{0:T(128)} %pad_add_fusion.ids_ref, f32[2]{0:T(128)} %fields_ref.1, f32[16,256]{1,0:T(8,128)} %pad.8.tensor_ref, f32[16,16]{1,0:T(8,128)} %pad.9.mask_ref), custom_call_target="tpu_custom_call" | custom-call | flops 268435456 | bytes 524288 | tf_op jit(solution)/shard_map/weights/pallas_call | solution.py:129
  61.6 0.7 constant_dynamic-slice_fusion.map_ref
  62.6 2.4 %collective-permute-start.3 = (bf16[4,192,384]{2,1,0:T(8,128)(2,1)S(1)}, bf16[4,192,384]{2,1,0:T(8,128)(2,1)S(1)}, u32[]{:S(2)}, u32[]{:S(2)}) collective-permute-start(bf16[4,192,384]{2,1,0:T(8,128)(2,1)S(1)} %get-tuple-element.10), channel_id=1, source_target_pairs={{0,2},{1,7},{2,4},{3,1},{4,6},{5,3},{6,0},{7,5},{8,10},{9,15},{10,... | collective-permute-start | bytes 1769480 | tf_op jit(solution)/shard_map/ppermute | solution.py:304
  65.0 10.6 %collective-permute-done.3 = bf16[4,192,384]{2,1,0:T(8,128)(2,1)S(1)} collective-permute-done((bf16[4,192,384]{2,1,0:T(8,128)(2,1)S(1)}, bf16[4,192,384]{2,1,0:T(8,128)(2,1)S(1)}, u32[]{:S(2)}, u32[]{:S(2)}) %collective-permute-start.3) | collective-permute-done | bytes 589856 | tf_op jit(solution)/shard_map/ppermute | solution.py:304
  75.8 2.0 %collective-permute-start.4 = (bf16[12,192,384]{2,1,0:T(8,128)(2,1)S(1)}, bf16[12,192,384]{2,1,0:T(8,128)(2,1)}, u32[]{:S(2)}, u32[]{:S(2)}) collective-permute-start(bf16[12,192,384]{2,1,0:T(8,128)(2,1)S(1)} %constant_dynamic-update-slice_fusion.got_ref), channel_id=1, source_target_pairs={{0,1},{1,0},{2,3},{3,2},{4,5},{5,4},{6,7},{7,6},{8,9},{9,8},{10,11... | collective-permute-start | bytes 5308424 | tf_op jit(solution)/shard_map/ppermute | solution.py:284
  77.8 24.6 %all-to-all-done = bf16[32,9,4,128]{3,2,1,0:T(4,128)(2,1)S(1)} async-done(((bf16[32,9,4,128]{3,2,1,0:T(4,128)(2,1)}), bf16[32,9,4,128]{3,2,1,0:T(4,128)(2,1)S(1)}, u32[]{:S(2)}, u32[]{:S(2)}) %all-to-all-start) | async-done | bytes 294944 | tf_op jit(solution)/shard_map/all_to_all | solution.py:288
  102.4 1.9 %collective-permute-start.2 = (bf16[1152,128]{1,0:T(8,128)(2,1)S(1)}, bf16[1152,128]{1,0:T(8,128)(2,1)S(1)}, u32[]{:S(2)}, u32[]{:S(2)}) collective-permute-start(bf16[1152,128]{1,0:T(8,128)(2,1)S(1)} %bitcast.11), channel_id=1, source_target_pairs={{0,1},{1,0},{2,3},{3,2},{4,5},{5,4},{6,7},{7,6},{8,9},{9,8},{10,11... | collective-permute-start | bytes 884744 | tf_op jit(solution)/shard_map/ppermute | solution.py:284
  104.3 1.5 %collective-permute-done.2.peer_ref = bf16[1152,128]{1,0:T(8,128)(2,1)S(1)} collective-permute-done((bf16[1152,128]{1,0:T(8,128)(2,1)S(1)}, bf16[1152,128]{1,0:T(8,128)(2,1)S(1)}, u32[]{:S(2)}, u32[]{:S(2)}) %collective-permute-start.2) | collective-permute-done | bytes 294944 | tf_op jit(solution)/shard_map/ppermute | solution.py:284
  105.9 2.7 %unpack.1 = bf16[8,192,384]{2,1,0:T(8,128)(2,1)} custom-call(s32[4]{0:T(128)S(1)} %copy-done, s32[1,192]{1,0:T(1,128)S(1)} %constant_dynamic-slice_fusion.map_ref, bf16[1152,128]{1,0:T(8,128)(2,1)S(1)} %bitcast.12, bf16[1152,128]{1,0:T(8,128)(2,1)S(1)} %collective-permute-done.2.peer_ref), custom_call_target="tpu_custom_call" | custom-call | flops 268435456 | bytes 2097152 | tf_op jit(solution)/shard_map/unpack/pallas_call | solution.py:228
  108.6 4.2 %all-to-all-start.1 = ((bf16[8,192,384]{2,1,0:T(8,128)(2,1)}), bf16[8,192,384]{2,1,0:T(8,128)(2,1)S(1)}, u32[]{:S(2)}, u32[]{:S(2)}) async-start(bf16[8,192,384]{2,1,0:T(8,128)(2,1)} %unpack.1), calls=%async_computation.1 | async-start | bytes 2359296 | tf_op jit(solution)/shard_map/all_to_all | solution.py:317
  113.4 4.9 %shard_map.74.refs_1_ = bf16[16,96,1536]{2,1,0:T(8,128)(2,1)} custom-call(s32[4]{0:T(128)} %pad_add_fusion.ids_ref, bf16[512,256]{1,0:T(8,128)(2,1)} %weights.1.weight_ref, bf16[4,384,384]{2,1,0:T(8,128)(2,1)} %bitcast.13, bf16[12,192,384]{2,1,0:T(8,128)(2,1)} %copy-done.1), custom_call_target="tpu_custom_call" | custom-call | flops 1207959552 | bytes 6291456 | tf_op jit(solution)/shard_map/pallas_call | solution.py:194
  118.3 4.9 %shard_map.73.refs_0_ = bf16[16,96,1536]{2,1,0:T(8,128)(2,1)} custom-call(s32[4]{0:T(128)} %pad_add_fusion.ids_ref, bf16[512,256]{1,0:T(8,128)(2,1)} %weights.1.weight_ref, bf16[4,384,384]{2,1,0:T(8,128)(2,1)} %bitcast.14, bf16[12,192,384]{2,1,0:T(8,128)(2,1)} %copy-done.1), custom_call_target="tpu_custom_call" | custom-call | flops 1207959552 | bytes 6291456 | tf_op jit(solution)/shard_map/pallas_call | solution.py:194
  123.2 7.9 %shard_map.75.refs_2_ = bf16[16,192,1536]{2,1,0:T(8,128)(2,1)} custom-call(s32[4]{0:T(128)} %pad_add_fusion.ids_ref, bf16[512,256]{1,0:T(8,128)(2,1)} %weights.1.weight_ref, bf16[4,384,384]{2,1,0:T(8,128)(2,1)} %bitcast.15, bf16[12,192,384]{2,1,0:T(8,128)(2,1)} %collective-permute-done.4.got_ref), custom_call_target="tpu_custom_call" | custom-call | flops 2415919104 | bytes 6291456 | tf_op jit(solution)/shard_map/pallas_call | solution.py:194
  131.1 1.0 copy-done.2
  132.2 13.2 %apply.1 = f32[4,1,192,384]{3,2,1,0:T(8,128)} custom-call(s32[4]{0:T(128)} %pad_add_fusion.ids_ref, s32[1]{0:T(128)S(6)} %copy.13.kept_ref, bf16[8,192,384]{2,1,0:T(8,128)(2,1)} %copy-done.2, bf16[16,96,1536]{2,1,0:T(8,128)(2,1)} %shard_map.73.refs_0_, bf16[16,96,1536]{2,1,0:T(8,128)(2,1)} %shard_map.74.refs_1_, bf16[16,192,1536]{2,1,0:T(8,128)(2,1)} %shard_map.75.refs_2_), custom_call_target="tpu_custom_call" | custom-call | flops 4831838208 | bytes 23068672 | tf_op jit(solution)/shard_map/apply/pallas_call | solution.py:246
  (18 shorter events, 0.5 us)
Async XLA Ops:
  0.0 57.9 %copy-start.3 = (f32[14,14,4,4]{1,3,2,0:T(4,128)S(1)}, f32[14,14,4,4]{1,3,2,0:T(4,128)}, u32[]{:S(2)}) copy-start(f32[14,14,4,4]{1,3,2,0:T(4,128)} %param.11) | copy-start | bytes 37636
  1.2 57.0 %copy-start.4 = (s32[14,14]{1,0:T(8,128)S(1)}, s32[14,14]{1,0:T(8,128)}, u32[]{:S(2)}) copy-start(s32[14,14]{1,0:T(8,128)} %param.12) | copy-start | bytes 2356
  1.2 61.1 %collective-permute-start.1 = (bf16[4,192,384]{2,1,0:T(8,128)(2,1)S(1)}, bf16[4,192,384]{2,1,0:T(8,128)(2,1)S(1)}, u32[]{:S(2)}, u32[]{:S(2)}) collective-permute-start(bf16[4,192,384]{2,1,0:T(8,128)(2,1)S(1)} %dynamic-slice_bitcast_fusion), channel_id=1, source_target_pairs={{0,6},{2,0},{4,2},{6,4},{1,7},{3,1},{5,3},{7,5},{8,14},{10,8},{12,... | collective-permute-start | bytes 1769480 | tf_op jit(solution)/shard_map/ppermute | solution.py:292
  6.3 56.0 %collective-permute-start = (bf16[4,192,384]{2,1,0:T(8,128)(2,1)S(1)}, bf16[4,192,384]{2,1,0:T(8,128)(2,1)S(1)}, u32[]{:S(2)}, u32[]{:S(2)}) collective-permute-start(bf16[4,192,384]{2,1,0:T(8,128)(2,1)S(1)} %dynamic-slice_bitcast_fusion), channel_id=1, source_target_pairs={{0,2},{2,4},{4,6},{6,0},{1,3},{3,5},{5,7},{7,1},{8,10},{10,12},{12... | collective-permute-start | bytes 1769480 | tf_op jit(solution)/shard_map/ppermute | solution.py:292
  12.1 90.3 %all-to-all-start = ((bf16[32,9,4,128]{3,2,1,0:T(4,128)(2,1)}), bf16[32,9,4,128]{3,2,1,0:T(4,128)(2,1)S(1)}, u32[]{:S(2)}, u32[]{:S(2)}) async-start(bf16[32,9,4,128]{3,2,1,0:T(4,128)(2,1)} %bitcast.17), calls=%async_computation | async-start | bytes 589824 | tf_op jit(solution)/shard_map/all_to_all | solution.py:288
  62.6 43.3 %copy-start = (s32[4]{0:T(128)S(1)}, s32[4]{0:T(128)}, u32[]{:S(2)}) copy-start(s32[4]{0:T(128)} %pad_add_fusion.ids_ref) | copy-start | bytes 52
  62.6 13.0 %collective-permute-start.3 = (bf16[4,192,384]{2,1,0:T(8,128)(2,1)S(1)}, bf16[4,192,384]{2,1,0:T(8,128)(2,1)S(1)}, u32[]{:S(2)}, u32[]{:S(2)}) collective-permute-start(bf16[4,192,384]{2,1,0:T(8,128)(2,1)S(1)} %get-tuple-element.10), channel_id=1, source_target_pairs={{0,2},{1,7},{2,4},{3,1},{4,6},{5,3},{6,0},{7,5},{8,10},{9,15},{10,... | collective-permute-start | bytes 1769480 | tf_op jit(solution)/shard_map/ppermute | solution.py:304
  75.8 32.8 %copy-start.1 = (bf16[12,192,384]{2,1,0:T(8,128)(2,1)}, bf16[12,192,384]{2,1,0:T(8,128)(2,1)S(1)}, u32[]{:S(2)}) copy-start(bf16[12,192,384]{2,1,0:T(8,128)(2,1)S(1)} %constant_dynamic-update-slice_fusion.got_ref) | copy-start | bytes 5308420
  75.8 47.4 %collective-permute-start.4 = (bf16[12,192,384]{2,1,0:T(8,128)(2,1)S(1)}, bf16[12,192,384]{2,1,0:T(8,128)(2,1)}, u32[]{:S(2)}, u32[]{:S(2)}) collective-permute-start(bf16[12,192,384]{2,1,0:T(8,128)(2,1)S(1)} %constant_dynamic-update-slice_fusion.got_ref), channel_id=1, source_target_pairs={{0,1},{1,0},{2,3},{3,2},{4,5},{5,4},{6,7},{7,6},{8,9},{9,8},{10,11... | collective-permute-start | bytes 5308424 | tf_op jit(solution)/shard_map/ppermute | solution.py:284
  102.4 3.5 %collective-permute-start.2 = (bf16[1152,128]{1,0:T(8,128)(2,1)S(1)}, bf16[1152,128]{1,0:T(8,128)(2,1)S(1)}, u32[]{:S(2)}, u32[]{:S(2)}) collective-permute-start(bf16[1152,128]{1,0:T(8,128)(2,1)S(1)} %bitcast.11), channel_id=1, source_target_pairs={{0,1},{1,0},{2,3},{3,2},{4,5},{5,4},{6,7},{7,6},{8,9},{9,8},{10,11... | collective-permute-start | bytes 884744 | tf_op jit(solution)/shard_map/ppermute | solution.py:284
  108.6 22.5 %all-to-all-start.1 = ((bf16[8,192,384]{2,1,0:T(8,128)(2,1)}), bf16[8,192,384]{2,1,0:T(8,128)(2,1)S(1)}, u32[]{:S(2)}, u32[]{:S(2)}) async-start(bf16[8,192,384]{2,1,0:T(8,128)(2,1)} %unpack.1), calls=%async_computation.1 | async-start | bytes 2359296 | tf_op jit(solution)/shard_map/all_to_all | solution.py:317
  131.1 1.0 copy-start.2
